TPU v7x, 256 devices: a whole 4x4x8 slice. The times are simulated.
256 devices in a mesh: seq: 64 (over z, y, core), feat: 4 (over x).
Axes of the slice: x: 4, y: 4, z: 8, core: 2. Of those that a mesh axis runs over, the one named last changes fastest.
Arguments:
- hidden_in: bfloat16 [4, 16384, 2048], P(None, 'seq'), may hold values from -6 to 6
- w_query: bfloat16 [2048, 256], replicated, may hold values from -0.125 to 0.125
- w_key: bfloat16 [2048, 256], replicated, may hold values from -0.125 to 0.125
- w_value: bfloat16 [2048, 2048], P(None, 'feat'), may hold values from -0.125 to 0.125
- lengths: int32 [4], replicated, may hold values from 8192 to 16384, as said below
- owners: int32 [4], replicated, may hold values from 0 to 63
Outputs:
- mixed: bfloat16 [4, 16384, 2048], P(None, 'seq', 'feat')
- state_quad: float32 [64, 4, 16, 256, 128], P('seq', None, None, 'feat')
- state_low: float32 [64, 4, 16, 17, 128], P('seq', None, 'feat')
- norm_quad: float32 [64, 4, 16, 256], P('seq', None, None, 'feat')
- norm_low: float32 [64, 4, 16, 17], P('seq', None, 'feat')
Inputs may be any that keep to these rules, and one draw needn't show every extreme that they name: `lengths`: every prompt holds 8192 to 16384 live tokens, and some prompt holds exactly 16384. `owners`: several prompts may share a decoding device.
All inputs are finite; a program needn't handle non-finite values.
Results may differ from a plain program's by a relative error of at most 0.0085.
Values may be sent and summed in bfloat16 or wider, within the bound.
No kernel may reach another device: no remote copies, remote signals or barrier semaphores. Data moves between devices by JAX's collectives and lax.ppermute only.
A program may use at most 256 MiB of HBM per device.

v0:
```python
import jax
import jax.numpy as jnp
from jax import lax
from jax.sharding import Mesh
from jax.sharding import PartitionSpec as P

H = 16
FD = 16
SEQ = ("seq_0", "seq_1", "seq_2")


NORM_FLOOR = 0.0001


def nothing_yet(shard, identity):
    return jax.tree.map(
        lambda a, e: jnp.broadcast_to(jnp.asarray(e, a.dtype), a.shape), shard, identity
    )


def carried_in(shard, axes, combine, identity):
    before = start = nothing_yet(shard, identity)
    total = shard
    for axis in reversed(axes):
        peers, mine = (lax.axis_size(axis), lax.axis_index(axis))
        pieces = jax.tree.map(
            lambda part, kind: lax.all_gather(part.astype(kind), axis),
            total,
            (jnp.bfloat16, jnp.bfloat16, jnp.bfloat16, jnp.bfloat16),
        )
        inside, total = (start, start)
        for k in range(peers):
            passed = k < mine
            total = combine(
                total, jax.tree.map(lambda part, own: part[k].astype(own.dtype), pieces, shard)
            )
            inside = jax.tree.map(lambda new, old: jnp.where(passed, new, old), total, inside)
        before = combine(inside, before)
    return before


def in_one(arrays, axis):
    ends = [0]
    for a in arrays:
        ends.append(ends[-1] + a.size)
    total = lax.psum(jnp.concatenate([a.ravel() for a in arrays]), axis)
    return tuple((total[b:e].reshape(a.shape) for a, b, e in zip(arrays, ends, ends[1:])))


def low_features(inputs):
    constant = jnp.ones(inputs.shape[:-1] + (1,), jnp.float32)
    return jnp.concatenate([constant, inputs * FD ** (-0.25)], axis=-1)


def quad_features(leading, inputs):
    products = leading[..., :, None] * inputs[..., None, :]
    return products.reshape(inputs.shape[:-1] + (leading.shape[-1] * inputs.shape[-1],)) * (
        2.0 * FD
    ) ** (-0.5)


def add_states(earlier_part, later_part):
    return jax.tree.map(
        lambda first_term, second_term: first_term + second_term, earlier_part, later_part
    )


def project(flat_rows, weight_cols, prompts, span, heads, width_last):
    projected = jnp.dot(flat_rows, weight_cols, preferred_element_type=jnp.float32).astype(
        jnp.bfloat16
    )
    return projected.reshape(prompts, span, heads, width_last).astype(jnp.float32)


def body(hidden_in, w_query, w_key, w_value, lengths, owners):
    highest = lax.Precision.HIGHEST
    prompts, span, width = hidden_in.shape
    n_feat = lax.axis_size("feat")
    feat_index = lax.axis_index("feat")
    seq_index = lax.axis_index(SEQ)
    own_heads = H // n_feat
    head_dim = width // H
    flat_rows = hidden_in.reshape(prompts * span, width)
    positions = seq_index * span + jnp.arange(span, dtype=jnp.int32)
    live_mask = (positions[None, :] < lengths[:, None]).astype(jnp.float32)
    key_mask = live_mask[:, :, None, None]
    values_own = jnp.dot(flat_rows, w_value, preferred_element_type=jnp.float32).astype(
        jnp.bfloat16
    )
    value_own = values_own.reshape(prompts, span, own_heads, head_dim).astype(jnp.float32)
    query_cols = lax.dynamic_slice_in_dim(w_query, feat_index * own_heads * FD, own_heads * FD, 1)
    key_cols = lax.dynamic_slice_in_dim(w_key, feat_index * own_heads * FD, own_heads * FD, 1)
    query_own = project(flat_rows, query_cols, prompts, span, own_heads, FD)
    key_own = project(flat_rows, key_cols, prompts, span, own_heads, FD)
    key_quad = quad_features(key_own, key_own) * key_mask
    query_quad = quad_features(query_own, query_own)
    span_quad = jnp.einsum("pchf,pchd->phfd", key_quad, value_own, precision=highest)
    norm_span = jnp.sum(key_quad, axis=1)
    key_low = low_features(key_own) * key_mask
    query_low = low_features(query_own)
    span_low = jnp.einsum("pchf,pchd->phfd", key_low, value_own, precision=highest)
    low_norm = jnp.sum(key_low, axis=1)
    empty_states = (
        jnp.zeros_like(span_quad),
        jnp.zeros_like(norm_span),
        jnp.zeros_like(span_low),
        jnp.zeros_like(low_norm),
    )
    pre_quad, pre_norm, pre_low, pre_lnorm = carried_in(
        (span_quad, norm_span, span_low, low_norm), SEQ, add_states, empty_states
    )
    final_quad, final_norm, final_low, final_lnorm = in_one(
        (span_quad, norm_span, span_low, low_norm), SEQ
    )
    num_low = jnp.einsum("pchf,phfd->pchd", query_low, pre_low, precision=highest)
    den_low = jnp.einsum("pchf,phf->pch", query_low, pre_lnorm, precision=highest)
    num_quad = jnp.einsum("pchf,phfd->pchd", query_quad, pre_quad, precision=highest)
    den_quad = jnp.einsum("pchf,phf->pch", query_quad, pre_norm, precision=highest)
    final_quad, final_norm = (
        lax.all_to_all(
            final_quad.astype(jnp.bfloat16), "feat", split_axis=2, concat_axis=1, tiled=True
        ).astype(final_quad.dtype),
        lax.all_to_all(
            final_norm.astype(jnp.bfloat16), "feat", split_axis=2, concat_axis=1, tiled=True
        ).astype(final_norm.dtype),
    )
    scores = jnp.einsum("pthf,puhf->phtu", query_own, key_own, precision=highest)
    kernel = 1.0 + scores * FD ** (-0.5) + scores * scores * (0.5 / FD)
    causal = (jnp.arange(span)[:, None] >= jnp.arange(span)[None, :]).astype(jnp.float32)
    weight = kernel * causal[None, None, :, :] * live_mask[:, None, None, :]
    num_self = jnp.einsum("phtu,puhd->pthd", weight, value_own, precision=highest)
    den_self = jnp.transpose(jnp.sum(weight, axis=3), (0, 2, 1))
    numerator = num_low + num_quad + num_self
    denominator = den_low + den_quad + den_self
    attended = numerator / denominator[..., None] * live_mask[:, :, None, None]
    squares = jnp.sum(attended * attended, axis=(2, 3))
    sum_squares = lax.psum(squares, "feat")
    scaled = attended * lax.rsqrt(sum_squares / width + NORM_FLOOR)[:, :, None, None]
    mixed = scaled.astype(jnp.bfloat16).reshape(prompts, span, own_heads * head_dim)
    owned = (owners == seq_index).astype(jnp.float32)
    state_quad = (owned[:, None, None, None] * final_quad)[None]
    state_low = (owned[:, None, None, None] * final_low)[None]
    norm_quad = (owned[:, None, None] * final_norm)[None]
    norm_low = (owned[:, None, None] * final_lnorm)[None]
    return (mixed, state_quad, state_low, norm_quad, norm_low)


def solution(mesh):
    torus = Mesh(
        mesh.devices.reshape(8, 4, 2, mesh.shape["feat"]), ("seq_0", "seq_1", "seq_2", "feat")
    )
    placed = (P(None, SEQ, None), P(), P(), P(None, "feat"), P(), P())
    return jax.shard_map(
        body,
        mesh=torus,
        in_specs=placed,
        out_specs=(
            P(None, SEQ, "feat"),
            P(SEQ, None, None, "feat", None),
            P(SEQ, None, "feat", None, None),
            P(SEQ, None, None, "feat"),
            P(SEQ, None, "feat", None),
        ),
        check_vma=False,
    )
```

profile of v0, /device:TPU:1, one launch (start us, length us, event | category | flops | bytes accessed | tf_op | source)
XLA Modules:
  0.0 372.7 jit_solution(8492412542840202425)
XLA Ops:
  8.1 4.2 %fusion.42 = bf16[1024,64]{0,1:T(8,128)(2,1)S(1)} fusion(bf16[1024,2048]{1,0:T(8,128)(2,1)} %bitcast.84, bf16[2048,256]{1,0:T(8,128)(2,1)} %param.8, s32[]{:T(128)S(6)} %select_n.405), kind=kOutput, calls=%fused_computation.60 | convolution fusion | flops 268500992 | bytes 4849668 | tf_op jit(solution)/shard_map/dot_general | solution.py:69
  12.4 4.5 %convolution_convert_fusion = bf16[1024,512]{1,0:T(8,128)(2,1)S(1)} fusion(bf16[1024,2048]{1,0:T(8,128)(2,1)} %bitcast.85, bf16[2048,512]{1,0:T(8,128)(2,1)S(1)} %copy-done), kind=kOutput, calls=%fused_computation.57 | convolution fusion | flops 2148007936 | bytes 7340032 | tf_op jit(solution)/shard_map/dot_general | solution.py:87
  17.0 0.3 reshape.403
  17.3 0.6 copy.97
  17.9 0.7 multiply_reduce_fusion
  18.6 0.7 bitcast_multiply_fusion
  19.4 3.7 fusion.152
  23.4 0.9 fusion.153
  24.5 19.1 %all-gather.11.cloned.1.call-done = bf16[8,4,256,128]{3,2,1,0:T(8,128)(2,1)} async-done(((bf16[4,4,256,128]{3,2,1,0:T(8,128)(2,1)}), bf16[8,4,256,128]{3,2,1,0:T(8,128)(2,1)}) %all-gather.11.cloned.1.call-update) | async-done | bytes 2097168 | tf_op jit(solution)/shard_map/all_gather | solution.py:27
  43.6 2.8 fusion.44
  46.5 3.2 pad_maximum_fusion
  49.8 49.4 %all-gather.7.cloned.1.call-done = bf16[4,4,4,256,128]{4,3,2,1,0:T(8,128)(2,1)} async-done(((bf16[1,4,4,256,128]{4,3,2,1,0:T(8,128)(2,1)}), bf16[4,4,4,256,128]{4,3,2,1,0:T(8,128)(2,1)}) %all-gather.7.cloned.1.call-update) | async-done | bytes 4194320 | tf_op jit(solution)/shard_map/all_gather | solution.py:27
  99.1 3.9 %fusion.41 = bf16[1,4,4,256,128]{4,3,2,1,0:T(8,128)(2,1)} fusion(bf16[4,4,4,256,128]{4,3,2,1,0:T(8,128)(2,1)} %all-gather.7.cloned.1.call-done), kind=kLoop, calls=%fused_computation.54 | loop fusion | flops 4194304 | bytes 5242880 | tf_op jit(solution)/shard_map/convert_element_type | solution.py:27
  103.1 4.0 %fusion.43 = bf16[1024,64]{0,1:T(8,128)(2,1)S(1)} fusion(bf16[1024,2048]{1,0:T(8,128)(2,1)} %bitcast.86, bf16[2048,256]{1,0:T(8,128)(2,1)S(1)} %copy-done.3, s32[]{:T(128)S(6)} %select_n.405), kind=kOutput, calls=%fused_computation.61 | convolution fusion | flops 268500992 | bytes 4849668 | tf_op jit(solution)/shard_map/dot_general | solution.py:69
  107.3 1.9 all-gather.2
  109.2 9.7 %all_gather.61 = bf16[4,4,4,17]{3,2,1,0:T(4,128)(2,1)S(1)} all-gather(bf16[1,4,4,17]{3,2,1,0:T(4,128)(2,1)S(1)} %fusion.142), channel_id=1, replica_groups=mesh['seq_0'=8,'seq_1'=4,'seq_2'=2,'feat'=4] {'seq_1'}, dimensions={0}, use_global_device_ids=true | all-gather | bytes 2720 | tf_op jit(solution)/shard_map/all_gather | solution.py:27
  118.9 23.0 %all_gather.62 = bf16[8,4,4,17]{3,2,1,0:T(4,128)(2,1)S(1)} all-gather(bf16[1,4,4,17]{3,2,1,0:T(4,128)(2,1)S(1)} %fusion.141), channel_id=1, replica_groups=mesh['seq_0'=8,'seq_1'=4,'seq_2'=2,'feat'=4] {'seq_0'}, dimensions={0}, use_global_device_ids=true | all-gather | bytes 4896 | tf_op jit(solution)/shard_map/all_gather | solution.py:27
  141.9 8.0 %all_gather.63 = bf16[2,4,4,256]{3,2,1,0:T(4,128)(2,1)S(1)} all-gather(bf16[1,4,4,256]{3,2,1,0:T(4,128)(2,1)S(1)} %convert_element_type.526), channel_id=1, replica_groups=mesh['seq_0'=8,'seq_1'=4,'seq_2'=2,'feat'=4] {'seq_2'}, dimensions={0}, use_global_device_ids=true | all-gather | bytes 24576 | tf_op jit(solution)/shard_map/all_gather | solution.py:27
  150.0 10.1 %all_gather.64 = bf16[4,4,4,256]{3,2,1,0:T(4,128)(2,1)S(1)} all-gather(bf16[1,4,4,256]{3,2,1,0:T(4,128)(2,1)S(1)} %fusion.125), channel_id=1, replica_groups=mesh['seq_0'=8,'seq_1'=4,'seq_2'=2,'feat'=4] {'seq_1'}, dimensions={0}, use_global_device_ids=true | all-gather | bytes 40960 | tf_op jit(solution)/shard_map/all_gather | solution.py:27
  160.1 21.9 %all_gather.65 = bf16[8,4,4,256]{3,2,1,0:T(4,128)(2,1)S(1)} all-gather(bf16[1,4,4,256]{3,2,1,0:T(4,128)(2,1)S(1)} %fusion.124), channel_id=1, replica_groups=mesh['seq_0'=8,'seq_1'=4,'seq_2'=2,'feat'=4] {'seq_0'}, dimensions={0}, use_global_device_ids=true | all-gather | bytes 73728 | tf_op jit(solution)/shard_map/all_gather | solution.py:27
  182.0 7.0 %all-gather = bf16[8,4,17,128]{3,1,2,0:T(4,128)(2,1)S(1)} all-gather(bf16[4,4,17,128]{3,1,2,0:T(4,128)(2,1)S(1)} %copy.89), channel_id=2, replica_groups=mesh['seq_0'=8,'seq_1'=4,'seq_2'=2,'feat'=4] {'seq_2'}, dimensions={0}, use_global_device_ids=true | all-gather | bytes 208896 | tf_op jit(solution)/shard_map/all_gather | solution.py:27
  189.0 10.2 %all_gather.54 = bf16[4,4,4,17,128]{4,2,3,1,0:T(4,128)(2,1)S(1)} all-gather(bf16[1,4,4,17,128]{4,2,3,1,0:T(4,128)(2,1)S(1)} %fusion.105), channel_id=1, replica_groups=mesh['seq_0'=8,'seq_1'=4,'seq_2'=2,'feat'=4] {'seq_1'}, dimensions={0}, use_global_device_ids=true | all-gather | bytes 348160 | tf_op jit(solution)/shard_map/all_gather | solution.py:27
  199.3 0.4 fusion.77
  199.8 21.4 %all_gather.55 = bf16[8,4,4,17,128]{4,2,3,1,0:T(4,128)(2,1)S(1)} all-gather(bf16[1,4,4,17,128]{4,2,3,1,0:T(4,128)(2,1)S(1)} %fusion.101), channel_id=1, replica_groups=mesh['seq_0'=8,'seq_1'=4,'seq_2'=2,'feat'=4] {'seq_0'}, dimensions={0}, use_global_device_ids=true | all-gather | bytes 626688 | tf_op jit(solution)/shard_map/all_gather | solution.py:27
  221.2 0.4 fusion.90
  221.6 0.6 multiply_multiply_fusion.1
  222.3 2.1 fusion.122
  224.4 1.5 fusion
  225.9 3.9 %fusion.1 = f32[4,4,128,256]{3,2,1,0:T(8,128)} fusion(bf16[4,256,4,128]{1,3,2,0:T(8,128)(2,1)S(1)} %copy.97, f32[4,4,256,256]{2,3,1,0:T(8,128)S(1)} %get-tuple-element.40, f32[4,256]{1,0:T(4,128)S(1)} %compare_convert_fusion, f32[256,256]{0,1:T(8,128)S(1)} %fusion.82), kind=kOutput, calls=%fused_computation.11 | convolution fusion | flops 1617952768 | bytes 7606272 | tf_op jit(solution)/shard_map/phtu,puhd->pthd/dot_general | solution.py:131
  229.8 83.4 %all-reduce.4.cloned.1.call-done = f32[563472]{0:T(1024)} async-done(((f32[563472]{0:T(1024)}), f32[563472]{0:T(1024)}) %all-reduce.4.cloned.1.call-update) | async-done | bytes 2253904 | tf_op jit(solution)/shard_map/psum | solution.py:46
  313.3 1.7 convert.26
  315.3 0.9 reshape.544
  316.2 4.0 %all-to-all-start.1 = ((bf16[4,2,512]{2,1,0:T(2,128)(2,1)}), bf16[4,2,512]{2,1,0:T(2,128)(2,1)S(1)}, u32[]{:S(2)}, u32[]{:S(2)}) async-start(bf16[4,2,512]{2,1,0:T(2,128)(2,1)} %reshape.544), calls=%async_computation.1 | async-start | bytes 16384 | tf_op jit(solution)/shard_map/all_to_all | solution.py:123
  320.3 1.8 copy.99
  322.1 2.3 all-to-all-done.1
  324.4 3.7 %all-to-all-start = ((bf16[4,4,256,128]{3,1,0,2:T(4,128)(2,1)}), bf16[4,4,256,128]{3,1,0,2:T(4,128)(2,1)S(1)}, u32[]{:S(2)}, u32[]{:S(2)}) async-start(bf16[4,4,256,128]{3,1,0,2:T(4,128)(2,1)} %copy.99), calls=%async_computation | async-start | bytes 2097152 | tf_op jit(solution)/shard_map/all_to_all | solution.py:120
  328.3 0.7 copy.106
  329.0 0.7 broadcast_multiply_fusion.6
  329.7 0.6 reshape.545
  330.6 0.7 broadcast_multiply_fusion.5
  331.3 7.6 %all-to-all-done = bf16[4,4,256,128]{3,1,0,2:T(4,128)(2,1)S(1)} async-done(((bf16[4,4,256,128]{3,1,0,2:T(4,128)(2,1)}), bf16[4,4,256,128]{3,1,0,2:T(4,128)(2,1)S(1)}, u32[]{:S(2)}, u32[]{:S(2)}) %all-to-all-start) | async-done | bytes 1048608 | tf_op jit(solution)/shard_map/all_to_all | solution.py:120
  338.9 0.3 copy.100
  339.6 1.7 broadcast_multiply_fusion.1
  341.3 10.5 %fusion.8 = f32[4,4,128,256]{3,2,1,0:T(8,128)S(1)} fusion(f32[4,256,4,256]{1,3,2,0:T(8,128)} %bitcast.88, bf16[8,4,4,256,128]{4,3,2,1,0:T(8,128)(2,1)} %all-gather.9.cloned.1.call-done, pred[]{:T(512)S(6)} %gt.54, pred[]{:T(512)S(6)} %gt.55, pred[]{:T(512)S(6)} %gt.42, pred[]{:T(512)S(6)} %gt.43, pred[]{:T(512)S(6)} %gt.44, pred[]{:T(512)S(6)} %gt.45, ...), kind=kOutput, calls=%fused_computation.19 | convolution fusion | flops 1632108544 | bytes 20971534 | tf_op jit(solution)/shard_map/pchf,phfd->pchd/dot_general | solution.py:117
  351.9 3.5 multiply_reduce_fusion.1
  355.4 6.8 %psum.14 = f32[4,256]{1,0:T(4,128)S(1)} all-reduce(f32[4,256]{1,0:T(4,128)S(1)} %get-tuple-element.43), channel_id=1, replica_groups=mesh['seq_0'=8,'seq_1'=4,'seq_2'=2,'feat'=4] {'feat'}, use_global_device_ids=true, to_apply=%region_4.5 | all-reduce | flops 1024 | bytes 8192 | tf_op jit(solution)/shard_map/psum | solution.py:137
  362.3 2.0 multiply_convert_fusion
  364.2 1.3 copy.105
  (68 shorter events, 2.7 us)
Async XLA Ops:
  8.0 4.4 %copy-start = (bf16[2048,512]{1,0:T(8,128)(2,1)S(1)}, bf16[2048,512]{1,0:T(8,128)(2,1)}, u32[]{:S(2)}) copy-start(bf16[2048,512]{1,0:T(8,128)(2,1)} %param.9) | copy-start | bytes 6291460
  8.0 35.6 %all-gather.11.cloned.1.call-start = ((), (), s32[]{:S(2)}) async-start(), calls=%async_computation.5 | async-start | bytes 3145728 | tf_op jit(solution)/shard_map/all_gather | solution.py:27
  16.9 0.9 copy-start.4
  23.0 76.1 %all-gather.7.cloned.1.call-start = ((), (), s32[]{:S(2)}) async-start(), calls=%async_computation.2 | async-start | bytes 5242880 | tf_op jit(solution)/shard_map/all_gather | solution.py:27
  46.4 266.8 %all-reduce.4.cloned.1.call-start = ((), (), s32[]{:S(2)}) async-start(), calls=%async_computation.4 | async-start | bytes 4513792 | tf_op jit(solution)/shard_map/psum | solution.py:46
  49.7 53.4 %copy-start.3 = (bf16[2048,256]{1,0:T(8,128)(2,1)S(1)}, bf16[2048,256]{1,0:T(8,128)(2,1)}, u32[]{:S(2)}) copy-start(bf16[2048,256]{1,0:T(8,128)(2,1)} %param.7) | copy-start | bytes 3145732
  49.7 291.6 %all-gather.9.cloned.1.call-start = ((), (), s32[]{:S(2)}) async-start(), calls=%async_computation.3 | async-start | bytes 9437184 | tf_op jit(solution)/shard_map/all_gather | solution.py:27
  222.3 2.1 copy-start.2
  316.2 8.1 %all-to-all-start.1 = ((bf16[4,2,512]{2,1,0:T(2,128)(2,1)}), bf16[4,2,512]{2,1,0:T(2,128)(2,1)S(1)}, u32[]{:S(2)}, u32[]{:S(2)}) async-start(bf16[4,2,512]{2,1,0:T(2,128)(2,1)} %reshape.544), calls=%async_computation.1 | async-start | bytes 16384 | tf_op jit(solution)/shard_map/all_to_all | solution.py:123
  320.3 7.8 %copy-start.5 = (s32[4]{0:T(128)S(1)}, s32[4]{0:T(128)}, u32[]{:S(2)}) copy-start(s32[4]{0:T(128)} %param.11) | copy-start | bytes 52
  320.3 7.8 %slice-start = ((f32[563472]{0:T(1024)}), f32[272]{0:T(512)S(1)}, s32[]{:S(2)}) async-start(f32[563472]{0:T(1024)} %all-reduce.4.cloned.1.call-done), calls=%async_computation.6 | async-start | bytes 4096 | tf_op jit(solution)/shard_map/slice | solution.py:47
  320.3 7.9 %slice-start.1 = ((f32[563472]{0:T(1024)}), f32[34816]{0:T(1024)S(1)}, s32[]{:S(2)}) async-start(f32[563472]{0:T(1024)} %all-reduce.4.cloned.1.call-done), calls=%async_computation.7 | async-start | bytes 278528 | tf_op jit(solution)/shard_map/slice | solution.py:47
  324.4 14.5 %all-to-all-start = ((bf16[4,4,256,128]{3,1,0,2:T(4,128)(2,1)}), bf16[4,4,256,128]{3,1,0,2:T(4,128)(2,1)S(1)}, u32[]{:S(2)}, u32[]{:S(2)}) async-start(bf16[4,4,256,128]{3,1,0,2:T(4,128)(2,1)} %copy.99), calls=%async_computation | async-start | bytes 2097152 | tf_op jit(solution)/shard_map/all_to_all | solution.py:120
  341.3 10.5 %copy-start.6 = (f32[4,4,128,256]{3,2,1,0:T(8,128)S(1)}, f32[4,4,128,256]{3,2,1,0:T(8,128)}, u32[]{:S(2)}) copy-start(f32[4,4,128,256]{3,2,1,0:T(8,128)} %fusion.1) | copy-start | bytes 6291460
  362.3 3.3 copy-start.1
Sparse Core Ops, SparseCore 0:
  23.2 20.4 all-gather.10
  46.6 52.5 all-gather.6
  103.2 97.5 all-gather.8
Sparse Core Ops, SparseCore 1:
  50.4 262.8 all-reduce.3
where the time goes:
time: 379 us; the launch traced here: 373 us
  waiting for transfers between devices  162 us (43%)
  blocking collectives  120 us (32%)
  matrix products  39.3 us (10%)
  other arithmetic  20.1 us (5%)
  between operations  15.7 us (4%)
  starting transfers between devices  7.87 us (2%)
  local copies, waits for them, and re-layouts  7.84 us (2%)
    all_gather x9, blocking collectives, carried_in(): lax.all_gather(part.astype(kind), axis)  113 us
    psum x1, waiting for transfers between devices, in_one(): total = lax.psum(jnp.concatenate([a.ravel() for a in arrays]), axis)  83.4 us
    all_gather x3, waiting for transfers between devices, carried_in(): lax.all_gather(part.astype(kind), axis)  68.5 us
    dot_general x1, matrix products, body(): jnp.einsum('pchf,phfd->pchd', query_quad, pre_quad, precision=highest)  10.5 us
    dot_general x2, matrix products, project(): jnp.dot(flat_rows, weight_cols, preferred_element_type=jnp.float32)  8.19 us
    all_to_all x1, waiting for transfers between devices, body(): lax.all_to_all(final_quad.astype(jnp.bfloat16), 'feat', split_axis=2, con...  7.61 us
  transfers between devices with their start and end apart: 6, of which 5 were waited for; matrix products, arithmetic and copies ran while one was open for 9% of the time, Pallas kernels for 0%

commit v1 on v0

v1 whole, which is shorter than its diff:
```python
import functools

import jax
import jax.numpy as jnp
import numpy as np
from jax import lax
from jax.experimental import pallas as pl
from jax.experimental.pallas import tpu as pltpu
from jax.sharding import Mesh
from jax.sharding import PartitionSpec as P

H = 16
FD = 16
HD = 128
D = 2048
SPAN = 256
OWN = 4
ROWS = 160
QUADS = 136
LOW = 128
NORM = 153
CHIPS = 32
SLICE = 2 * OWN * ROWS // CHIPS
NORM_FLOOR = 0.0001
BF = jnp.bfloat16
F32 = jnp.float32
CHIP = ("z", "y")


def feature_rows():
    pairs = [(i, j) for i in range(FD) for j in range(i, FD)]
    rows = [u if u < LOW else u + FD + 1 for u in range(QUADS)]
    return pairs, rows


def tables():
    pairs, rows = feature_rows()
    first = np.zeros((ROWS, FD), np.float32)
    second = np.zeros((ROWS, FD), np.float32)
    spread = np.zeros((FD * FD, ROWS), np.float32)
    for (i, j), row in zip(pairs, rows):
        first[row, i] = 1
        second[row, j] = 1
        spread[i * FD + j, row] = 1
        spread[j * FD + i, row] = 1
    for i in range(FD):
        first[LOW + 1 + i, i] = 1
    picks = np.zeros((2, 2, OWN, ROWS, 2 * OWN * FD), np.float32)
    for half in range(2):
        for head in range(OWN):
            at = half * OWN * FD + head * FD
            picks[half, 0, head, :, at : at + FD] = first
            picks[half, 1, head, :, at : at + FD] = second
    lines = np.zeros((8, ROWS), np.float32)
    for (i, j), row in zip(pairs, rows):
        lines[0, row] = (1.0 if i == j else 2.0) * (2.0 * FD) ** -0.5
    lines[0, LOW + 1 : LOW + 1 + FD] = lines[1, LOW + 1 : LOW + 1 + FD] = FD**-0.25
    lines[:3, LOW] = 1.0
    return picks.reshape(2, 2, OWN * ROWS, 2 * OWN * FD), spread, lines


PICKS, SPREAD, LINES = tables()


def is_low(row):
    return (row >= LOW) & (row <= LOW + FD)


def nt(a, b):
    return lax.dot_general(a, b, (((1,), (1,)), ((), ())), preferred_element_type=F32)


def project_kernel(s, hid, wv, wq, wk, picks, q_o, k_o, v_o, send_o, keep_o, wqk):
    step = pl.program_id(0)
    local = (step + 2) % 4

    @pl.when(step == 0)
    def _():
        wqk[:, :128] = wq[...]
        wqk[:, 128:] = wk[...]

    x = hid[0]
    qk = jnp.dot(x, wqk[...], preferred_element_type=F32)
    v = jnp.dot(x, wv[...], preferred_element_type=F32).astype(BF)
    v_o[0] = v
    q_o[0] = qk[:, :128].astype(BF)
    key = qk[:, 128:].astype(BF)
    k_o[0] = key
    key_t = key.astype(F32).T.astype(BF)
    token = s[2] * SPAN + lax.broadcasted_iota(jnp.int32, (1, SPAN), 1)
    live = (token < s[3 + local]).astype(F32)
    row = lax.broadcasted_iota(jnp.int32, (ROWS, SPAN), 0)
    low = is_low(row)
    const = (row == LOW).astype(F32)
    scale = jnp.where(row == LOW, 1.0, jnp.where(low, FD**-0.25, (2.0 * FD) ** -0.5)) * live
    bias = jnp.where(low, scale, 0.0)
    ones = jnp.ones((8, SPAN), BF)
    tail_row = lax.broadcasted_iota(jnp.int32, (8, HD), 0) + (ROWS - 8)
    for h in range(OWN):
        at = h * ROWS
        u = jnp.dot(picks[0, 0, at : at + ROWS], key_t, preferred_element_type=F32)
        w = jnp.dot(picks[0, 1, at : at + ROWS], key_t, preferred_element_type=F32)
        feats = ((u + const) * (w * scale + bias)).astype(BF)
        state = jnp.dot(feats, v[:, h * HD : (h + 1) * HD], preferred_element_type=F32)
        norm = nt(ones, feats)
        rest = jnp.concatenate([norm[:, HD:], jnp.zeros((8, 2 * HD - ROWS), F32)], axis=1)
        tail = state[ROWS - 8 :]
        tail = jnp.where(tail_row == NORM, norm[:, :HD], jnp.where(tail_row == NORM + 1, rest, tail))
        packed = jnp.concatenate([state[: ROWS - 8], tail], axis=0).astype(BF)

        @pl.when(step < 2)
        def _():
            send_o[0, at : at + ROWS] = packed

        @pl.when(step >= 2)
        def _():
            keep_o[0, at : at + ROWS] = packed


def self_kernel(s, q, k, v, picks, lines, num_o, den_o, feat_o):
    local = pl.program_id(0)
    query, key, value = q[0], k[0], v[0]
    tq = lax.broadcasted_iota(jnp.int32, (SPAN, SPAN), 0)
    tk = lax.broadcasted_iota(jnp.int32, (SPAN, SPAN), 1)
    seen = (tk <= tq) & (s[2] * SPAN + tk < s[3 + local])
    lane = lax.broadcasted_iota(jnp.int32, (SPAN, HD), 1)
    scale, bias, const = lines[0:1], lines[1:2], lines[2:3]
    ones = jnp.ones((SPAN, HD), BF)
    den_all = jnp.zeros((SPAN, HD), F32)
    for h in range(OWN):
        at = h * ROWS
        mine = jnp.where(lane // FD == s[1] * OWN + h, query, jnp.zeros_like(query))
        score = nt(mine, key)
        weight = jnp.where(seen, 1.0 + score * (FD**-0.5) + score * score * (0.5 / FD), 0.0).astype(BF)
        num_o[0, :, h * HD : (h + 1) * HD] = jnp.dot(
            weight, value[:, h * HD : (h + 1) * HD], preferred_element_type=F32
        )
        den = jnp.dot(weight, ones, preferred_element_type=F32)
        den_all = jnp.where(lane == h, den, den_all)
        u = nt(query, picks[0, 0, at : at + ROWS])
        w = nt(query, picks[0, 1, at : at + ROWS])
        feat_o[0, h] = ((u + const) * (w * scale + bias)).astype(BF)
    den_o[0] = den_all


def scan_kernel(s, pieces, out):
    before = jnp.zeros((SLICE, HD), F32)
    for chip in range(CHIPS):
        out[chip, :SLICE] = before.astype(BF)
        before = before + pieces[chip].astype(F32)
    total = before.astype(BF)
    nothing = jnp.zeros_like(total)
    for chip in range(CHIPS):
        out[chip, SLICE:] = jnp.where(s[7] == chip, total, nothing)


def prefix_kernel(s, back, keep, recv, own_o, other_o):
    before = back[...].reshape(2 * OWN * ROWS, HD).astype(F32)
    second = s[0] == 1
    added = jnp.where(second, recv[...], keep[...]).reshape(2 * OWN * ROWS, HD).astype(F32)
    both = (before + added).astype(BF)
    plain = before.astype(BF)
    own_o[...] = jnp.where(second, both, plain).reshape(2, OWN * ROWS, HD)
    other_o[...] = jnp.where(second, plain, both).reshape(2, OWN * ROWS, HD)


def spread_kernel(back, spread, out, low_o):
    total = back[...].reshape(2 * OWN, ROWS, HD)
    low_o[...] = total[:, LOW:]
    rows = []
    for n in range(2 * OWN):
        wide = jnp.dot(spread[...], total[n], preferred_element_type=F32).astype(BF)
        for f in range(4):
            out[f, n * 64 : (n + 1) * 64] = wide[f * 64 : (f + 1) * 64]
        rows.append(
            jnp.concatenate(
                [total[n, NORM : NORM + 1], total[n, NORM + 1 : NORM + 2, : ROWS - HD]], axis=1
            )
        )
    norm = nt(jnp.concatenate(rows, axis=0), spread[...])
    pad = jnp.zeros((8, 64), F32)
    for f in range(4):
        out[f, 512:] = jnp.concatenate([norm[:, f * 64 : (f + 1) * 64], pad], axis=1).astype(BF)


def attend_kernel(s, first, state, num, den, feat, att_o, square_o):
    step = pl.program_id(0)
    lane = lax.broadcasted_iota(jnp.int32, (SPAN, HD), 1)
    token = s[2] * SPAN + lax.broadcasted_iota(jnp.int32, (SPAN, HD), 0)
    live = token < s[3 + first + step]
    den_all = den[0]
    squares = jnp.zeros((SPAN, HD), F32)
    for h in range(OWN):
        feats = feat[0, h]
        part = state[0, h * ROWS : (h + 1) * ROWS]
        norm = jnp.concatenate([part[NORM : NORM + 1], part[NORM + 1 : NORM + 2, : ROWS - HD]], axis=1)
        total = num[0, :, h * HD : (h + 1) * HD] + jnp.dot(feats, part, preferred_element_type=F32)
        below = nt(feats, jnp.broadcast_to(norm, (HD, ROWS))) + den_all[:, h : h + 1]
        att = jnp.where(live, total / below, 0.0)
        att_o[0, :, h * HD : (h + 1) * HD] = att
        squares = squares + att * att
    ones = jnp.ones((8, HD), F32)
    square_o[0] = lax.dot_general(
        ones, squares, (((1,), (1,)), ((), ())), precision=lax.Precision.HIGHEST, preferred_element_type=F32
    )


def mix_kernel(s, own, other, square, mixed_o):
    step = pl.program_id(0)
    factor = lax.rsqrt(square[0] * (1.0 / D) + NORM_FLOOR)
    column = factor.T[:, :1]

    @pl.when(step < 2)
    def _():
        mixed_o[0] = (own[0] * column).astype(BF)

    @pl.when(step >= 2)
    def _():
        mixed_o[0] = (other[0] * column).astype(BF)


def final_kernel(s, mine, theirs, low_mine, low_theirs, quad_o, low_o, nquad_o, nlow_o):
    prompt = pl.program_id(0)
    local = (prompt + 2 * s[0]) % 4
    keep = s[8 + prompt] == s[2]

    def write(wide, low, at):
        for f in range(4):
            for h in range(OWN):
                piece = wide[f, (at * OWN + h) * 64 : (at * OWN + h + 1) * 64].astype(F32)
                quad_o[0, 0, f * OWN + h] = jnp.where(keep, piece, 0.0)
                norm = wide[f, 512 + at * OWN + h : 513 + at * OWN + h].astype(F32)
                nquad_o[0, 0, f * OWN + h : f * OWN + h + 1] = jnp.where(keep, norm, 0.0)[:, :64]
        for h in range(OWN):
            piece = low[at * OWN + h].astype(F32)
            piece = jnp.where(keep, piece, 0.0)
            low_o[0, 0, h] = piece[: FD + 1]
            at_norm = NORM + 1 - LOW
            nlow_o[0, 0, h : h + 1] = piece[at_norm : at_norm + 1, : FD + 1]

    for at in range(2):

        @pl.when(local == at)
        def _():
            write(mine, low_mine, at)

        @pl.when(local == 2 + at)
        def _():
            write(theirs, low_theirs, at)


def grid_call(kernel, grid, in_specs, out_specs, out_shape, scratch=(), flops=0, scalars=1):
    return pl.pallas_call(
        kernel,
        grid_spec=pltpu.PrefetchScalarGridSpec(
            num_scalar_prefetch=scalars, grid=grid, in_specs=in_specs, out_specs=out_specs, scratch_shapes=scratch
        ),
        out_shape=out_shape,
        cost_estimate=pl.CostEstimate(flops=flops, transcendentals=0, bytes_accessed=1 << 20),
        compiler_params=pltpu.CompilerParams(dimension_semantics=("arbitrary",) * len(grid)),
    )


def shape(dims, dtype=BF):
    return jax.ShapeDtypeStruct(dims, dtype)


def whole(*dims):
    return pl.BlockSpec(dims, lambda i, *_: (0,) * len(dims))


def per_step(*dims):
    return pl.BlockSpec((1,) + dims, lambda i, *_: (i,) + (0,) * len(dims))


def body(hidden_in, w_query, w_key, w_value, lengths, owners):
    core = lax.axis_index("c")
    feat = lax.axis_index("feat")
    chip = lax.axis_index("z") * 4 + lax.axis_index("y")
    seq = chip * 2 + core
    local = (jnp.arange(4) + 2 * core) % 4
    slice_prompt = 2 * core + chip // 16
    s = jnp.concatenate(
        [
            jnp.stack([core, feat % 2, seq]).astype(jnp.int32),
            lengths[local],
            (owners[slice_prompt] // 2)[None],
            owners,
            (feat // 2)[None].astype(jnp.int32),
        ]
    )
    picks = jnp.asarray(PICKS, BF)
    spread = jnp.asarray(SPREAD, BF)
    swap = [(0, 1), (1, 0)]

    picks_spec = pl.BlockSpec((1, 2, OWN * ROWS, 128), lambda i, s: (s[1], 0, 0, 0))
    q, k, v, send, keep = grid_call(
        project_kernel,
        (4,),
        [
            pl.BlockSpec((1, SPAN, D), lambda i, s: ((i + 2 + 2 * s[0]) % 4, 0, 0)),
            whole(D, 512),
            pl.BlockSpec((D, 128), lambda i, s: (0, s[12])),
            pl.BlockSpec((D, 128), lambda i, s: (0, s[12])),
            picks_spec,
        ],
        [
            pl.BlockSpec((1, SPAN, 128), lambda i, s: ((i + 2) % 4, 0, 0)),
            pl.BlockSpec((1, SPAN, 128), lambda i, s: ((i + 2) % 4, 0, 0)),
            pl.BlockSpec((1, SPAN, 512), lambda i, s: ((i + 2) % 4, 0, 0)),
            pl.BlockSpec((1, OWN * ROWS, HD), lambda i, s: (jnp.minimum(i, 1), 0, 0)),
            pl.BlockSpec((1, OWN * ROWS, HD), lambda i, s: (jnp.maximum(i - 2, 0), 0, 0)),
        ],
        [
            shape((4, SPAN, 128)),
            shape((4, SPAN, 128)),
            shape((4, SPAN, 512)),
            shape((2, OWN * ROWS, HD)),
            shape((2, OWN * ROWS, HD)),
        ],
        [pltpu.VMEM((D, 256), BF)],
        flops=3_000_000_000,
    )(s, hidden_in, w_value, w_query, w_key, picks)

    recv = lax.ppermute(send, "c", swap)
    pair = (keep.astype(F32) + recv.astype(F32)).astype(BF).reshape(CHIPS, SLICE, HD)
    pieces = lax.all_to_all(pair, CHIP, 0, 0)

    num, den, feats = grid_call(
        self_kernel,
        (4,),
        [per_step(SPAN, 128), per_step(SPAN, 128), per_step(SPAN, 512), picks_spec, whole(8, ROWS)],
        [per_step(SPAN, 512), per_step(SPAN, 128), per_step(OWN, SPAN, ROWS)],
        [shape((4, SPAN, 512), F32), shape((4, SPAN, 128), F32), shape((4, OWN, SPAN, ROWS))],
        flops=2_000_000_000,
    )(s, q, k, v, picks, jnp.asarray(LINES))

    both = grid_call(
        scan_kernel,
        (1,),
        [whole(CHIPS, SLICE, HD)],
        whole(CHIPS, 2 * SLICE, HD),
        shape((CHIPS, 2 * SLICE, HD)),
    )(s, pieces)
    back = lax.all_to_all(both, CHIP, 0, 0)
    back_spec = [pl.BlockSpec((CHIPS, SLICE, HD), functools.partial(lambda n, i, *_: (0, n, 0), n)) for n in range(2)]
    half = whole(2, OWN * ROWS, HD)
    own_state, their_state = grid_call(
        prefix_kernel,
        (1,),
        [back_spec[0], half, half],
        [half, half],
        [shape((2, OWN * ROWS, HD)), shape((2, OWN * ROWS, HD))],
    )(s, back, keep, recv)
    other_state = lax.ppermute(their_state, "c", swap)

    wide, low = grid_call(
        spread_kernel,
        (1,),
        [back_spec[1], whole(FD * FD, ROWS)],
        [whole(4, 520, HD), whole(2 * OWN, ROWS - LOW, HD)],
        [shape((4, 520, HD)), shape((2 * OWN, ROWS - LOW, HD))],
        scalars=0,
    )(back, spread)
    wide = lax.all_to_all(wide, "feat", 0, 0)

    def attend(state, first):
        shifted = lambda *dims: pl.BlockSpec((1,) + dims, lambda i, *_: (i + first,) + (0,) * len(dims))
        return grid_call(
            lambda s, *refs: attend_kernel(s, first, *refs),
            (2,),
            [per_step(OWN * ROWS, HD), shifted(SPAN, 512), shifted(SPAN, 128), shifted(OWN, SPAN, ROWS)],
            [per_step(SPAN, 512), per_step(8, SPAN)],
            [shape((2, SPAN, 512), F32), shape((2, 8, SPAN), F32)],
            flops=500_000_000,
        )(s, state, num, den, feats)

    own_att, own_square = attend(own_state, 0)
    other_att, other_square = attend(other_state, 2)
    square = jnp.concatenate([own_square[:, :1], other_square[:, :1]], axis=0)
    square = square + lax.ppermute(square, "feat", [(n, n ^ 1) for n in range(4)])
    square = square + lax.ppermute(square, "feat", [(n, 3 - n) for n in range(4)])
    mixed = grid_call(
        mix_kernel,
        (4,),
        [
            pl.BlockSpec((1, SPAN, 512), lambda i, s: (jnp.minimum(i, 1), 0, 0)),
            pl.BlockSpec((1, SPAN, 512), lambda i, s: (jnp.maximum(i - 2, 0), 0, 0)),
            per_step(1, SPAN),
        ],
        pl.BlockSpec((1, SPAN, 512), lambda i, s: ((i + 2 * s[0]) % 4, 0, 0)),
        shape((4, SPAN, 512)),
    )(s, own_att, other_att, square)

    their_wide = lax.ppermute(wide, "c", swap)
    their_low = lax.ppermute(low, "c", swap)
    quad, low_out, norm_quad, norm_low = grid_call(
        final_kernel,
        (4,),
        [
            whole(4, 520, HD),
            whole(4, 520, HD),
            whole(2 * OWN, ROWS - LOW, HD),
            whole(2 * OWN, ROWS - LOW, HD),
        ],
        [
            pl.BlockSpec((1, 1, H, 64, HD), lambda i, s: (0, i, 0, 0, 0)),
            pl.BlockSpec((1, 1, OWN, FD + 1, HD), lambda i, s: (0, i, 0, 0, 0)),
            pl.BlockSpec((1, 1, H, 64), lambda i, s: (0, i, 0, 0)),
            pl.BlockSpec((1, 1, OWN, FD + 1), lambda i, s: (0, i, 0, 0)),
        ],
        [
            shape((1, 4, H, 64, HD), F32),
            shape((1, 4, OWN, FD + 1, HD), F32),
            shape((1, 4, H, 64), F32),
            shape((1, 4, OWN, FD + 1), F32),
        ],
    )(s, wide, their_wide, low, their_low)
    return mixed, quad, low_out, norm_quad, norm_low


def solution(mesh):
    torus = Mesh(mesh.devices.reshape(8, 4, 2, 4), ("z", "y", "c", "feat"))
    seq = ("z", "y", "c")
    return jax.shard_map(
        body,
        mesh=torus,
        in_specs=(P(None, seq, None), P(), P(), P(None, "feat"), P(), P()),
        out_specs=(
            P(None, seq, "feat"),
            P(seq, None, None, "feat", None),
            P(seq, None, "feat", None, None),
            P(seq, None, None, "feat"),
            P(seq, None, "feat", None),
        ),
        check_vma=False,
    )
```

time: 379 us -> 129 us (0.34); the launches traced: 373 us -> 128 us
  waiting for transfers between devices: 162 us -> 6.33 us
  blocking collectives: 120 us -> 44.7 us
  Pallas kernels: 0 us -> 45.8 us
  matrix products: 39.3 us -> 0 us
  other arithmetic: 20.1 us -> 1.83 us
  between operations: 15.7 us -> 3.37 us
  starting transfers between devices: 7.87 us -> 17.8 us
    all_gather x9 -> x0, blocking collectives: 113 us -> none  [carried_in(): lax.all_gather(part.astype(kind), axis)]
    psum x1 -> x0, waiting for transfers between devices: 83.4 us -> none  [in_one(): total = lax.psum(jnp.concatenate([a.ravel() for a in arrays]), axis)]
    all_gather x3 -> x0, waiting for transfers between devices: 68.5 us -> none  [carried_in(): lax.all_gather(part.astype(kind), axis)]
    pallas_call x0 -> x9, Pallas kernels: none -> 45.8 us  [the longest x1 13.5 us: body(): grid_call(project_kernel, (4,), [pl.BlockSpec((1, SPAN, D), lambda i, s:...]
    all_to_all x0 -> x2, blocking collectives: none -> 44.7 us  [the longest x1 22.6 us: body(): back = lax.all_to_all(both, CHIP, 0, 0)]
    dot_general x11 -> x0, matrix products: 39.3 us -> none  [the longest x1 10.5 us: body(): jnp.einsum('pchf,phfd->pchd', query_quad, pre_quad, precision=highest)]
    ppermute x0 -> x6, starting transfers between devices: none -> 13.8 us  [the longest x1 5.11 us: body(): their_wide = lax.ppermute(wide, 'c', swap)]
    all_to_all x2 -> x1, waiting for transfers between devices: 9.88 us -> 0.19 us  [body(): wide = lax.all_to_all(wide, 'feat', 0, 0)]
  transfers between devices with their start and end apart: 6 -> 7, of which waited for: 5 -> 4; matrix products, arithmetic and copies ran while one was open for 9% -> 2% of each run, Pallas kernels for 0% -> 18%
where the time goes in v1:
time: 129 us; the launch traced here: 128 us
  Pallas kernels  45.8 us (36%)
  blocking collectives  44.7 us (35%)
  starting transfers between devices  17.8 us (14%)
  local copies, waits for them, and re-layouts  8.37 us (6%)
  waiting for transfers between devices  6.33 us (5%)
  between operations  3.37 us (3%)
  other arithmetic  1.83 us (1%)
    all_to_all x1, blocking collectives, body(): back = lax.all_to_all(both, CHIP, 0, 0)  22.6 us
    all_to_all x1, blocking collectives, body(): pieces = lax.all_to_all(pair, CHIP, 0, 0)  22.2 us
    pallas_call x1, Pallas kernels, body(): grid_call(project_kernel, (4,), [pl.BlockSpec((1, SPAN, D), lambda i, s:...  13.5 us
    pallas_call x2, Pallas kernels, attend(): grid_call(lambda s, *refs: attend_kernel(s, first, *refs), (2,), [per_ste...  8.16 us
    pallas_call x1, Pallas kernels, body(): grid_call(self_kernel, (4,), [per_step(SPAN, 128), per_step(SPAN, 128), p...  7.82 us
    ppermute x1, starting transfers between devices, body(): their_wide = lax.ppermute(wide, 'c', swap)  5.11 us
    pallas_call x1, Pallas kernels, body(): grid_call(mix_kernel, (4,), [pl.BlockSpec((1, SPAN, 512), lambda i, s: (j...  4.83 us
    all_to_all x1, starting transfers between devices, body(): wide = lax.all_to_all(wide, 'feat', 0, 0)  4.02 us
  transfers between devices with their start and end apart: 7, of which 4 were waited for; matrix products, arithmetic and copies ran while one was open for 2% of the time, Pallas kernels for 18%

profile of v1, /device:TPU:1, one launch (start us, length us, event | category | flops | bytes accessed | tf_op | source)
XLA Modules:
  0.0 128.3 jit_solution(8317471588649474057)
XLA Ops:
  0.6 0.0 copy-start
  0.7 1.2 dynamic_slice.3
  4.6 0.0 copy-done
  4.6 0.6 gather_fusion
  5.2 1.3 concatenate.6.s
  6.5 13.5 %shard_map.128 = (bf16[4,256,128]{2,1,0:T(8,128)(2,1)}, bf16[4,256,128]{2,1,0:T(8,128)(2,1)}, bf16[4,256,512]{2,1,0:T(8,128)(2,1)}, bf16[2,640,128]{2,1,0:T(8,128)(2,1)}, bf16[2,640,128]{2,1,0:T(8,128)(2,1)}) custom-call(s32[13]{0:T(128)} %concatenate.6.s, bf16[4,256,2048]{2,1,0:T(8,128)(2,1)} %hid.1, bf16[2048,512]{1,0:T(8,128)(2,1)} %wv.1, ...), custom_call_target="tpu_custom_call" | custom-call | flops 3000000000 | bytes 1048576 | tf_op jit(solution)/shard_map/pallas_call | solution.py:297
  20.0 3.2 %collective-permute-start = (bf16[2,640,128]{2,1,0:T(8,128)(2,1)}, bf16[2,640,128]{2,1,0:T(8,128)(2,1)S(1)}, u32[]{:S(2)}, u32[]{:S(2)}) collective-permute-start(bf16[2,640,128]{2,1,0:T(8,128)(2,1)} %get-tuple-element.26), channel_id=1, source_target_pairs={{0,4},{4,0},{1,5},{5,1},{2,6},{6,2},{3,7},{7,3},{8,12},{12,8},{9,1... | collective-permute-start | bytes 983048 | tf_op jit(solution)/shard_map/ppermute | solution.py:325
  23.2 1.5 %collective-permute-done.recv = bf16[2,640,128]{2,1,0:T(8,128)(2,1)S(1)} collective-permute-done((bf16[2,640,128]{2,1,0:T(8,128)(2,1)}, bf16[2,640,128]{2,1,0:T(8,128)(2,1)S(1)}, u32[]{:S(2)}, u32[]{:S(2)}) %collective-permute-start) | collective-permute-done | bytes 327712 | tf_op jit(solution)/shard_map/ppermute | solution.py:325
  24.7 0.0 copy-start.2
  24.7 1.2 add_convert_fusion
  25.9 22.2 %all_to_all.15.pieces = bf16[32,40,128]{2,1,0:T(8,128)(2,1)} all-to-all(bf16[32,40,128]{2,1,0:T(8,128)(2,1)S(1)} %bitcast.9), channel_id=1, replica_groups=mesh['z'=8,'y'=4,'c'=2,'feat'=4] {'z','y'}, dimensions={0} | all-to-all | bytes 655360 | tf_op jit(solution)/shard_map/all_to_all | solution.py:327
  48.0 2.6 %shard_map.129 = bf16[32,80,128]{2,1,0:T(8,128)(2,1)} custom-call(s32[13]{0:T(128)} %concatenate.6.s, bf16[32,40,128]{2,1,0:T(8,128)(2,1)} %all_to_all.15.pieces), custom_call_target="tpu_custom_call" | custom-call | bytes 1048576 | tf_op jit(solution)/shard_map/pallas_call | solution.py:338
  50.6 22.6 %all_to_all.16.back = bf16[32,80,128]{2,1,0:T(8,128)(2,1)} all-to-all(bf16[32,80,128]{2,1,0:T(8,128)(2,1)} %shard_map.129), channel_id=1, replica_groups=mesh['z'=8,'y'=4,'c'=2,'feat'=4] {'z','y'}, dimensions={0} | all-to-all | bytes 1310720 | tf_op jit(solution)/shard_map/all_to_all | solution.py:345
  73.2 2.3 %shard_map.135 = (bf16[4,520,128]{2,1,0:T(8,128)(2,1)}, bf16[8,32,128]{2,1,0:T(8,128)(2,1)}) custom-call(bf16[32,80,128]{2,1,0:T(8,128)(2,1)} %all_to_all.16.back, bf16[256,160]{1,0:T(8,128)(2,1)} %constant.82.clone.spread), custom_call_target="tpu_custom_call" | custom-call | bytes 1048576 | tf_op jit(solution)/shard_map/pallas_call | solution.py:357
  75.5 0.0 copy-done.2
  75.5 4.0 %all-to-all-start.2 = ((bf16[4,520,128]{2,1,0:T(8,128)(2,1)}), bf16[4,520,128]{2,1,0:T(8,128)(2,1)S(1)}, u32[]{:S(2)}, u32[]{:S(2)}) async-start(bf16[4,520,128]{2,1,0:T(8,128)(2,1)} %get-tuple-element.39), calls=%async_computation.2 | async-start | bytes 1064960 | tf_op jit(solution)/shard_map/all_to_all | solution.py:365
  79.5 2.8 %shard_map.130 = (bf16[2,640,128]{2,1,0:T(8,128)(2,1)}, bf16[2,640,128]{2,1,0:T(8,128)(2,1)}) custom-call(s32[13]{0:T(128)} %concatenate.6.s, bf16[32,80,128]{2,1,0:T(8,128)(2,1)} %all_to_all.16.back, bf16[2,640,128]{2,1,0:T(8,128)(2,1)} %get-tuple-element.25.keep, bf16[2,640,128]{2,1,0:T(8,128)(2,1)} %copy-done.2), custom_call_target="tpu_custom_call" | custom-call | bytes 1048576 | tf_op jit(solution)/shard_map/pallas_call | solution.py:348
  82.3 4.0 %collective-permute-start.1 = (bf16[2,640,128]{2,1,0:T(8,128)(2,1)}, bf16[2,640,128]{2,1,0:T(8,128)(2,1)S(1)}, u32[]{:S(2)}, u32[]{:S(2)}) collective-permute-start(bf16[2,640,128]{2,1,0:T(8,128)(2,1)} %get-tuple-element.35), channel_id=1, source_target_pairs={{0,4},{4,0},{1,5},{5,1},{2,6},{6,2},{3,7},{7,3},{8,12},{12,8},{9,1... | collective-permute-start | bytes 983048 | tf_op jit(solution)/shard_map/ppermute | solution.py:355
  86.3 0.2 all-to-all-done.2.mine
  86.5 0.0 copy-start.1
  86.5 5.1 %collective-permute-start.4 = (bf16[4,520,128]{2,1,0:T(8,128)(2,1)S(1)}, bf16[4,520,128]{2,1,0:T(8,128)(2,1)S(1)}, u32[]{:S(2)}, u32[]{:S(2)}) collective-permute-start(bf16[4,520,128]{2,1,0:T(8,128)(2,1)S(1)} %all-to-all-done.2.mine), channel_id=1, source_target_pairs={{0,4},{4,0},{1,5},{5,1},{2,6},{6,2},{3,7},{7,3},{8,12},{12,8},{9,1... | collective-permute-start | bytes 1597448 | tf_op jit(solution)/shard_map/ppermute | solution.py:395
  91.6 7.8 %shard_map.131 = (f32[4,256,512]{2,1,0:T(8,128)}, f32[4,256,128]{2,1,0:T(8,128)}, bf16[4,4,256,160]{3,2,1,0:T(8,128)(2,1)}) custom-call(s32[13]{0:T(128)} %concatenate.6.s, bf16[4,256,128]{2,1,0:T(8,128)(2,1)} %get-tuple-element.28.q, bf16[4,256,128]{2,1,0:T(8,128)(2,1)} %get-tuple-element.29.k, bf16[4,256,512]{2,1,0:T(8,128)(2,1)} %get-tuple-element.30.v, ...), custom_call_target="tpu_custom_call" | custom-call | flops 2000000000 | bytes 1048576 | tf_op jit(solution)/shard_map/pallas_call | solution.py:329
  99.4 0.0 copy-done.1
  99.4 4.1 %shard_map.132 = (f32[2,256,512]{2,1,0:T(8,128)}, f32[2,8,256]{2,1,0:T(8,128)}) custom-call(s32[13]{0:T(128)} %concatenate.6.s, bf16[2,640,128]{2,1,0:T(8,128)(2,1)} %get-tuple-element.27.refs_0_, f32[4,256,512]{2,1,0:T(8,128)} %get-tuple-element.31.refs_1_, f32[4,256,128]{2,1,0:T(8,128)} %get-tuple-element.32.refs_2_, ...), custom_call_target="tpu_custom_call" | custom-call | flops 500000000 | bytes 1048576 | tf_op jit(solution)/shard_map/pallas_call | solution.py:369
  103.5 0.7 slice.6
  104.2 0.0 copy-start.5
  104.2 0.0 collective-permute-done.1.refs_0_
  104.2 0.0 copy-start.4
  104.2 0.7 copy-done.4
  104.9 4.1 %shard_map.133 = (f32[2,256,512]{2,1,0:T(8,128)}, f32[2,8,256]{2,1,0:T(8,128)}) custom-call(s32[13]{0:T(128)} %concatenate.6.s, bf16[2,640,128]{2,1,0:T(8,128)(2,1)} %copy-done.4, f32[4,256,512]{2,1,0:T(8,128)} %get-tuple-element.31.refs_1_, f32[4,256,128]{2,1,0:T(8,128)} %get-tuple-element.32.refs_2_, bf16[4,4,256,160]{3,2,1,0:T(8,128)(2,1)} %get-tuple-element.33.refs_3_), custom_call_target="tpu_custom_call" | custom-call | flops 500000000 | bytes 1048576 | tf_op jit(solution)/shard_map/pallas_call | solution.py:369
  109.0 0.7 slice.7
  109.7 0.3 collective-permute-start.2
  110.0 0.0 copy-done.5
  110.0 0.3 collective-permute-start.5
  110.3 1.9 %collective-permute-done.2 = f32[4,1,256]{2,1,0:T(1,128)S(1)} collective-permute-done((f32[4,1,256]{2,1,0:T(1,128)S(1)}, f32[4,1,256]{2,1,0:T(1,128)S(1)}, u32[]{:S(2)}, u32[]{:S(2)}) %collective-permute-start.2) | collective-permute-done | bytes 4128 | tf_op jit(solution)/shard_map/ppermute | solution.py:381
  112.2 1.0 collective-permute-start.3
  113.2 2.8 %collective-permute-done.3 = f32[4,1,256]{2,1,0:T(1,128)S(1)} collective-permute-done((f32[4,1,256]{2,1,0:T(1,128)S(1)}, f32[4,1,256]{2,1,0:T(1,128)S(1)}, u32[]{:S(2)}, u32[]{:S(2)}) %collective-permute-start.3) | collective-permute-done | bytes 4128 | tf_op jit(solution)/shard_map/ppermute | solution.py:382
  116.0 0.6 add.75.square
  116.6 4.8 %shard_map.134 = bf16[4,256,512]{2,1,0:T(8,128)(2,1)} custom-call(s32[13]{0:T(128)} %concatenate.6.s, f32[2,256,512]{2,1,0:T(8,128)} %get-tuple-element.34.own, f32[2,256,512]{2,1,0:T(8,128)} %get-tuple-element.36.other, f32[4,1,256]{2,1,0:T(1,128)} %add.75.square), custom_call_target="tpu_custom_call" | custom-call | bytes 1048576 | tf_op jit(solution)/shard_map/pallas_call | solution.py:383
  121.4 0.0 collective-permute-done.5.low_theirs
  121.4 0.0 copy-start.6
  121.4 0.0 collective-permute-done.4.theirs
  121.4 0.6 copy-done.6
  122.0 0.0 copy-start.3
  122.0 0.8 copy-done.3
  122.8 3.8 %shard_map.136 = (f32[1,4,16,64,128]{4,3,2,1,0:T(8,128)}, f32[1,4,4,17,128]{4,3,2,1,0:T(8,128)}, f32[1,4,16,64]{3,2,1,0:T(8,128)}, f32[1,4,4,17]{3,2,1,0:T(4,128)}) custom-call(s32[13]{0:T(128)} %concatenate.6.s, bf16[4,520,128]{2,1,0:T(8,128)(2,1)} %copy-done.1, bf16[4,520,128]{2,1,0:T(8,128)(2,1)} %copy-done.3, ...), custom_call_target="tpu_custom_call" | custom-call | bytes 1048576 | tf_op jit(solution)/shard_map/pallas_call | solution.py:397
  126.7 1.6 %copy.15 = f32[1,4,4,17,128]{4,2,3,1,0:T(4,128)} copy(f32[1,4,4,17,128]{4,3,2,1,0:T(8,128)} %get-tuple-element.52) | data formatting | bytes 278528
  (4 shorter events, 0.0 us)
Async XLA Ops:
  0.6 4.0 %copy-start = (s32[4]{0:T(128)S(1)}, s32[4]{0:T(128)}, u32[]{:S(2)}) copy-start(s32[4]{0:T(128)} %param.13) | copy-start | bytes 52
  20.0 4.7 %collective-permute-start = (bf16[2,640,128]{2,1,0:T(8,128)(2,1)}, bf16[2,640,128]{2,1,0:T(8,128)(2,1)S(1)}, u32[]{:S(2)}, u32[]{:S(2)}) collective-permute-start(bf16[2,640,128]{2,1,0:T(8,128)(2,1)} %get-tuple-element.26), channel_id=1, source_target_pairs={{0,4},{4,0},{1,5},{5,1},{2,6},{6,2},{3,7},{7,3},{8,12},{12,8},{9,1... | collective-permute-start | bytes 983048 | tf_op jit(solution)/shard_map/ppermute | solution.py:325
  24.7 50.8 %copy-start.2 = (bf16[2,640,128]{2,1,0:T(8,128)(2,1)}, bf16[2,640,128]{2,1,0:T(8,128)(2,1)S(1)}, u32[]{:S(2)}) copy-start(bf16[2,640,128]{2,1,0:T(8,128)(2,1)S(1)} %collective-permute-done.recv) | copy-start | bytes 983044
  75.5 11.0 %all-to-all-start.2 = ((bf16[4,520,128]{2,1,0:T(8,128)(2,1)}), bf16[4,520,128]{2,1,0:T(8,128)(2,1)S(1)}, u32[]{:S(2)}, u32[]{:S(2)}) async-start(bf16[4,520,128]{2,1,0:T(8,128)(2,1)} %get-tuple-element.39), calls=%async_computation.2 | async-start | bytes 1064960 | tf_op jit(solution)/shard_map/all_to_all | solution.py:365
  82.3 21.9 %collective-permute-start.1 = (bf16[2,640,128]{2,1,0:T(8,128)(2,1)}, bf16[2,640,128]{2,1,0:T(8,128)(2,1)S(1)}, u32[]{:S(2)}, u32[]{:S(2)}) collective-permute-start(bf16[2,640,128]{2,1,0:T(8,128)(2,1)} %get-tuple-element.35), channel_id=1, source_target_pairs={{0,4},{4,0},{1,5},{5,1},{2,6},{6,2},{3,7},{7,3},{8,12},{12,8},{9,1... | collective-permute-start | bytes 983048 | tf_op jit(solution)/shard_map/ppermute | solution.py:355
  86.5 12.9 %copy-start.1 = (bf16[4,520,128]{2,1,0:T(8,128)(2,1)}, bf16[4,520,128]{2,1,0:T(8,128)(2,1)S(1)}, u32[]{:S(2)}) copy-start(bf16[4,520,128]{2,1,0:T(8,128)(2,1)S(1)} %all-to-all-done.2.mine) | copy-start | bytes 1597444
  86.5 34.9 %collective-permute-start.4 = (bf16[4,520,128]{2,1,0:T(8,128)(2,1)S(1)}, bf16[4,520,128]{2,1,0:T(8,128)(2,1)S(1)}, u32[]{:S(2)}, u32[]{:S(2)}) collective-permute-start(bf16[4,520,128]{2,1,0:T(8,128)(2,1)S(1)} %all-to-all-done.2.mine), channel_id=1, source_target_pairs={{0,4},{4,0},{1,5},{5,1},{2,6},{6,2},{3,7},{7,3},{8,12},{12,8},{9,1... | collective-permute-start | bytes 1597448 | tf_op jit(solution)/shard_map/ppermute | solution.py:395
  104.2 5.8 %copy-start.5 = (bf16[8,32,128]{2,1,0:T(8,128)(2,1)S(1)}, bf16[8,32,128]{2,1,0:T(8,128)(2,1)}, u32[]{:S(2)}) copy-start(bf16[8,32,128]{2,1,0:T(8,128)(2,1)} %get-tuple-element.40.low_mine) | copy-start | bytes 196612
  104.2 0.7 copy-start.4
  109.7 2.5 %collective-permute-start.2 = (f32[4,1,256]{2,1,0:T(1,128)S(1)}, f32[4,1,256]{2,1,0:T(1,128)S(1)}, u32[]{:S(2)}, u32[]{:S(2)}) collective-permute-start(f32[4,1,256]{2,1,0:T(1,128)S(1)} %pad_maximum_fusion), channel_id=1, source_target_pairs={{0,1},{1,0},{2,3},{3,2},{4,5},{5,4},{6,7},{7,6},{8,9},{9,8},{10,11... | collective-permute-start | bytes 12296 | tf_op jit(solution)/shard_map/ppermute | solution.py:381
  110.0 11.4 %collective-permute-start.5 = (bf16[8,32,128]{2,1,0:T(8,128)(2,1)S(1)}, bf16[8,32,128]{2,1,0:T(8,128)(2,1)S(1)}, u32[]{:S(2)}, u32[]{:S(2)}) collective-permute-start(bf16[8,32,128]{2,1,0:T(8,128)(2,1)S(1)} %copy-done.5), channel_id=1, source_target_pairs={{0,4},{4,0},{1,5},{5,1},{2,6},{6,2},{3,7},{7,3},{8,12},{12,8},{9,1... | collective-permute-start | bytes 196616 | tf_op jit(solution)/shard_map/ppermute | solution.py:396
  112.2 3.8 %collective-permute-start.3 = (f32[4,1,256]{2,1,0:T(1,128)S(1)}, f32[4,1,256]{2,1,0:T(1,128)S(1)}, u32[]{:S(2)}, u32[]{:S(2)}) collective-permute-start(f32[4,1,256]{2,1,0:T(1,128)S(1)} %fusion.2), channel_id=1, source_target_pairs={{0,3},{1,2},{2,1},{3,0},{4,7},{5,6},{6,5},{7,4},{8,11},{9,10},{10,... | collective-permute-start | bytes 12296 | tf_op jit(solution)/shard_map/ppermute | solution.py:382
  121.4 0.6 copy-start.6
  122.0 0.8 copy-start.3

commit v2 on v0

v2 whole, which is shorter than its diff:
```python
import functools

import jax
import jax.numpy as jnp
import numpy as np
from jax import lax
from jax.experimental import pallas as pl
from jax.experimental.pallas import tpu as pltpu
from jax.sharding import Mesh
from jax.sharding import PartitionSpec as P

H = 16
FD = 16
HD = 128
D = 2048
SPAN = 256
OWN = 4
ROWS = 160
QUADS = 136
LOW = 128
NORM = 153
CHIPS = 32
SLICE = 2 * OWN * ROWS // CHIPS
NORM_FLOOR = 0.0001
BF = jnp.bfloat16
F32 = jnp.float32
CHIP = ("z", "y")


def feature_rows():
    pairs = [(i, j) for i in range(FD) for j in range(i, FD)]
    rows = [u if u < LOW else u + FD + 1 for u in range(QUADS)]
    return pairs, rows


def tables():
    pairs, rows = feature_rows()
    first = np.zeros((ROWS, FD), np.float32)
    second = np.zeros((ROWS, FD), np.float32)
    spread = np.zeros((FD * FD, ROWS), np.float32)
    for (i, j), row in zip(pairs, rows):
        first[row, i] = 1
        second[row, j] = 1
        spread[i * FD + j, row] = 1
        spread[j * FD + i, row] = 1
    for i in range(FD):
        first[LOW + 1 + i, i] = 1
    picks = np.zeros((2, 2, OWN, ROWS, 2 * OWN * FD), np.float32)
    for half in range(2):
        for head in range(OWN):
            at = half * OWN * FD + head * FD
            picks[half, 0, head, :, at : at + FD] = first
            picks[half, 1, head, :, at : at + FD] = second
    lines = np.zeros((8, ROWS), np.float32)
    for (i, j), row in zip(pairs, rows):
        lines[0, row] = (1.0 if i == j else 2.0) * (2.0 * FD) ** -0.5
    lines[0, LOW + 1 : LOW + 1 + FD] = lines[1, LOW + 1 : LOW + 1 + FD] = FD**-0.25
    lines[:3, LOW] = 1.0
    return picks.reshape(2, 2, OWN * ROWS, 2 * OWN * FD), spread, lines


PICKS, SPREAD, LINES = tables()


def is_low(row):
    return (row >= LOW) & (row <= LOW + FD)


def nt(a, b):
    return lax.dot_general(a, b, (((1,), (1,)), ((), ())), preferred_element_type=F32)


def place():
    core = lax.axis_index("c")
    chip = lax.axis_index("z") * 4 + lax.axis_index("y")
    return core, chip, chip * 2 + core, lax.axis_index("feat")


CHUNK = 512


def project_kernel(
    lens_h, hid, wv, wq, wk, picks_h, q_o, k_o, v_o, send_o, keep_o, picks, hid_b, wv_b, wqk_b, lens, sems, rest, small
):
    core, _, seq, feat = place()
    lanes = pl.ds(pl.multiple_of(feat // 2 * 128, 128), 128)
    first = (2 + 2 * core) % 4
    early = []
    for n in range(D // CHUNK):
        rows = pl.ds(n * CHUNK, CHUNK)
        early.append(
            [
                pltpu.make_async_copy(hid.at[first, :, rows], hid_b.at[2, :, rows], sems.at[n, 0]),
                pltpu.make_async_copy(wq.at[rows, lanes], wqk_b.at[rows, :128], sems.at[n, 1]),
                pltpu.make_async_copy(wk.at[rows, lanes], wqk_b.at[rows, 128:], sems.at[n, 2]),
                pltpu.make_async_copy(wv.at[rows], wv_b.at[rows], sems.at[n, 3]),
            ]
        )
        for copy in early[-1]:
            copy.start()
    tiny = [
        pltpu.make_async_copy(lens_h, lens, small.at[0]),
        pltpu.make_async_copy(picks_h.at[feat % 2], picks, small.at[1]),
    ]
    for copy in tiny:
        copy.start()
    late = []
    for n, local in enumerate((3, 0, 1)):
        late.append(pltpu.make_async_copy(hid.at[(local + 2 * core) % 4], hid_b.at[local], rest.at[n]))
        late[-1].start()
    row = lax.broadcasted_iota(jnp.int32, (ROWS, SPAN), 0)
    low = is_low(row)
    const = (row == LOW).astype(F32)
    fixed = jnp.where(row == LOW, 1.0, jnp.where(low, FD**-0.25, (2.0 * FD) ** -0.5))
    ones = jnp.ones((8, SPAN), BF)
    tail_row = lax.broadcasted_iota(jnp.int32, (8, HD), 0) + (ROWS - 8)
    for n, local in enumerate((2, 3, 0, 1)):
        if n == 0:
            v = jnp.zeros((SPAN, 512), F32)
            qk = jnp.zeros((SPAN, 256), F32)
            for m in range(D // CHUNK):
                for copy in early[m]:
                    copy.wait()
                rows = slice(m * CHUNK, (m + 1) * CHUNK)
                x = hid_b[local, :, rows]
                qk = qk + jnp.dot(x, wqk_b[rows], preferred_element_type=F32)
                v = v + jnp.dot(x, wv_b[rows], preferred_element_type=F32)
            for copy in tiny:
                copy.wait()
        else:
            late[n - 1].wait()
            x = hid_b[local]
            qk = jnp.dot(x, wqk_b[...], preferred_element_type=F32)
            v = jnp.dot(x, wv_b[...], preferred_element_type=F32)
        v = v.astype(BF)
        key = qk[:, 128:].astype(BF)
        q_o[local] = qk[:, :128].astype(BF)
        v_o[local] = v
        k_o[local] = key
        key_t = key.astype(F32).T.astype(BF)
        token = seq * SPAN + lax.broadcasted_iota(jnp.int32, (1, SPAN), 1)
        scale = jnp.where(token < lens[(local + 2 * core) % 4], fixed, 0.0)
        bias = jnp.where(low, scale, 0.0)
        target = send_o if local >= 2 else keep_o
        for h in range(OWN):
            at = h * ROWS
            u = jnp.dot(picks[0, at : at + ROWS], key_t, preferred_element_type=F32)
            w = jnp.dot(picks[1, at : at + ROWS], key_t, preferred_element_type=F32)
            feats = ((u + const) * (w * scale + bias)).astype(BF)
            state = jnp.dot(feats, v[:, h * HD : (h + 1) * HD], preferred_element_type=F32)
            norm = nt(ones, feats)
            rest_norm = jnp.concatenate([norm[:, HD:], jnp.zeros((8, 2 * HD - ROWS), F32)], axis=1)
            tail = state[ROWS - 8 :]
            tail = jnp.where(tail_row == NORM, norm[:, :HD], jnp.where(tail_row == NORM + 1, rest_norm, tail))
            target[local % 2, at : at + ROWS] = jnp.concatenate([state[: ROWS - 8], tail], axis=0).astype(BF)


def self_kernel(lens, q, k, v, picks, lines, num_o, den_o, feat_o):
    core, _, seq, feat = place()
    tq = lax.broadcasted_iota(jnp.int32, (SPAN, SPAN), 0)
    tk = lax.broadcasted_iota(jnp.int32, (SPAN, SPAN), 1)
    lane = lax.broadcasted_iota(jnp.int32, (SPAN, HD), 1)
    scale, bias, const = lines[0:1], lines[1:2], lines[2:3]
    ones = jnp.ones((SPAN, HD), BF)

    def prompt(local, _):
        query = q[local]
        key = k[local]
        seen = (tk <= tq) & (seq * SPAN + tk < lens[(local + 2 * core) % 4])
        den_all = jnp.zeros((SPAN, HD), F32)
        for h in range(OWN):
            at = h * ROWS
            mine = jnp.where(lane // FD == feat % 2 * OWN + h, query, jnp.zeros_like(query))
            score = nt(mine, key)
            weight = jnp.where(seen, 1.0 + score * (FD**-0.5) + score * score * (0.5 / FD), 0.0).astype(BF)
            value = v[local, :, h * HD : (h + 1) * HD]
            num_o[local, :, h * HD : (h + 1) * HD] = jnp.dot(weight, value, preferred_element_type=F32)
            den = jnp.dot(weight, ones, preferred_element_type=F32)
            den_all = jnp.where(lane == h, den, den_all)
            u = nt(query, picks[0, at : at + ROWS])
            w = nt(query, picks[1, at : at + ROWS])
            feat_o[local, h] = ((u + const) * (w * scale + bias)).astype(BF)
        den_o[local] = den_all
        return _

    lax.fori_loop(0, 4, prompt, 0)


def pair_kernel(keep, recv, after, out):
    pair = (keep[...].astype(F32) + recv[...].astype(F32)).astype(BF)
    out[...] = pair.reshape(CHIPS, SLICE, HD)


def scan_kernel(owners, pieces, out):
    core, chip, _, _ = place()
    home = owners[2 * core + chip // 16] // 2
    before = jnp.zeros((SLICE, HD), F32)
    for n in range(CHIPS):
        out[n, :SLICE] = before.astype(BF)
        before = before + pieces[n].astype(F32)
    total = before.astype(BF)
    nothing = jnp.zeros_like(total)
    for n in range(CHIPS):
        out[n, SLICE:] = jnp.where(home == n, total, nothing)


STATE = 2 * OWN * ROWS
LOW_ROWS = ROWS - LOW
WIDE = 2 * OWN * 64
NORMS = WIDE + 8
SENT = NORMS + 16


def prefix_kernel(back, keep, recv, own_o, other_o):
    before = back[:, :SLICE].reshape(STATE, HD).astype(F32)
    second = lax.axis_index("c") == 1
    added = jnp.where(second, recv[...], keep[...]).reshape(STATE, HD).astype(F32)
    both = (before + added).astype(BF)
    plain = before.astype(BF)
    own_o[...] = jnp.where(second, both, plain).reshape(2, OWN * ROWS, HD)
    other_o[:STATE] = jnp.where(second, plain, both)
    total = back[:, SLICE:].reshape(2 * OWN, ROWS, HD)
    other_o[STATE:] = total[:, LOW:].reshape(2 * OWN * LOW_ROWS, HD)


def norm_row(part):
    return jnp.concatenate([part[NORM : NORM + 1], part[NORM + 1 : NORM + 2, : ROWS - HD]], axis=1)


def spread(total, table, out):
    for n in range(2 * OWN):
        wide = jnp.dot(table[...], total[n], preferred_element_type=F32).astype(BF)
        for f in range(4):
            out[f, n * 64 : (n + 1) * 64] = wide[f * 64 : (f + 1) * 64]
    norm = nt(jnp.concatenate([norm_row(total[n]) for n in range(2 * OWN)], axis=0), table[...])
    pad = jnp.zeros((8, 64), F32)
    for f in range(4):
        out[f, WIDE:NORMS] = jnp.concatenate([norm[:, f * 64 : (f + 1) * 64], pad], axis=1).astype(BF)


def attend(first, lens, state, num, den, feat, att_o):
    core, _, seq, _ = place()
    token = seq * SPAN + lax.broadcasted_iota(jnp.int32, (SPAN, HD), 0)
    ones = jnp.ones((8, HD), F32)
    found = []
    for n in range(2):
        live = token < lens[(first + n + 2 * core) % 4]
        den_all = den[first + n]
        squares = jnp.zeros((SPAN, HD), F32)
        for h in range(OWN):
            feats = feat[first + n, h]
            part = state(n, h)
            total = num[first + n, :, h * HD : (h + 1) * HD] + jnp.dot(feats, part, preferred_element_type=F32)
            below = nt(feats, jnp.broadcast_to(norm_row(part), (HD, ROWS))) + den_all[:, h : h + 1]
            att = jnp.where(live, total / below, 0.0)
            att_o[n, :, h * HD : (h + 1) * HD] = att
            squares = squares + att * att
        sums = lax.dot_general(
            ones,
            squares,
            (((1,), (1,)), ((), ())),
            precision=lax.Precision.HIGHEST,
            preferred_element_type=F32,
        )
        found += [sums[:1, :HD], sums[:1, HD:]]
    return found


def own_kernel(lens, state, num, den, feat, att_o, square_o):
    found = attend(0, lens, lambda n, h: state[n, h * ROWS : (h + 1) * ROWS], num, den, feat, att_o)
    square_o[...] = jnp.concatenate(found + [jnp.zeros((4, HD), F32)], axis=0)


def other_kernel(lens, state, num, den, feat, square, back, table, att_o, sent_o):
    def part(n, h):
        at = (n * OWN + h) * ROWS
        return state[at : at + ROWS]

    found = attend(2, lens, part, num, den, feat, att_o)
    squares = jnp.concatenate([square[:4]] + found, axis=0)
    high = squares.astype(BF)
    rest = (squares - high.astype(F32)).astype(BF)
    for f in range(4):
        sent_o[f, NORMS : NORMS + 8] = high
        sent_o[f, NORMS + 8 :] = rest
    spread(back[:, SLICE:].reshape(2 * OWN, ROWS, HD), table, sent_o)


def mix_kernel(own, other, sent, mixed_o):
    step = pl.program_id(0)
    square = jnp.zeros((8, HD), F32)
    for f in range(4):
        square = square + (sent[f, NORMS : NORMS + 8].astype(F32) + sent[f, NORMS + 8 :].astype(F32))
    factor = lax.rsqrt(square * (1.0 / D) + NORM_FLOOR).T
    lane = lax.broadcasted_iota(jnp.int32, (HD, 8), 1)
    for k in range(2):
        column = jnp.sum(jnp.where(lane == 2 * step + k, factor, 0.0), axis=1, keepdims=True)
        rows = slice(k * HD, (k + 1) * HD)

        @pl.when(step < 2)
        def _():
            mixed_o[0, rows] = (own[step, rows] * column).astype(BF)

        @pl.when(step >= 2)
        def _():
            mixed_o[0, rows] = (other[step - 2, rows] * column).astype(BF)


def final_kernel(owners, mine, theirs, low_mine, low_theirs, quad_o, low_o, nquad_o, nlow_o):
    core, _, seq, _ = place()
    prompt = pl.program_id(0)
    local = (prompt + 2 * core) % 4
    keep = owners[prompt] == seq

    def write(wide, low, at):
        for f in range(4):
            for h in range(OWN):
                piece = wide[f, (at * OWN + h) * 64 : (at * OWN + h + 1) * 64].astype(F32)
                quad_o[0, 0, f * OWN + h] = jnp.where(keep, piece, 0.0)
                norm = wide[f, WIDE + at * OWN + h : WIDE + 1 + at * OWN + h].astype(F32)
                nquad_o[0, 0, f * OWN + h : f * OWN + h + 1] = jnp.where(keep, norm, 0.0)[:, :64]
        for h in range(OWN):
            piece = low[pl.ds(STATE + (at * OWN + h) * LOW_ROWS, LOW_ROWS)].astype(F32)
            piece = jnp.where(keep, piece, 0.0)
            for r in range(FD + 1):
                low_o[0, 0, r, h : h + 1] = piece[r : r + 1]
            at_norm = NORM + 1 - LOW
            nlow_o[0, 0, h : h + 1] = piece[at_norm : at_norm + 1, : FD + 1]

    for at in range(2):

        @pl.when(local == at)
        def _():
            write(mine, low_mine, at)

        @pl.when(local == 2 + at)
        def _():
            write(theirs, low_theirs, at)


SMEM = pl.BlockSpec(memory_space=pltpu.SMEM)
VMEM = pl.BlockSpec(memory_space=pltpu.VMEM)
ANY = pl.BlockSpec(memory_space=pl.ANY)
MIB = 1 << 20


def near(*arrays):
    return [pltpu.with_memory_space_constraint(a, pltpu.VMEM) for a in arrays]


def call(kernel, in_specs, out_shape, out_specs=None, grid=(), scratch=(), flops=0, limit=16):
    if out_specs is None:
        out_specs = jax.tree.map(lambda _: VMEM, out_shape, is_leaf=lambda x: not isinstance(x, (list, tuple)))
    return pl.pallas_call(
        kernel,
        grid=grid,
        in_specs=in_specs,
        out_specs=out_specs,
        out_shape=out_shape,
        scratch_shapes=scratch,
        cost_estimate=pl.CostEstimate(flops=flops, transcendentals=0, bytes_accessed=MIB),
        compiler_params=pltpu.CompilerParams(
            dimension_semantics=("arbitrary",) * len(grid), vmem_limit_bytes=limit * MIB
        ),
    )


def far(dims, dtype=BF):
    return jax.ShapeDtypeStruct(dims, dtype)


def shape(dims, dtype=BF):
    return pltpu.VMEM(dims, dtype)


def held(*arrays):
    return [pltpu.with_memory_space_constraint(a, pltpu.HBM) for a in arrays]


def body(hidden_in, w_query, w_key, w_value, lengths, owners):
    swap = [(0, 1), (1, 0)]
    half = (2, OWN * ROWS, HD)
    packed = OWN * ROWS

    q, k, v, send, keep, picks = call(
        project_kernel,
        [ANY] * 6,
        [
            shape((4, SPAN, 128)),
            shape((4, SPAN, 128)),
            shape((4, SPAN, 512)),
            shape(half),
            shape(half),
            shape((2, packed, 128)),
        ],
        scratch=[
            pltpu.VMEM((4, SPAN, D), BF),
            pltpu.VMEM((D, 512), BF),
            pltpu.VMEM((D, 256), BF),
            pltpu.SMEM((4,), jnp.int32),
            pltpu.SemaphoreType.DMA((D // CHUNK, 4)),
            pltpu.SemaphoreType.DMA((3,)),
            pltpu.SemaphoreType.DMA((2,)),
        ],
        flops=3_000_000_000,
        limit=24,
    )(*held(lengths, hidden_in, w_value, w_query, w_key, jnp.asarray(PICKS, BF)))

    recv = lax.ppermute(send, "c", swap)
    num, den, feats = call(
        self_kernel,
        [SMEM] + [VMEM] * 5,
        [shape((4, SPAN, 512), F32), shape((4, SPAN, 128), F32), shape((4, OWN, SPAN, ROWS))],
        flops=3_000_000_000,
    )(lengths, *near(q, k, v, picks, jnp.asarray(LINES)))
    pair = call(pair_kernel, [VMEM, VMEM, ANY], shape((CHIPS, SLICE, HD)))(*near(keep, recv, den))
    pieces = lax.all_to_all(pair, CHIP, 0, 0)
    both = call(scan_kernel, [SMEM, VMEM], shape((CHIPS, 2 * SLICE, HD)))(owners, *near(pieces))
    back = lax.all_to_all(both, CHIP, 0, 0)
    own_state, given = call(
        prefix_kernel, [VMEM] * 3, [shape(half), shape((STATE + 2 * OWN * LOW_ROWS, HD))]
    )(*near(back, keep, recv))
    taken = lax.ppermute(given, "c", swap)

    own_att, square = call(
        own_kernel,
        [SMEM] + [VMEM] * 4,
        [shape((2, SPAN, 512), F32), shape((8, HD), F32)],
        flops=500_000_000,
    )(lengths, *near(own_state, num, den, feats))
    other_att, sent = call(
        other_kernel,
        [SMEM] + [VMEM] * 7,
        [shape((2, SPAN, 512), F32), shape((4, SENT, HD))],
        flops=500_000_000,
    )(lengths, *near(taken, num, den, feats, square, back, jnp.asarray(SPREAD, BF)))
    mine = lax.all_to_all(sent, "feat", 0, 0)
    theirs = lax.ppermute(mine, "c", swap)
    mixed = call(
        mix_kernel,
        [VMEM] * 3,
        far((4, SPAN, 512)),
        pl.BlockSpec((1, SPAN, 512), lambda i: ((i + 2 * lax.axis_index("c")) % 4, 0, 0)),
        (4,),
        flops=500_000_000,
    )(*near(own_att, other_att, mine))

    quad, low_out, norm_quad, norm_low = call(
        final_kernel,
        [SMEM] + [VMEM] * 4,
        [
            far((1, 4, H, 64, HD), F32),
            far((1, 4, FD + 1, OWN, HD), F32),
            far((1, 4, H, 64), F32),
            far((1, 4, OWN, FD + 1), F32),
        ],
        [
            pl.BlockSpec((1, 1, H, 64, HD), lambda i: (0, i, 0, 0, 0)),
            pl.BlockSpec((1, 1, FD + 1, OWN, HD), lambda i: (0, i, 0, 0, 0)),
            pl.BlockSpec((1, 1, H, 64), lambda i: (0, i, 0, 0)),
            pl.BlockSpec((1, 1, OWN, FD + 1), lambda i: (0, i, 0, 0)),
        ],
        (4,),
    )(owners, *near(mine, theirs, given, taken))
    return mixed, quad, jnp.transpose(low_out, (0, 1, 3, 2, 4)), norm_quad, norm_low


def solution(mesh):
    torus = Mesh(mesh.devices.reshape(8, 4, 2, 4), ("z", "y", "c", "feat"))
    seq = ("z", "y", "c")
    return jax.shard_map(
        body,
        mesh=torus,
        in_specs=(P(None, seq, None), P(), P(), P(None, "feat"), P(), P()),
        out_specs=(
            P(None, seq, "feat"),
            P(seq, None, None, "feat", None),
            P(seq, None, "feat", None, None),
            P(seq, None, None, "feat"),
            P(seq, None, "feat", None),
        ),
        check_vma=False,
    )
```

time: 379 us -> 91.7 us (0.24); the launches traced: 373 us -> 91.5 us
  waiting for transfers between devices: 162 us -> 0.01 us
  blocking collectives: 120 us -> 57.7 us
  matrix products: 39.3 us -> 0 us
  Pallas kernels: 0 us -> 25 us
  other arithmetic: 20.1 us -> 0 us
  between operations: 15.7 us -> 0.72 us
  local copies, waits for them, and re-layouts: 7.84 us -> 0.05 us
    all_gather x9 -> x0, blocking collectives: 113 us -> none  [carried_in(): lax.all_gather(part.astype(kind), axis)]
    psum x1 -> x0, waiting for transfers between devices: 83.4 us -> none  [in_one(): total = lax.psum(jnp.concatenate([a.ravel() for a in arrays]), axis)]
    all_gather x3 -> x0, waiting for transfers between devices: 68.5 us -> none  [carried_in(): lax.all_gather(part.astype(kind), axis)]
    all_to_all x0 -> x3, blocking collectives: none -> 57.7 us  [the longest x1 22.5 us: body(): pieces = lax.all_to_all(pair, CHIP, 0, 0)]
    dot_general x11 -> x0, matrix products: 39.3 us -> none  [the longest x1 10.5 us: body(): jnp.einsum('pchf,phfd->pchd', query_quad, pre_quad, precision=highest)]
    pallas_call x0 -> x9, Pallas kernels: none -> 25 us  [the longest x1 9.94 us: body(): call(project_kernel, [ANY] * 6, [shape((4, SPAN, 128)), shape((4, SPAN, 1...]
    all_to_all x2 -> x0, waiting for transfers between devices: 9.88 us -> none  [the longest x1 7.61 us: body(): lax.all_to_all(final_quad.astype(jnp.bfloat16), 'feat', split_axis=2, con...]
    convert_element_type x17 -> x0, other arithmetic: 9.17 us -> none  [the longest x10 6.84 us: carried_in(): part.astype(kind)]
  transfers between devices with their start and end apart: 6 -> 3, of which waited for: 5 -> 0; matrix products, arithmetic and copies ran while one was open for 9% -> 0% of each run, Pallas kernels for 0% -> 10%
where the time goes in v2:
time: 91.7 us; the launch traced here: 91.5 us
  blocking collectives  57.7 us (63%)
  Pallas kernels  25 us (27%)
  starting transfers between devices  8 us (9%)
    all_to_all x1, blocking collectives, body(): pieces = lax.all_to_all(pair, CHIP, 0, 0)  22.5 us
    all_to_all x1, blocking collectives, body(): back = lax.all_to_all(both, CHIP, 0, 0)  21.9 us
    all_to_all x1, blocking collectives, body(): mine = lax.all_to_all(sent, 'feat', 0, 0)  13.2 us
    pallas_call x1, Pallas kernels, body(): call(project_kernel, [ANY] * 6, [shape((4, SPAN, 128)), shape((4, SPAN, 1...  9.94 us
    pallas_call x1, Pallas kernels, body(): call(self_kernel, [SMEM] + [VMEM] * 5, [shape((4, SPAN, 512), F32), shape...  5.37 us
    ppermute x1, starting transfers between devices, body(): taken = lax.ppermute(given, 'c', swap)  3.41 us
    ppermute x1, starting transfers between devices, body(): recv = lax.ppermute(send, 'c', swap)  3.29 us
    pallas_call x1, Pallas kernels, body(): call(final_kernel, [SMEM] + [VMEM] * 4, [far((1, 4, H, 64, HD), F32), far...  2.54 us
  transfers between devices with their start and end apart: 3, of which 0 were waited for; matrix products, arithmetic and copies ran while one was open for 0% of the time, Pallas kernels for 10%

profile of v2, /device:TPU:1, one launch (start us, length us, event | category | flops | bytes accessed | tf_op | source)
XLA Modules:
  0.0 91.5 jit_solution(740213739685092643)
XLA Ops:
  0.6 0.0 copy-start.3
  0.6 0.0 copy-start.2
  0.7 9.9 %shard_map.128 = (bf16[4,256,128]{2,1,0:T(8,128)(2,1)S(1)}, bf16[4,256,128]{2,1,0:T(8,128)(2,1)S(1)}, bf16[4,256,512]{2,1,0:T(8,128)(2,1)S(1)}, bf16[2,640,128]{...) custom-call(s32[4]{0:T(128)} %lens.5, bf16[4,256,2048]{2,1,0:T(8,128)(2,1)} %hid.1, ...), custom_call_target="tpu_custom_call" | custom-call | flops 3000000000 | bytes 1048576 | tf_op jit(solution)/shard_map/pallas_call | solution.py:385
  10.6 3.3 %collective-permute-start = (bf16[2,640,128]{2,1,0:T(8,128)(2,1)S(1)}, bf16[2,640,128]{2,1,0:T(8,128)(2,1)S(1)}, u32[]{:S(2)}, u32[]{:S(2)}) collective-permute-start(bf16[2,640,128]{2,1,0:T(8,128)(2,1)S(1)} %get-tuple-element.25), channel_id=1, source_target_pairs={{0,4},{4,0},{1,5},{5,1},{2,6},{6,2},{3,7},{7,3},{8,12},{12,8},{9,1... | collective-permute-start | bytes 983048 | tf_op jit(solution)/shard_map/ppermute | solution.py:409
  13.9 0.0 copy-done.3
  13.9 0.0 copy-done.2
  13.9 5.4 %shard_map.129 = (f32[4,256,512]{2,1,0:T(8,128)S(1)}, f32[4,256,128]{2,1,0:T(8,128)S(1)}, bf16[4,4,256,160]{3,2,1,0:T(8,128)(2,1)S(1)}) custom-call(s32[4]{0:T(128)S(1)} %copy-done.2, bf16[4,256,128]{2,1,0:T(8,128)(2,1)S(1)} %get-tuple-element.26.q, bf16[4,256,128]{2,1,0:T(8,128)(2,1)S(1)} %get-tuple-element.27.k, ...), custom_call_target="tpu_custom_call" | custom-call | flops 3000000000 | bytes 1048576 | tf_op jit(solution)/shard_map/pallas_call | solution.py:410
  19.3 0.0 copy-start.1
  19.3 0.0 collective-permute-done.recv
  19.3 0.1 shard_map.130
  19.4 22.5 %all_to_all.15.pieces = bf16[32,40,128]{2,1,0:T(8,128)(2,1)S(1)} all-to-all(bf16[32,40,128]{2,1,0:T(8,128)(2,1)S(1)} %shard_map.130), channel_id=1, replica_groups=mesh['z'=8,'y'=4,'c'=2,'feat'=4] {'z','y'}, dimensions={0} | all-to-all | bytes 655360 | tf_op jit(solution)/shard_map/all_to_all | solution.py:417
  41.9 0.0 copy-done.1
  41.9 0.6 shard_map.131
  42.5 21.9 %all_to_all.16.back = bf16[32,80,128]{2,1,0:T(8,128)(2,1)S(1)} all-to-all(bf16[32,80,128]{2,1,0:T(8,128)(2,1)S(1)} %shard_map.131), channel_id=1, replica_groups=mesh['z'=8,'y'=4,'c'=2,'feat'=4] {'z','y'}, dimensions={0} | all-to-all | bytes 1310720 | tf_op jit(solution)/shard_map/all_to_all | solution.py:419
  64.5 0.2 shard_map.132
  64.7 3.4 %collective-permute-start.1 = (bf16[1536,128]{1,0:T(8,128)(2,1)S(1)}, bf16[1536,128]{1,0:T(8,128)(2,1)S(1)}, u32[]{:S(2)}, u32[]{:S(2)}) collective-permute-start(bf16[1536,128]{1,0:T(8,128)(2,1)S(1)} %get-tuple-element.35.low_mine), channel_id=1, source_target_pairs={{0,4},{4,0},{1,5},{5,1},{2,6},{6,2},{3,7},{7,3},{8,12},{12,8},{9,1... | collective-permute-start | bytes 1179656 | tf_op jit(solution)/shard_map/ppermute | solution.py:423
  68.1 0.0 copy-start
  68.1 1.9 %shard_map.133 = (f32[2,256,512]{2,1,0:T(8,128)S(1)}, f32[8,128]{1,0:T(8,128)S(1)}) custom-call(s32[4]{0:T(128)S(1)} %copy-done.2, bf16[2,640,128]{2,1,0:T(8,128)(2,1)S(1)} %get-tuple-element.31.state, f32[4,256,512]{2,1,0:T(8,128)S(1)} %get-tuple-element.32.num, f32[4,256,128]{2,1,0:T(8,128)S(1)} %get-tuple-element.30.after.den, ...), custom_call_target="tpu_custom_call" | custom-call | flops 500000000 | bytes 1048576 | tf_op jit(solution)/shard_map/pallas_call | solution.py:425
  69.9 0.0 collective-permute-done.1.state.low_theirs
  69.9 0.0 copy-done
  70.0 2.1 %shard_map.134 = (f32[2,256,512]{2,1,0:T(8,128)S(1)}, bf16[4,536,128]{2,1,0:T(8,128)(2,1)S(1)}) custom-call(s32[4]{0:T(128)S(1)} %copy-done.2, bf16[1536,128]{1,0:T(8,128)(2,1)S(1)} %collective-permute-done.1.state.low_theirs, f32[4,256,512]{2,1,0:T(8,128)S(1)} %get-tuple-element.32.num, f32[4,256,128]{2,1,0:T(8,128)S(1)} %get-tuple-element.30.after.den, ...), custom_call_target="tpu_custom_call" | custom-call | flops 500000000 | bytes 1048576 | tf_op jit(solution)/shard_map/pallas_call | solution.py:431
  72.0 13.2 %all_to_all.17.sent.mine = bf16[4,536,128]{2,1,0:T(8,128)(2,1)S(1)} all-to-all(bf16[4,536,128]{2,1,0:T(8,128)(2,1)S(1)} %get-tuple-element.38), channel_id=1, replica_groups=mesh['z'=8,'y'=4,'c'=2,'feat'=4] {'feat'}, dimensions={0} | all-to-all | bytes 1097728 | tf_op jit(solution)/shard_map/all_to_all | solution.py:437
  85.3 1.3 %collective-permute-start.2 = (bf16[4,536,128]{2,1,0:T(8,128)(2,1)S(1)}, bf16[4,536,128]{2,1,0:T(8,128)(2,1)S(1)}, u32[]{:S(2)}, u32[]{:S(2)}) collective-permute-start(bf16[4,536,128]{2,1,0:T(8,128)(2,1)S(1)} %all_to_all.17.sent.mine), channel_id=1, source_target_pairs={{0,4},{4,0},{1,5},{5,1},{2,6},{6,2},{3,7},{7,3},{8,12},{12,8},{9,1... | collective-permute-start | bytes 1646600 | tf_op jit(solution)/shard_map/ppermute | solution.py:438
  86.6 2.4 %shard_map.135 = bf16[4,256,512]{2,1,0:T(8,128)(2,1)} custom-call(f32[2,256,512]{2,1,0:T(8,128)S(1)} %get-tuple-element.34.own, f32[2,256,512]{2,1,0:T(8,128)S(1)} %get-tuple-element.37.other, bf16[4,536,128]{2,1,0:T(8,128)(2,1)S(1)} %all_to_all.17.sent.mine), custom_call_target="tpu_custom_call" | custom-call | flops 500000000 | bytes 1048576 | tf_op jit(solution)/shard_map/pallas_call | solution.py:439
  88.9 0.0 collective-permute-done.2.theirs
  88.9 2.5 %shard_map.136 = (f32[1,4,16,64,128]{4,3,2,1,0:T(8,128)}, f32[1,4,17,4,128]{4,3,2,1,0:T(4,128)}, f32[1,4,16,64]{3,2,1,0:T(8,128)}, f32[1,4,4,17]{3,2,1,0:T(4,128)}) custom-call(s32[4]{0:T(128)S(1)} %copy-done.1, bf16[4,536,128]{2,1,0:T(8,128)(2,1)S(1)} %all_to_all.17.sent.mine, bf16[4,536,128]{2,1,0:T(8,128)(2,1)S(1)} %collective-permute-done.2.theirs, ...), custom_call_target="tpu_custom_call" | custom-call | bytes 1048576 | tf_op jit(solution)/shard_map/pallas_call | solution.py:448
Async XLA Ops:
  0.6 13.3 %copy-start.3 = (f32[8,160]{1,0:T(8,128)S(1)}, f32[8,160]{1,0:T(8,128)}, u32[]{:S(2)}) copy-start(f32[8,160]{1,0:T(8,128)} %constant.7.clone.lines) | copy-start | bytes 15364
  0.6 13.3 %copy-start.2 = (s32[4]{0:T(128)S(1)}, s32[4]{0:T(128)}, u32[]{:S(2)}) copy-start(s32[4]{0:T(128)} %lens.5) | copy-start | bytes 52
  10.6 8.7 %collective-permute-start = (bf16[2,640,128]{2,1,0:T(8,128)(2,1)S(1)}, bf16[2,640,128]{2,1,0:T(8,128)(2,1)S(1)}, u32[]{:S(2)}, u32[]{:S(2)}) collective-permute-start(bf16[2,640,128]{2,1,0:T(8,128)(2,1)S(1)} %get-tuple-element.25), channel_id=1, source_target_pairs={{0,4},{4,0},{1,5},{5,1},{2,6},{6,2},{3,7},{7,3},{8,12},{12,8},{9,1... | collective-permute-start | bytes 983048 | tf_op jit(solution)/shard_map/ppermute | solution.py:409
  19.3 22.6 %copy-start.1 = (s32[4]{0:T(128)S(1)}, s32[4]{0:T(128)}, u32[]{:S(2)}) copy-start(s32[4]{0:T(128)} %owners.3) | copy-start | bytes 52
  64.7 5.3 %collective-permute-start.1 = (bf16[1536,128]{1,0:T(8,128)(2,1)S(1)}, bf16[1536,128]{1,0:T(8,128)(2,1)S(1)}, u32[]{:S(2)}, u32[]{:S(2)}) collective-permute-start(bf16[1536,128]{1,0:T(8,128)(2,1)S(1)} %get-tuple-element.35.low_mine), channel_id=1, source_target_pairs={{0,4},{4,0},{1,5},{5,1},{2,6},{6,2},{3,7},{7,3},{8,12},{12,8},{9,1... | collective-permute-start | bytes 1179656 | tf_op jit(solution)/shard_map/ppermute | solution.py:423
  68.1 1.9 %copy-start = (bf16[256,160]{1,0:T(8,128)(2,1)S(1)}, bf16[256,160]{1,0:T(8,128)(2,1)}, u32[]{:S(2)}) copy-start(bf16[256,160]{1,0:T(8,128)(2,1)} %constant.8.clone.table) | copy-start | bytes 245764
  85.3 3.7 %collective-permute-start.2 = (bf16[4,536,128]{2,1,0:T(8,128)(2,1)S(1)}, bf16[4,536,128]{2,1,0:T(8,128)(2,1)S(1)}, u32[]{:S(2)}, u32[]{:S(2)}) collective-permute-start(bf16[4,536,128]{2,1,0:T(8,128)(2,1)S(1)} %all_to_all.17.sent.mine), channel_id=1, source_target_pairs={{0,4},{4,0},{1,5},{5,1},{2,6},{6,2},{3,7},{7,3},{8,12},{12,8},{9,1... | collective-permute-start | bytes 1646600 | tf_op jit(solution)/shard_map/ppermute | solution.py:438

commit v3 on v2

--- a/solution.py
+++ b/solution.py
@@ -77,6 +77,7 @@
 
 
 CHUNK = 512
+AHEAD = 5
 
 
 def project_kernel(
@@ -85,10 +86,10 @@
     core, _, seq, feat = place()
     lanes = pl.ds(pl.multiple_of(feat // 2 * 128, 128), 128)
     first = (2 + 2 * core) % 4
-    early = []
+    queue = []
     for n in range(D // CHUNK):
         rows = pl.ds(n * CHUNK, CHUNK)
-        early.append(
+        queue.append(
             [
                 pltpu.make_async_copy(hid.at[first, :, rows], hid_b.at[2, :, rows], sems.at[n, 0]),
                 pltpu.make_async_copy(wq.at[rows, lanes], wqk_b.at[rows, :128], sems.at[n, 1]),
@@ -96,48 +97,56 @@
                 pltpu.make_async_copy(wv.at[rows], wv_b.at[rows], sems.at[n, 3]),
             ]
         )
-        for copy in early[-1]:
-            copy.start()
-    tiny = [
-        pltpu.make_async_copy(lens_h, lens, small.at[0]),
-        pltpu.make_async_copy(picks_h.at[feat % 2], picks, small.at[1]),
-    ]
-    for copy in tiny:
-        copy.start()
-    late = []
+    queue.append(
+        [
+            pltpu.make_async_copy(lens_h, lens, small.at[0]),
+            pltpu.make_async_copy(picks_h.at[feat % 2], picks, small.at[1]),
+        ]
+    )
     for n, local in enumerate((3, 0, 1)):
-        late.append(pltpu.make_async_copy(hid.at[(local + 2 * core) % 4], hid_b.at[local], rest.at[n]))
-        late[-1].start()
+        queue.append([pltpu.make_async_copy(hid.at[(local + 2 * core) % 4], hid_b.at[local], rest.at[n])])
+
+    def start(n):
+        if n < len(queue):
+            for copy in queue[n]:
+                copy.start()
+
+    def arrive(n):
+        for copy in queue[n]:
+            copy.wait()
+        start(n + AHEAD)
+
+    for n in range(AHEAD):
+        start(n)
     row = lax.broadcasted_iota(jnp.int32, (ROWS, SPAN), 0)
     low = is_low(row)
     const = (row == LOW).astype(F32)
     fixed = jnp.where(row == LOW, 1.0, jnp.where(low, FD**-0.25, (2.0 * FD) ** -0.5))
     ones = jnp.ones((8, SPAN), BF)
     tail_row = lax.broadcasted_iota(jnp.int32, (8, HD), 0) + (ROWS - 8)
-    for n, local in enumerate((2, 3, 0, 1)):
+
+    def project(n, local):
         if n == 0:
             v = jnp.zeros((SPAN, 512), F32)
             qk = jnp.zeros((SPAN, 256), F32)
             for m in range(D // CHUNK):
-                for copy in early[m]:
-                    copy.wait()
+                arrive(m)
                 rows = slice(m * CHUNK, (m + 1) * CHUNK)
                 x = hid_b[local, :, rows]
                 qk = qk + jnp.dot(x, wqk_b[rows], preferred_element_type=F32)
                 v = v + jnp.dot(x, wv_b[rows], preferred_element_type=F32)
-            for copy in tiny:
-                copy.wait()
+            arrive(D // CHUNK)
         else:
-            late[n - 1].wait()
+            arrive(D // CHUNK + n)
             x = hid_b[local]
             qk = jnp.dot(x, wqk_b[...], preferred_element_type=F32)
             v = jnp.dot(x, wv_b[...], preferred_element_type=F32)
-        v = v.astype(BF)
-        key = qk[:, 128:].astype(BF)
         q_o[local] = qk[:, :128].astype(BF)
-        v_o[local] = v
-        k_o[local] = key
-        key_t = key.astype(F32).T.astype(BF)
+        k_o[local] = qk[:, 128:].astype(BF)
+        v_o[local] = v.astype(BF)
+
+    def states(local):
+        key_t = k_o[local].astype(F32).T.astype(BF)
         token = seq * SPAN + lax.broadcasted_iota(jnp.int32, (1, SPAN), 1)
         scale = jnp.where(token < lens[(local + 2 * core) % 4], fixed, 0.0)
         bias = jnp.where(low, scale, 0.0)
@@ -147,16 +156,24 @@
             u = jnp.dot(picks[0, at : at + ROWS], key_t, preferred_element_type=F32)
             w = jnp.dot(picks[1, at : at + ROWS], key_t, preferred_element_type=F32)
             feats = ((u + const) * (w * scale + bias)).astype(BF)
-            state = jnp.dot(feats, v[:, h * HD : (h + 1) * HD], preferred_element_type=F32)
+            state = jnp.dot(feats, v_o[local, :, h * HD : (h + 1) * HD], preferred_element_type=F32)
             norm = nt(ones, feats)
             rest_norm = jnp.concatenate([norm[:, HD:], jnp.zeros((8, 2 * HD - ROWS), F32)], axis=1)
             tail = state[ROWS - 8 :]
             tail = jnp.where(tail_row == NORM, norm[:, :HD], jnp.where(tail_row == NORM + 1, rest_norm, tail))
             target[local % 2, at : at + ROWS] = jnp.concatenate([state[: ROWS - 8], tail], axis=0).astype(BF)
 
-
-def self_kernel(lens, q, k, v, picks, lines, num_o, den_o, feat_o):
+    order = (2, 3, 0, 1)
+    for n in range(5):
+        if n < 4:
+            project(n, order[n])
+        if n > 0:
+            states(order[n - 1])
+
+
+def self_kernel(lens, q, k, v, picks, lines, num_o, den_o, feat_o, late=False):
     core, _, seq, feat = place()
+    split = jnp.maximum(4 - lax.axis_index("z"), 0)
     tq = lax.broadcasted_iota(jnp.int32, (SPAN, SPAN), 0)
     tk = lax.broadcasted_iota(jnp.int32, (SPAN, SPAN), 1)
     lane = lax.broadcasted_iota(jnp.int32, (SPAN, HD), 1)
@@ -183,7 +200,11 @@
         den_o[local] = den_all
         return _
 
-    lax.fori_loop(0, 4, prompt, 0)
+    lax.fori_loop(split if late else 0, 4 if late else split, prompt, 0)
+
+
+def late_kernel(lens, q, k, v, picks, lines, num, den, feat, after, num_o, den_o, feat_o):
+    self_kernel(lens, q, k, v, picks, lines, num_o, den_o, feat_o, late=True)
 
 
 def pair_kernel(keep, recv, after, out):
@@ -348,7 +369,7 @@
     return [pltpu.with_memory_space_constraint(a, pltpu.VMEM) for a in arrays]
 
 
-def call(kernel, in_specs, out_shape, out_specs=None, grid=(), scratch=(), flops=0, limit=16):
+def call(kernel, in_specs, out_shape, out_specs=None, grid=(), scratch=(), flops=0, limit=16, aliases=None):
     if out_specs is None:
         out_specs = jax.tree.map(lambda _: VMEM, out_shape, is_leaf=lambda x: not isinstance(x, (list, tuple)))
     return pl.pallas_call(
@@ -358,6 +379,7 @@
         out_specs=out_specs,
         out_shape=out_shape,
         scratch_shapes=scratch,
+        input_output_aliases=aliases or {},
         cost_estimate=pl.CostEstimate(flops=flops, transcendentals=0, bytes_accessed=MIB),
         compiler_params=pltpu.CompilerParams(
             dimension_semantics=("arbitrary",) * len(grid), vmem_limit_bytes=limit * MIB
@@ -407,12 +429,11 @@
     )(*held(lengths, hidden_in, w_value, w_query, w_key, jnp.asarray(PICKS, BF)))
 
     recv = lax.ppermute(send, "c", swap)
-    num, den, feats = call(
-        self_kernel,
-        [SMEM] + [VMEM] * 5,
-        [shape((4, SPAN, 512), F32), shape((4, SPAN, 128), F32), shape((4, OWN, SPAN, ROWS))],
-        flops=3_000_000_000,
-    )(lengths, *near(q, k, v, picks, jnp.asarray(LINES)))
+    lines = jnp.asarray(LINES)
+    own_shapes = [shape((4, SPAN, 512), F32), shape((4, SPAN, 128), F32), shape((4, OWN, SPAN, ROWS))]
+    num, den, feats = call(self_kernel, [SMEM] + [VMEM] * 5, own_shapes, flops=3_000_000_000)(
+        lengths, *near(q, k, v, picks, lines)
+    )
     pair = call(pair_kernel, [VMEM, VMEM, ANY], shape((CHIPS, SLICE, HD)))(*near(keep, recv, den))
     pieces = lax.all_to_all(pair, CHIP, 0, 0)
     both = call(scan_kernel, [SMEM, VMEM], shape((CHIPS, 2 * SLICE, HD)))(owners, *near(pieces))
@@ -421,6 +442,13 @@
         prefix_kernel, [VMEM] * 3, [shape(half), shape((STATE + 2 * OWN * LOW_ROWS, HD))]
     )(*near(back, keep, recv))
     taken = lax.ppermute(given, "c", swap)
+    num, den, feats = call(
+        late_kernel,
+        [SMEM] + [VMEM] * 8 + [ANY],
+        own_shapes,
+        flops=3_000_000_000,
+        aliases={6: 0, 7: 1, 8: 2},
+    )(lengths, *near(q, k, v, picks, lines, num, den, feats, own_state))
 
     own_att, square = call(
         own_kernel,

time: 91.7 us -> 88 us (0.960)
  blocking collectives: 57.7 us -> 53.5 us
    all_to_all x1, blocking collectives: 22.5 us -> 17.9 us  [body(): pieces = lax.all_to_all(pair, CHIP, 0, 0)]
    pallas_call x1 -> x2, Pallas kernels: 5.37 us -> 6.12 us  [the longest x1 5.38 us: body(): call(self_kernel, [SMEM] + [VMEM] * 5, own_shapes, flops=3000000000)]
  transfers between devices with their start and end apart: 3 -> 3, of which waited for: 0 -> 0; matrix products, arithmetic and copies ran while one was open for 0% -> 0% of each run, Pallas kernels for 10% -> 12%
where the time goes in v3:
time: 88 us; the launch traced here: 87.2 us
  blocking collectives  53.5 us (61%)
  Pallas kernels  24.9 us (28%)
  starting transfers between devices  8.01 us (9%)
    all_to_all x1, blocking collectives, body(): back = lax.all_to_all(both, CHIP, 0, 0)  22.4 us
    all_to_all x1, blocking collectives, body(): pieces = lax.all_to_all(pair, CHIP, 0, 0)  17.9 us
    all_to_all x1, blocking collectives, body(): mine = lax.all_to_all(sent, 'feat', 0, 0)  13.2 us
    pallas_call x1, Pallas kernels, body(): call(project_kernel, [ANY] * 6, [shape((4, SPAN, 128)), shape((4, SPAN, 1...  9.06 us
    pallas_call x1, Pallas kernels, body(): call(self_kernel, [SMEM] + [VMEM] * 5, own_shapes, flops=3000000000)  5.38 us
    ppermute x1, starting transfers between devices, body(): taken = lax.ppermute(given, 'c', swap)  3.41 us
    ppermute x1, starting transfers between devices, body(): recv = lax.ppermute(send, 'c', swap)  3.29 us
    pallas_call x1, Pallas kernels, body(): call(final_kernel, [SMEM] + [VMEM] * 4, [far((1, 4, H, 64, HD), F32), far...  2.54 us
  transfers between devices with their start and end apart: 3, of which 0 were waited for; matrix products, arithmetic and copies ran while one was open for 0% of the time, Pallas kernels for 12%

profile of v3, /device:TPU:1, one launch (start us, length us, event | category | flops | bytes accessed | tf_op | source)
XLA Modules:
  0.0 87.2 jit_solution(2777398417592816131)
XLA Ops:
  0.6 0.0 copy-start.3
  0.6 0.0 copy-start.2
  0.7 9.1 %shard_map.128 = (bf16[4,256,128]{2,1,0:T(8,128)(2,1)S(1)}, bf16[4,256,128]{2,1,0:T(8,128)(2,1)S(1)}, bf16[4,256,512]{2,1,0:T(8,128)(2,1)S(1)}, bf16[2,640,128]{...) custom-call(s32[4]{0:T(128)} %lens.7, bf16[4,256,2048]{2,1,0:T(8,128)(2,1)} %hid.1, ...), custom_call_target="tpu_custom_call" | custom-call | flops 3000000000 | bytes 1048576 | tf_op jit(solution)/shard_map/pallas_call | solution.py:407
  9.7 3.3 %collective-permute-start = (bf16[2,640,128]{2,1,0:T(8,128)(2,1)S(1)}, bf16[2,640,128]{2,1,0:T(8,128)(2,1)S(1)}, u32[]{:S(2)}, u32[]{:S(2)}) collective-permute-start(bf16[2,640,128]{2,1,0:T(8,128)(2,1)S(1)} %get-tuple-element.28), channel_id=1, source_target_pairs={{0,4},{4,0},{1,5},{5,1},{2,6},{6,2},{3,7},{7,3},{8,12},{12,8},{9,1... | collective-permute-start | bytes 983048 | tf_op jit(solution)/shard_map/ppermute | solution.py:431
  13.0 0.0 copy-done.3
  13.0 0.0 copy-done.2
  13.0 5.4 %shard_map.129 = (f32[4,256,512]{2,1,0:T(8,128)S(1)}, f32[4,256,128]{2,1,0:T(8,128)S(1)}, bf16[4,4,256,160]{3,2,1,0:T(8,128)(2,1)S(1)}) custom-call(s32[4]{0:T(128)S(1)} %copy-done.2, bf16[4,256,128]{2,1,0:T(8,128)(2,1)S(1)} %get-tuple-element.29.q, bf16[4,256,128]{2,1,0:T(8,128)(2,1)S(1)} %get-tuple-element.30.k, ...), custom_call_target="tpu_custom_call" | custom-call | flops 3000000000 | bytes 1048576 | tf_op jit(solution)/shard_map/pallas_call | solution.py:434
  18.4 0.0 copy-start.1
  18.4 0.0 collective-permute-done.recv
  18.4 0.1 shard_map.130
  18.5 17.9 %all_to_all.15.pieces = bf16[32,40,128]{2,1,0:T(8,128)(2,1)S(1)} all-to-all(bf16[32,40,128]{2,1,0:T(8,128)(2,1)S(1)} %shard_map.130), channel_id=1, replica_groups=mesh['z'=8,'y'=4,'c'=2,'feat'=4] {'z','y'}, dimensions={0} | all-to-all | bytes 655360 | tf_op jit(solution)/shard_map/all_to_all | solution.py:438
  36.4 0.0 copy-done.1
  36.4 0.6 shard_map.131
  37.1 22.4 %all_to_all.16.back = bf16[32,80,128]{2,1,0:T(8,128)(2,1)S(1)} all-to-all(bf16[32,80,128]{2,1,0:T(8,128)(2,1)S(1)} %shard_map.131), channel_id=1, replica_groups=mesh['z'=8,'y'=4,'c'=2,'feat'=4] {'z','y'}, dimensions={0} | all-to-all | bytes 1310720 | tf_op jit(solution)/shard_map/all_to_all | solution.py:440
  59.4 0.2 shard_map.132
  59.6 3.4 %collective-permute-start.1 = (bf16[1536,128]{1,0:T(8,128)(2,1)S(1)}, bf16[1536,128]{1,0:T(8,128)(2,1)S(1)}, u32[]{:S(2)}, u32[]{:S(2)}) collective-permute-start(bf16[1536,128]{1,0:T(8,128)(2,1)S(1)} %get-tuple-element.41.low_mine), channel_id=1, source_target_pairs={{0,4},{4,0},{1,5},{5,1},{2,6},{6,2},{3,7},{7,3},{8,12},{12,8},{9,1... | collective-permute-start | bytes 1179656 | tf_op jit(solution)/shard_map/ppermute | solution.py:444
  63.1 0.7 shard_map.133
  63.8 0.0 copy-start
  63.8 1.9 %shard_map.134 = (f32[2,256,512]{2,1,0:T(8,128)S(1)}, f32[8,128]{1,0:T(8,128)S(1)}) custom-call(s32[4]{0:T(128)S(1)} %copy-done.2, bf16[2,640,128]{2,1,0:T(8,128)(2,1)S(1)} %get-tuple-element.34.after.state, f32[4,256,512]{2,1,0:T(8,128)S(1)} %get-tuple-element.37.num, f32[4,256,128]{2,1,0:T(8,128)S(1)} %get-tuple-element.38.den, ...), custom_call_target="tpu_custom_call" | custom-call | flops 500000000 | bytes 1048576 | tf_op jit(solution)/shard_map/pallas_call | solution.py:453
  65.7 0.0 collective-permute-done.1.state.low_theirs
  65.7 0.0 copy-done
  65.7 2.1 %shard_map.135 = (f32[2,256,512]{2,1,0:T(8,128)S(1)}, bf16[4,536,128]{2,1,0:T(8,128)(2,1)S(1)}) custom-call(s32[4]{0:T(128)S(1)} %copy-done.2, bf16[1536,128]{1,0:T(8,128)(2,1)S(1)} %collective-permute-done.1.state.low_theirs, f32[4,256,512]{2,1,0:T(8,128)S(1)} %get-tuple-element.37.num, f32[4,256,128]{2,1,0:T(8,128)S(1)} %get-tuple-element.38.den, ...), custom_call_target="tpu_custom_call" | custom-call | flops 500000000 | bytes 1048576 | tf_op jit(solution)/shard_map/pallas_call | solution.py:459
  67.8 13.2 %all_to_all.17.sent.mine = bf16[4,536,128]{2,1,0:T(8,128)(2,1)S(1)} all-to-all(bf16[4,536,128]{2,1,0:T(8,128)(2,1)S(1)} %get-tuple-element.44), channel_id=1, replica_groups=mesh['z'=8,'y'=4,'c'=2,'feat'=4] {'feat'}, dimensions={0} | all-to-all | bytes 1097728 | tf_op jit(solution)/shard_map/all_to_all | solution.py:465
  81.0 1.3 %collective-permute-start.2 = (bf16[4,536,128]{2,1,0:T(8,128)(2,1)S(1)}, bf16[4,536,128]{2,1,0:T(8,128)(2,1)S(1)}, u32[]{:S(2)}, u32[]{:S(2)}) collective-permute-start(bf16[4,536,128]{2,1,0:T(8,128)(2,1)S(1)} %all_to_all.17.sent.mine), channel_id=1, source_target_pairs={{0,4},{4,0},{1,5},{5,1},{2,6},{6,2},{3,7},{7,3},{8,12},{12,8},{9,1... | collective-permute-start | bytes 1646600 | tf_op jit(solution)/shard_map/ppermute | solution.py:466
  82.3 2.4 %shard_map.136 = bf16[4,256,512]{2,1,0:T(8,128)(2,1)} custom-call(f32[2,256,512]{2,1,0:T(8,128)S(1)} %get-tuple-element.40.own, f32[2,256,512]{2,1,0:T(8,128)S(1)} %get-tuple-element.43.other, bf16[4,536,128]{2,1,0:T(8,128)(2,1)S(1)} %all_to_all.17.sent.mine), custom_call_target="tpu_custom_call" | custom-call | flops 500000000 | bytes 1048576 | tf_op jit(solution)/shard_map/pallas_call | solution.py:467
  84.7 0.0 collective-permute-done.2.theirs
  84.7 2.5 %shard_map.137 = (f32[1,4,16,64,128]{4,3,2,1,0:T(8,128)}, f32[1,4,17,4,128]{4,3,2,1,0:T(4,128)}, f32[1,4,16,64]{3,2,1,0:T(8,128)}, f32[1,4,4,17]{3,2,1,0:T(4,128)}) custom-call(s32[4]{0:T(128)S(1)} %copy-done.1, bf16[4,536,128]{2,1,0:T(8,128)(2,1)S(1)} %all_to_all.17.sent.mine, bf16[4,536,128]{2,1,0:T(8,128)(2,1)S(1)} %collective-permute-done.2.theirs, ...), custom_call_target="tpu_custom_call" | custom-call | bytes 1048576 | tf_op jit(solution)/shard_map/pallas_call | solution.py:476
Async XLA Ops:
  0.6 12.4 %copy-start.3 = (f32[8,160]{1,0:T(8,128)S(1)}, f32[8,160]{1,0:T(8,128)}, u32[]{:S(2)}) copy-start(f32[8,160]{1,0:T(8,128)} %constant.7.clone.lines) | copy-start | bytes 15364
  0.6 12.4 %copy-start.2 = (s32[4]{0:T(128)S(1)}, s32[4]{0:T(128)}, u32[]{:S(2)}) copy-start(s32[4]{0:T(128)} %lens.7) | copy-start | bytes 52
  9.7 8.7 %collective-permute-start = (bf16[2,640,128]{2,1,0:T(8,128)(2,1)S(1)}, bf16[2,640,128]{2,1,0:T(8,128)(2,1)S(1)}, u32[]{:S(2)}, u32[]{:S(2)}) collective-permute-start(bf16[2,640,128]{2,1,0:T(8,128)(2,1)S(1)} %get-tuple-element.28), channel_id=1, source_target_pairs={{0,4},{4,0},{1,5},{5,1},{2,6},{6,2},{3,7},{7,3},{8,12},{12,8},{9,1... | collective-permute-start | bytes 983048 | tf_op jit(solution)/shard_map/ppermute | solution.py:431
  18.4 18.0 %copy-start.1 = (s32[4]{0:T(128)S(1)}, s32[4]{0:T(128)}, u32[]{:S(2)}) copy-start(s32[4]{0:T(128)} %owners.3) | copy-start | bytes 52
  59.6 6.0 %collective-permute-start.1 = (bf16[1536,128]{1,0:T(8,128)(2,1)S(1)}, bf16[1536,128]{1,0:T(8,128)(2,1)S(1)}, u32[]{:S(2)}, u32[]{:S(2)}) collective-permute-start(bf16[1536,128]{1,0:T(8,128)(2,1)S(1)} %get-tuple-element.41.low_mine), channel_id=1, source_target_pairs={{0,4},{4,0},{1,5},{5,1},{2,6},{6,2},{3,7},{7,3},{8,12},{12,8},{9,1... | collective-permute-start | bytes 1179656 | tf_op jit(solution)/shard_map/ppermute | solution.py:444
  63.8 1.9 %copy-start = (bf16[256,160]{1,0:T(8,128)(2,1)S(1)}, bf16[256,160]{1,0:T(8,128)(2,1)}, u32[]{:S(2)}) copy-start(bf16[256,160]{1,0:T(8,128)(2,1)} %constant.8.clone.table) | copy-start | bytes 245764
  81.0 3.7 %collective-permute-start.2 = (bf16[4,536,128]{2,1,0:T(8,128)(2,1)S(1)}, bf16[4,536,128]{2,1,0:T(8,128)(2,1)S(1)}, u32[]{:S(2)}, u32[]{:S(2)}) collective-permute-start(bf16[4,536,128]{2,1,0:T(8,128)(2,1)S(1)} %all_to_all.17.sent.mine), channel_id=1, source_target_pairs={{0,4},{4,0},{1,5},{5,1},{2,6},{6,2},{3,7},{7,3},{8,12},{12,8},{9,1... | collective-permute-start | bytes 1646600 | tf_op jit(solution)/shard_map/ppermute | solution.py:466

commit v4 on v3

--- a/solution.py
+++ b/solution.py
@@ -173,7 +173,9 @@
 
 def self_kernel(lens, q, k, v, picks, lines, num_o, den_o, feat_o, late=False):
     core, _, seq, feat = place()
-    split = jnp.maximum(4 - lax.axis_index("z"), 0)
+    z = lax.axis_index("z")
+    early = jnp.where(z < 4, 5 - z, 0) + (lax.axis_index("y") == 0).astype(jnp.int32)
+    split = jnp.minimum(early, 4)
     tq = lax.broadcasted_iota(jnp.int32, (SPAN, SPAN), 0)
     tk = lax.broadcasted_iota(jnp.int32, (SPAN, SPAN), 1)
     lane = lax.broadcasted_iota(jnp.int32, (SPAN, HD), 1)
@@ -190,10 +192,10 @@
             mine = jnp.where(lane // FD == feat % 2 * OWN + h, query, jnp.zeros_like(query))
             score = nt(mine, key)
             weight = jnp.where(seen, 1.0 + score * (FD**-0.5) + score * score * (0.5 / FD), 0.0).astype(BF)
-            value = v[local, :, h * HD : (h + 1) * HD]
-            num_o[local, :, h * HD : (h + 1) * HD] = jnp.dot(weight, value, preferred_element_type=F32)
-            den = jnp.dot(weight, ones, preferred_element_type=F32)
-            den_all = jnp.where(lane == h, den, den_all)
+            value = jnp.concatenate([v[local, :, h * HD : (h + 1) * HD], ones], axis=1)
+            both = jnp.dot(weight, value, preferred_element_type=F32)
+            num_o[local, :, h * HD : (h + 1) * HD] = both[:, :HD]
+            den_all = jnp.where(lane == h, both[:, HD:], den_all)
             u = nt(query, picks[0, at : at + ROWS])
             w = nt(query, picks[1, at : at + ROWS])
             feat_o[local, h] = ((u + const) * (w * scale + bias)).astype(BF)
@@ -201,10 +203,6 @@
         return _
 
     lax.fori_loop(split if late else 0, 4 if late else split, prompt, 0)
-
-
-def late_kernel(lens, q, k, v, picks, lines, num, den, feat, after, num_o, den_o, feat_o):
-    self_kernel(lens, q, k, v, picks, lines, num_o, den_o, feat_o, late=True)
 
 
 def pair_kernel(keep, recv, after, out):
@@ -238,7 +236,7 @@
     added = jnp.where(second, recv[...], keep[...]).reshape(STATE, HD).astype(F32)
     both = (before + added).astype(BF)
     plain = before.astype(BF)
-    own_o[...] = jnp.where(second, both, plain).reshape(2, OWN * ROWS, HD)
+    own_o[...] = jnp.where(second, both, plain)
     other_o[:STATE] = jnp.where(second, plain, both)
     total = back[:, SLICE:].reshape(2 * OWN, ROWS, HD)
     other_o[STATE:] = total[:, LOW:].reshape(2 * OWN * LOW_ROWS, HD)
@@ -248,7 +246,8 @@
     return jnp.concatenate([part[NORM : NORM + 1], part[NORM + 1 : NORM + 2, : ROWS - HD]], axis=1)
 
 
-def spread(total, table, out):
+def spread_kernel(back, table, out):
+    total = back[:, SLICE:].reshape(2 * OWN, ROWS, HD)
     for n in range(2 * OWN):
         wide = jnp.dot(table[...], total[n], preferred_element_type=F32).astype(BF)
         for f in range(4):
@@ -287,76 +286,110 @@
     return found
 
 
-def own_kernel(lens, state, num, den, feat, att_o, square_o):
-    found = attend(0, lens, lambda n, h: state[n, h * ROWS : (h + 1) * ROWS], num, den, feat, att_o)
-    square_o[...] = jnp.concatenate(found + [jnp.zeros((4, HD), F32)], axis=0)
-
-
-def other_kernel(lens, state, num, den, feat, square, back, table, att_o, sent_o):
+def part_of(state):
     def part(n, h):
         at = (n * OWN + h) * ROWS
         return state[at : at + ROWS]
 
-    found = attend(2, lens, part, num, den, feat, att_o)
+    return part
+
+
+def own_kernel(
+    lens, state, q, k, v, picks, lines, num_i, den_i, feat_i, num, den, feat, att_o, square_o, quad_o, blank, sem
+):
+    blank[...] = jnp.zeros_like(blank)
+    clear = [pltpu.make_async_copy(blank, quad_o.at[0, n], sem.at[n]) for n in range(4)]
+    for copy in clear:
+        copy.start()
+    self_kernel(lens, q, k, v, picks, lines, num, den, feat, late=True)
+    found = attend(0, lens, part_of(state), num, den, feat, att_o)
+    square_o[...] = jnp.concatenate(found + [jnp.zeros((4, HD), F32)], axis=0)
+    for copy in clear:
+        copy.wait()
+
+
+def other_kernel(lens, state, num, den, feat, square, sent_i, att_o, sent_o):
+    found = attend(2, lens, part_of(state), num, den, feat, att_o)
     squares = jnp.concatenate([square[:4]] + found, axis=0)
     high = squares.astype(BF)
     rest = (squares - high.astype(F32)).astype(BF)
     for f in range(4):
         sent_o[f, NORMS : NORMS + 8] = high
         sent_o[f, NORMS + 8 :] = rest
-    spread(back[:, SLICE:].reshape(2 * OWN, ROWS, HD), table, sent_o)
-
-
-def mix_kernel(own, other, sent, mixed_o):
-    step = pl.program_id(0)
+
+
+def mix_kernel(own, other, sent, mixed_o, block, sem):
+    core = lax.axis_index("c")
     square = jnp.zeros((8, HD), F32)
     for f in range(4):
         square = square + (sent[f, NORMS : NORMS + 8].astype(F32) + sent[f, NORMS + 8 :].astype(F32))
     factor = lax.rsqrt(square * (1.0 / D) + NORM_FLOOR).T
-    lane = lax.broadcasted_iota(jnp.int32, (HD, 8), 1)
-    for k in range(2):
-        column = jnp.sum(jnp.where(lane == 2 * step + k, factor, 0.0), axis=1, keepdims=True)
-        rows = slice(k * HD, (k + 1) * HD)
-
-        @pl.when(step < 2)
+    copies = []
+    for local in range(4):
+        source = own if local < 2 else other
+        for k in range(2):
+            column = factor[:, 2 * local + k : 2 * local + k + 1]
+            rows = slice(k * HD, (k + 1) * HD)
+            block[local, rows] = (source[local % 2, rows] * column).astype(BF)
+        copies.append(pltpu.make_async_copy(block.at[local], mixed_o.at[(local + 2 * core) % 4], sem.at[local]))
+        copies[-1].start()
+    for copy in copies:
+        copy.wait()
+
+
+def final_kernel(
+    owners, mine, theirs, low_mine, low_theirs, cleared, quad_o, low_o, nquad_o, nlow_o, block, low_b, nquad_b, nlow_b, sem
+):
+    core, _, seq, _ = place()
+    low_b[...] = jnp.zeros_like(low_b)
+    nquad_b[...] = jnp.zeros_like(nquad_b)
+    nlow_b[...] = jnp.zeros_like(nlow_b)
+
+    def move(local, f):
+        heads = pl.ds(f * OWN, OWN)
+        prompt = (local + 2 * core) % 4
+        return pltpu.make_async_copy(block.at[local, heads], quad_o.at[0, prompt, heads], sem.at[local, f])
+
+    for local in range(4):
+        prompt = (local + 2 * core) % 4
+        wide, low = (mine, low_mine) if local < 2 else (theirs, low_theirs)
+        at = local % 2
+
+        @pl.when(owners[prompt] == seq)
         def _():
-            mixed_o[0, rows] = (own[step, rows] * column).astype(BF)
-
-        @pl.when(step >= 2)
+            for f in range(4):
+                for h in range(OWN):
+                    row = (at * OWN + h) * 64
+                    block[local, f * OWN + h] = wide[f, row : row + 64].astype(F32)
+                move(local, f).start()
+            for f in range(4):
+                for h in range(OWN):
+                    row = WIDE + at * OWN + h
+                    nquad_b[prompt, f * OWN + h : f * OWN + h + 1] = wide[f, row : row + 1].astype(F32)[:, :64]
+            for h in range(OWN):
+                row = STATE + (at * OWN + h) * LOW_ROWS
+                piece = low[row : row + LOW_ROWS].astype(F32)
+                for r in range(FD + 1):
+                    low_b[prompt, r, h : h + 1] = piece[r : r + 1]
+                at_norm = NORM + 1 - LOW
+                nlow_b[prompt, h : h + 1] = piece[at_norm : at_norm + 1, : FD + 1]
+
+    small = [
+        pltpu.make_async_copy(low_b, low_o.at[0], sem.at[4, 0]),
+        pltpu.make_async_copy(nquad_b, nquad_o.at[0], sem.at[4, 1]),
+        pltpu.make_async_copy(nlow_b, nlow_o.at[0], sem.at[4, 2]),
+    ]
+    for copy in small:
+        copy.start()
+    for local in range(4):
+
+        @pl.when(owners[(local + 2 * core) % 4] == seq)
         def _():
-            mixed_o[0, rows] = (other[step - 2, rows] * column).astype(BF)
-
-
-def final_kernel(owners, mine, theirs, low_mine, low_theirs, quad_o, low_o, nquad_o, nlow_o):
-    core, _, seq, _ = place()
-    prompt = pl.program_id(0)
-    local = (prompt + 2 * core) % 4
-    keep = owners[prompt] == seq
-
-    def write(wide, low, at):
-        for f in range(4):
-            for h in range(OWN):
-                piece = wide[f, (at * OWN + h) * 64 : (at * OWN + h + 1) * 64].astype(F32)
-                quad_o[0, 0, f * OWN + h] = jnp.where(keep, piece, 0.0)
-                norm = wide[f, WIDE + at * OWN + h : WIDE + 1 + at * OWN + h].astype(F32)
-                nquad_o[0, 0, f * OWN + h : f * OWN + h + 1] = jnp.where(keep, norm, 0.0)[:, :64]
-        for h in range(OWN):
-            piece = low[pl.ds(STATE + (at * OWN + h) * LOW_ROWS, LOW_ROWS)].astype(F32)
-            piece = jnp.where(keep, piece, 0.0)
-            for r in range(FD + 1):
-                low_o[0, 0, r, h : h + 1] = piece[r : r + 1]
-            at_norm = NORM + 1 - LOW
-            nlow_o[0, 0, h : h + 1] = piece[at_norm : at_norm + 1, : FD + 1]
-
-    for at in range(2):
-
-        @pl.when(local == at)
-        def _():
-            write(mine, low_mine, at)
-
-        @pl.when(local == 2 + at)
-        def _():
-            write(theirs, low_theirs, at)
+            for f in range(4):
+                move(local, f).wait()
+
+    for copy in small:
+        copy.wait()
 
 
 SMEM = pl.BlockSpec(memory_space=pltpu.SMEM)
@@ -439,57 +472,58 @@
     both = call(scan_kernel, [SMEM, VMEM], shape((CHIPS, 2 * SLICE, HD)))(owners, *near(pieces))
     back = lax.all_to_all(both, CHIP, 0, 0)
     own_state, given = call(
-        prefix_kernel, [VMEM] * 3, [shape(half), shape((STATE + 2 * OWN * LOW_ROWS, HD))]
+        prefix_kernel, [VMEM] * 3, [shape((STATE, HD)), shape((STATE + 2 * OWN * LOW_ROWS, HD))]
     )(*near(back, keep, recv))
     taken = lax.ppermute(given, "c", swap)
-    num, den, feats = call(
-        late_kernel,
-        [SMEM] + [VMEM] * 8 + [ANY],
-        own_shapes,
+    num, den, feats, own_att, square, quad = call(
+        own_kernel,
+        [SMEM] + [VMEM] * 9,
+        own_shapes + [shape((2, SPAN, 512), F32), shape((8, HD), F32), pltpu.HBM((1, 4, H, 64, HD), F32)],
+        [VMEM] * 5 + [ANY],
+        scratch=[pltpu.VMEM((H, 64, HD), F32), pltpu.SemaphoreType.DMA((4,))],
         flops=3_000_000_000,
-        aliases={6: 0, 7: 1, 8: 2},
-    )(lengths, *near(q, k, v, picks, lines, num, den, feats, own_state))
-
-    own_att, square = call(
-        own_kernel,
-        [SMEM] + [VMEM] * 4,
-        [shape((2, SPAN, 512), F32), shape((8, HD), F32)],
-        flops=500_000_000,
-    )(lengths, *near(own_state, num, den, feats))
+        aliases={7: 0, 8: 1, 9: 2},
+    )(lengths, *near(own_state, q, k, v, picks, lines, num, den, feats))
+    sent = call(spread_kernel, [VMEM] * 2, shape((4, SENT, HD)), flops=500_000_000)(
+        *near(back, jnp.asarray(SPREAD, BF))
+    )
     other_att, sent = call(
         other_kernel,
-        [SMEM] + [VMEM] * 7,
+        [SMEM] + [VMEM] * 6,
         [shape((2, SPAN, 512), F32), shape((4, SENT, HD))],
         flops=500_000_000,
-    )(lengths, *near(taken, num, den, feats, square, back, jnp.asarray(SPREAD, BF)))
+        aliases={6: 1},
+    )(lengths, *near(taken, num, den, feats, square, sent))
     mine = lax.all_to_all(sent, "feat", 0, 0)
     theirs = lax.ppermute(mine, "c", swap)
     mixed = call(
         mix_kernel,
         [VMEM] * 3,
-        far((4, SPAN, 512)),
-        pl.BlockSpec((1, SPAN, 512), lambda i: ((i + 2 * lax.axis_index("c")) % 4, 0, 0)),
-        (4,),
+        pltpu.HBM((4, SPAN, 512), BF),
+        ANY,
+        scratch=[pltpu.VMEM((4, SPAN, 512), BF), pltpu.SemaphoreType.DMA((4,))],
         flops=500_000_000,
     )(*near(own_att, other_att, mine))
 
     quad, low_out, norm_quad, norm_low = call(
         final_kernel,
-        [SMEM] + [VMEM] * 4,
+        [SMEM] + [VMEM] * 4 + [ANY],
         [
-            far((1, 4, H, 64, HD), F32),
-            far((1, 4, FD + 1, OWN, HD), F32),
-            far((1, 4, H, 64), F32),
-            far((1, 4, OWN, FD + 1), F32),
+            pltpu.HBM((1, 4, H, 64, HD), F32),
+            pltpu.HBM((1, 4, FD + 1, OWN, HD), F32),
+            pltpu.HBM((1, 4, H, 64), F32),
+            pltpu.HBM((1, 4, OWN, FD + 1), F32),
         ],
-        [
-            pl.BlockSpec((1, 1, H, 64, HD), lambda i: (0, i, 0, 0, 0)),
-            pl.BlockSpec((1, 1, FD + 1, OWN, HD), lambda i: (0, i, 0, 0, 0)),
-            pl.BlockSpec((1, 1, H, 64), lambda i: (0, i, 0, 0)),
-            pl.BlockSpec((1, 1, OWN, FD + 1), lambda i: (0, i, 0, 0)),
+        [ANY] * 4,
+        scratch=[
+            pltpu.VMEM((4, H, 64, HD), F32),
+            pltpu.VMEM((4, FD + 1, OWN, HD), F32),
+            pltpu.VMEM((4, H, 64), F32),
+            pltpu.VMEM((4, OWN, FD + 1), F32),
+            pltpu.SemaphoreType.DMA((5, 4)),
         ],
-        (4,),
-    )(owners, *near(mine, theirs, given, taken))
+        aliases={5: 0},
+    )(owners, *near(mine, theirs, given, taken), *held(quad))
     return mixed, quad, jnp.transpose(low_out, (0, 1, 3, 2, 4)), norm_quad, norm_low
 
 

time: 88 us -> 85.3 us (0.969)
  Pallas kernels: 24.9 us -> 20.9 us
  blocking collectives: 53.5 us -> 55.1 us
    pallas_call x6, Pallas kernels: 9.77 us -> 7.26 us  [the longest x1 2 us: body(): call(own_kernel, [SMEM] + [VMEM] * 9, own_shapes + [shape((2, SPAN, 512),...]
    all_to_all x1, blocking collectives: 17.9 us -> 19.5 us  [body(): pieces = lax.all_to_all(pair, CHIP, 0, 0)]
    pallas_call x1, Pallas kernels: 5.38 us -> 3.9 us  [body(): call(self_kernel, [SMEM] + [VMEM] * 5, own_shapes, flops=3000000000)]
  transfers between devices with their start and end apart: 3 -> 3, of which waited for: 0 -> 1; matrix products, arithmetic and copies ran while one was open for 0% -> 0% of each run, Pallas kernels for 12% -> 9%
where the time goes in v4:
time: 85.3 us; the launch traced here: 85.1 us
  blocking collectives  55.1 us (65%)
  Pallas kernels  20.9 us (25%)
  starting transfers between devices  8 us (9%)
    all_to_all x1, blocking collectives, body(): back = lax.all_to_all(both, CHIP, 0, 0)  22.4 us
    all_to_all x1, blocking collectives, body(): pieces = lax.all_to_all(pair, CHIP, 0, 0)  19.5 us
    all_to_all x1, blocking collectives, body(): mine = lax.all_to_all(sent, 'feat', 0, 0)  13.2 us
    pallas_call x1, Pallas kernels, body(): call(project_kernel, [ANY] * 6, [shape((4, SPAN, 128)), shape((4, SPAN, 1...  9.05 us
    pallas_call x1, Pallas kernels, body(): call(self_kernel, [SMEM] + [VMEM] * 5, own_shapes, flops=3000000000)  3.9 us
    ppermute x1, starting transfers between devices, body(): taken = lax.ppermute(given, 'c', swap)  3.41 us
    ppermute x1, starting transfers between devices, body(): recv = lax.ppermute(send, 'c', swap)  3.29 us
    pallas_call x1, Pallas kernels, body(): call(own_kernel, [SMEM] + [VMEM] * 9, own_shapes + [shape((2, SPAN, 512),...  2 us
  transfers between devices with their start and end apart: 3, of which 1 were waited for; matrix products, arithmetic and copies ran while one was open for 0% of the time, Pallas kernels for 9%

profile of v4, /device:TPU:1, one launch (start us, length us, event | category | flops | bytes accessed | tf_op | source)
XLA Modules:
  0.0 85.1 jit_solution(15075700691340196971)
XLA Ops:
  0.6 0.0 copy-start.3
  0.6 0.0 copy-start.1
  0.7 9.0 %shard_map.128 = (bf16[4,256,128]{2,1,0:T(8,128)(2,1)S(1)}, bf16[4,256,128]{2,1,0:T(8,128)(2,1)S(1)}, bf16[4,256,512]{2,1,0:T(8,128)(2,1)S(1)}, bf16[2,640,128]{...) custom-call(s32[4]{0:T(128)} %lens.5, bf16[4,256,2048]{2,1,0:T(8,128)(2,1)} %hid.1, ...), custom_call_target="tpu_custom_call" | custom-call | flops 3000000000 | bytes 1048576 | tf_op jit(solution)/shard_map/pallas_call | solution.py:440
  9.7 3.3 %collective-permute-start = (bf16[2,640,128]{2,1,0:T(8,128)(2,1)S(1)}, bf16[2,640,128]{2,1,0:T(8,128)(2,1)S(1)}, u32[]{:S(2)}, u32[]{:S(2)}) collective-permute-start(bf16[2,640,128]{2,1,0:T(8,128)(2,1)S(1)} %get-tuple-element.29), channel_id=1, source_target_pairs={{0,4},{4,0},{1,5},{5,1},{2,6},{6,2},{3,7},{7,3},{8,12},{12,8},{9,1... | collective-permute-start | bytes 983048 | tf_op jit(solution)/shard_map/ppermute | solution.py:464
  13.0 0.0 copy-done.3
  13.0 0.0 copy-done.1
  13.0 3.9 %shard_map.129 = (f32[4,256,512]{2,1,0:T(8,128)S(1)}, f32[4,256,128]{2,1,0:T(8,128)S(1)}, bf16[4,4,256,160]{3,2,1,0:T(8,128)(2,1)S(1)}) custom-call(s32[4]{0:T(128)S(1)} %copy-done.1, bf16[4,256,128]{2,1,0:T(8,128)(2,1)S(1)} %get-tuple-element.30.q, bf16[4,256,128]{2,1,0:T(8,128)(2,1)S(1)} %get-tuple-element.31.k, ...), custom_call_target="tpu_custom_call" | custom-call | flops 3000000000 | bytes 1048576 | tf_op jit(solution)/shard_map/pallas_call | solution.py:467
  16.9 0.0 copy-start
  16.9 0.0 collective-permute-done.recv
  16.9 0.1 shard_map.130
  17.0 0.0 copy-start.2
  17.0 19.5 %all_to_all.15.pieces = bf16[32,40,128]{2,1,0:T(8,128)(2,1)S(1)} all-to-all(bf16[32,40,128]{2,1,0:T(8,128)(2,1)S(1)} %shard_map.130), channel_id=1, replica_groups=mesh['z'=8,'y'=4,'c'=2,'feat'=4] {'z','y'}, dimensions={0} | all-to-all | bytes 655360 | tf_op jit(solution)/shard_map/all_to_all | solution.py:471
  36.5 0.0 copy-done
  36.5 0.6 shard_map.131
  37.2 22.4 %all_to_all.16.back = bf16[32,80,128]{2,1,0:T(8,128)(2,1)S(1)} all-to-all(bf16[32,80,128]{2,1,0:T(8,128)(2,1)S(1)} %shard_map.131), channel_id=1, replica_groups=mesh['z'=8,'y'=4,'c'=2,'feat'=4] {'z','y'}, dimensions={0} | all-to-all | bytes 1310720 | tf_op jit(solution)/shard_map/all_to_all | solution.py:473
  59.6 0.2 shard_map.132
  59.8 3.4 %collective-permute-start.1 = (bf16[1536,128]{1,0:T(8,128)(2,1)S(1)}, bf16[1536,128]{1,0:T(8,128)(2,1)S(1)}, u32[]{:S(2)}, u32[]{:S(2)}) collective-permute-start(bf16[1536,128]{1,0:T(8,128)(2,1)S(1)} %get-tuple-element.39.low_mine), channel_id=1, source_target_pairs={{0,4},{4,0},{1,5},{5,1},{2,6},{6,2},{3,7},{7,3},{8,12},{12,8},{9,1... | collective-permute-start | bytes 1179656 | tf_op jit(solution)/shard_map/ppermute | solution.py:477
  63.2 0.0 copy-done.2
  63.2 0.5 shard_map.134.sent_i
  63.7 2.0 %shard_map.133 = (f32[4,256,512]{2,1,0:T(8,128)S(1)}, f32[4,256,128]{2,1,0:T(8,128)S(1)}, bf16[4,4,256,160]{3,2,1,0:T(8,128)(2,1)S(1)}, f32[2,256,512]{2,1,0:T(8...) custom-call(s32[4]{0:T(128)S(1)} %copy-done.1, ...), custom_call_target="tpu_custom_call", output_to_operand_aliasing={{0}: (7, {}), {1}: (8, {}), {2}: (9, {})} | custom-call | flops 3000000000 | bytes 1048576 | tf_op jit(solution)/shard_map/pallas_call | solution.py:478
  65.7 0.0 collective-permute-done.1.state.low_theirs
  65.7 1.9 %shard_map.135 = (f32[2,256,512]{2,1,0:T(8,128)S(1)}, bf16[4,536,128]{2,1,0:T(8,128)(2,1)S(1)}) custom-call(s32[4]{0:T(128)S(1)} %copy-done.1, bf16[1536,128]{1,0:T(8,128)(2,1)S(1)} %collective-permute-done.1.state.low_theirs, f32[4,256,512]{2,1,0:T(8,128)S(1)} %get-tuple-element.40.num, ...), custom_call_target="tpu_custom_call", output_to_operand_aliasing={{1}: (6, {})} | custom-call | flops 500000000 | bytes 1048576 | tf_op jit(solution)/shard_map/pallas_call | solution.py:490
  67.6 13.2 %all_to_all.17.sent.mine = bf16[4,536,128]{2,1,0:T(8,128)(2,1)S(1)} all-to-all(bf16[4,536,128]{2,1,0:T(8,128)(2,1)S(1)} %get-tuple-element.45), channel_id=1, replica_groups=mesh['z'=8,'y'=4,'c'=2,'feat'=4] {'feat'}, dimensions={0} | all-to-all | bytes 1097728 | tf_op jit(solution)/shard_map/all_to_all | solution.py:497
  80.8 1.3 %collective-permute-start.2 = (bf16[4,536,128]{2,1,0:T(8,128)(2,1)S(1)}, bf16[4,536,128]{2,1,0:T(8,128)(2,1)S(1)}, u32[]{:S(2)}, u32[]{:S(2)}) collective-permute-start(bf16[4,536,128]{2,1,0:T(8,128)(2,1)S(1)} %all_to_all.17.sent.mine), channel_id=1, source_target_pairs={{0,4},{4,0},{1,5},{5,1},{2,6},{6,2},{3,7},{7,3},{8,12},{12,8},{9,1... | collective-permute-start | bytes 1646600 | tf_op jit(solution)/shard_map/ppermute | solution.py:498
  82.1 1.3 %shard_map.136 = bf16[4,256,512]{2,1,0:T(8,128)(2,1)} custom-call(f32[2,256,512]{2,1,0:T(8,128)S(1)} %get-tuple-element.38.own, f32[2,256,512]{2,1,0:T(8,128)S(1)} %get-tuple-element.44.other, bf16[4,536,128]{2,1,0:T(8,128)(2,1)S(1)} %all_to_all.17.sent.mine), custom_call_target="tpu_custom_call" | custom-call | flops 500000000 | bytes 1048576 | tf_op jit(solution)/shard_map/pallas_call | solution.py:499
  83.4 0.3 collective-permute-done.2.theirs
  83.7 1.4 %shard_map.137 = (f32[1,4,16,64,128]{4,3,2,1,0:T(8,128)}, f32[1,4,17,4,128]{4,3,2,1,0:T(4,128)}, f32[1,4,16,64]{3,2,1,0:T(8,128)}, f32[1,4,4,17]{3,2,1,0:T(4,128)}) custom-call(s32[4]{0:T(128)S(1)} %copy-done, bf16[4,536,128]{2,1,0:T(8,128)(2,1)S(1)} %all_to_all.17.sent.mine, ...), custom_call_target="tpu_custom_call", output_to_operand_aliasing={{0}: (5, {})} | custom-call | bytes 1048576 | tf_op jit(solution)/shard_map/pallas_call | solution.py:508
Async XLA Ops:
  0.6 12.4 %copy-start.3 = (f32[8,160]{1,0:T(8,128)S(1)}, f32[8,160]{1,0:T(8,128)}, u32[]{:S(2)}) copy-start(f32[8,160]{1,0:T(8,128)} %constant.7.clone.lines) | copy-start | bytes 15364
  0.6 12.4 %copy-start.1 = (s32[4]{0:T(128)S(1)}, s32[4]{0:T(128)}, u32[]{:S(2)}) copy-start(s32[4]{0:T(128)} %lens.5) | copy-start | bytes 52
  9.7 7.2 %collective-permute-start = (bf16[2,640,128]{2,1,0:T(8,128)(2,1)S(1)}, bf16[2,640,128]{2,1,0:T(8,128)(2,1)S(1)}, u32[]{:S(2)}, u32[]{:S(2)}) collective-permute-start(bf16[2,640,128]{2,1,0:T(8,128)(2,1)S(1)} %get-tuple-element.29), channel_id=1, source_target_pairs={{0,4},{4,0},{1,5},{5,1},{2,6},{6,2},{3,7},{7,3},{8,12},{12,8},{9,1... | collective-permute-start | bytes 983048 | tf_op jit(solution)/shard_map/ppermute | solution.py:464
  16.9 19.6 %copy-start = (s32[4]{0:T(128)S(1)}, s32[4]{0:T(128)}, u32[]{:S(2)}) copy-start(s32[4]{0:T(128)} %owners.3) | copy-start | bytes 52
  17.0 46.2 %copy-start.2 = (bf16[256,160]{1,0:T(8,128)(2,1)S(1)}, bf16[256,160]{1,0:T(8,128)(2,1)}, u32[]{:S(2)}) copy-start(bf16[256,160]{1,0:T(8,128)(2,1)} %constant.8.clone.table) | copy-start | bytes 245764
  59.8 5.9 %collective-permute-start.1 = (bf16[1536,128]{1,0:T(8,128)(2,1)S(1)}, bf16[1536,128]{1,0:T(8,128)(2,1)S(1)}, u32[]{:S(2)}, u32[]{:S(2)}) collective-permute-start(bf16[1536,128]{1,0:T(8,128)(2,1)S(1)} %get-tuple-element.39.low_mine), channel_id=1, source_target_pairs={{0,4},{4,0},{1,5},{5,1},{2,6},{6,2},{3,7},{7,3},{8,12},{12,8},{9,1... | collective-permute-start | bytes 1179656 | tf_op jit(solution)/shard_map/ppermute | solution.py:477
  80.8 2.9 %collective-permute-start.2 = (bf16[4,536,128]{2,1,0:T(8,128)(2,1)S(1)}, bf16[4,536,128]{2,1,0:T(8,128)(2,1)S(1)}, u32[]{:S(2)}, u32[]{:S(2)}) collective-permute-start(bf16[4,536,128]{2,1,0:T(8,128)(2,1)S(1)} %all_to_all.17.sent.mine), channel_id=1, source_target_pairs={{0,4},{4,0},{1,5},{5,1},{2,6},{6,2},{3,7},{7,3},{8,12},{12,8},{9,1... | collective-permute-start | bytes 1646600 | tf_op jit(solution)/shard_map/ppermute | solution.py:498

commit v5 on v4

--- a/solution.py
+++ b/solution.py
@@ -80,9 +80,7 @@
 AHEAD = 5
 
 
-def project_kernel(
-    lens_h, hid, wv, wq, wk, picks_h, q_o, k_o, v_o, send_o, keep_o, picks, hid_b, wv_b, wqk_b, lens, sems, rest, small
-):
+def project_kernel(lens_h, hid, wv, wq, wk, picks_h, q_o, k_o, v_o, send_o, picks, hid_b, wv_b, wqk_b, lens, sems, rest, small):
     core, _, seq, feat = place()
     lanes = pl.ds(pl.multiple_of(feat // 2 * 128, 128), 128)
     first = (2 + 2 * core) % 4
@@ -118,60 +116,75 @@
 
     for n in range(AHEAD):
         start(n)
+    def first_product():
+        v = jnp.zeros((SPAN, 512), F32)
+        qk = jnp.zeros((SPAN, 256), F32)
+        for m in range(D // CHUNK):
+            arrive(m)
+            rows = slice(m * CHUNK, (m + 1) * CHUNK)
+            x = hid_b[2, :, rows]
+            qk = qk + jnp.dot(x, wqk_b[rows], preferred_element_type=F32)
+            v = v + jnp.dot(x, wv_b[rows], preferred_element_type=F32)
+        arrive(D // CHUNK)
+        return qk, v
+
+    keep_rows(0, first_product(), q_o, k_o, v_o)
+    arrive(D // CHUNK + 1)
+    keep_rows(1, product(hid_b[3], wqk_b, wv_b), q_o, k_o, v_o)
+    states(0, 2, lens, k_o, v_o, picks, send_o)
+    states(1, 3, lens, k_o, v_o, picks, send_o)
+    for n in range(2, 4):
+        arrive(D // CHUNK + n)
+
+
+def product(x, wqk, wv):
+    return (
+        jnp.dot(x, wqk[...], preferred_element_type=F32),
+        jnp.dot(x, wv[...], preferred_element_type=F32),
+    )
+
+
+def keep_rows(n, products, q_o, k_o, v_o):
+    qk, v = products
+    q_o[n] = qk[:, :128].astype(BF)
+    k_o[n] = qk[:, 128:].astype(BF)
+    v_o[n] = v.astype(BF)
+
+
+def states(n, local, lens, k, v, picks, out):
+    core, _, seq, _ = place()
     row = lax.broadcasted_iota(jnp.int32, (ROWS, SPAN), 0)
     low = is_low(row)
     const = (row == LOW).astype(F32)
     fixed = jnp.where(row == LOW, 1.0, jnp.where(low, FD**-0.25, (2.0 * FD) ** -0.5))
     ones = jnp.ones((8, SPAN), BF)
     tail_row = lax.broadcasted_iota(jnp.int32, (8, HD), 0) + (ROWS - 8)
-
-    def project(n, local):
-        if n == 0:
-            v = jnp.zeros((SPAN, 512), F32)
-            qk = jnp.zeros((SPAN, 256), F32)
-            for m in range(D // CHUNK):
-                arrive(m)
-                rows = slice(m * CHUNK, (m + 1) * CHUNK)
-                x = hid_b[local, :, rows]
-                qk = qk + jnp.dot(x, wqk_b[rows], preferred_element_type=F32)
-                v = v + jnp.dot(x, wv_b[rows], preferred_element_type=F32)
-            arrive(D // CHUNK)
-        else:
-            arrive(D // CHUNK + n)
-            x = hid_b[local]
-            qk = jnp.dot(x, wqk_b[...], preferred_element_type=F32)
-            v = jnp.dot(x, wv_b[...], preferred_element_type=F32)
-        q_o[local] = qk[:, :128].astype(BF)
-        k_o[local] = qk[:, 128:].astype(BF)
-        v_o[local] = v.astype(BF)
-
-    def states(local):
-        key_t = k_o[local].astype(F32).T.astype(BF)
-        token = seq * SPAN + lax.broadcasted_iota(jnp.int32, (1, SPAN), 1)
-        scale = jnp.where(token < lens[(local + 2 * core) % 4], fixed, 0.0)
-        bias = jnp.where(low, scale, 0.0)
-        target = send_o if local >= 2 else keep_o
-        for h in range(OWN):
-            at = h * ROWS
-            u = jnp.dot(picks[0, at : at + ROWS], key_t, preferred_element_type=F32)
-            w = jnp.dot(picks[1, at : at + ROWS], key_t, preferred_element_type=F32)
-            feats = ((u + const) * (w * scale + bias)).astype(BF)
-            state = jnp.dot(feats, v_o[local, :, h * HD : (h + 1) * HD], preferred_element_type=F32)
-            norm = nt(ones, feats)
-            rest_norm = jnp.concatenate([norm[:, HD:], jnp.zeros((8, 2 * HD - ROWS), F32)], axis=1)
-            tail = state[ROWS - 8 :]
-            tail = jnp.where(tail_row == NORM, norm[:, :HD], jnp.where(tail_row == NORM + 1, rest_norm, tail))
-            target[local % 2, at : at + ROWS] = jnp.concatenate([state[: ROWS - 8], tail], axis=0).astype(BF)
-
-    order = (2, 3, 0, 1)
-    for n in range(5):
-        if n < 4:
-            project(n, order[n])
-        if n > 0:
-            states(order[n - 1])
-
-
-def self_kernel(lens, q, k, v, picks, lines, num_o, den_o, feat_o, late=False):
+    key_t = k[n].astype(F32).T.astype(BF)
+    token = seq * SPAN + lax.broadcasted_iota(jnp.int32, (1, SPAN), 1)
+    scale = jnp.where(token < lens[(local + 2 * core) % 4], fixed, 0.0)
+    bias = jnp.where(low, scale, 0.0)
+    for h in range(OWN):
+        at = h * ROWS
+        u = jnp.dot(picks[0, at : at + ROWS], key_t, preferred_element_type=F32)
+        w = jnp.dot(picks[1, at : at + ROWS], key_t, preferred_element_type=F32)
+        feats = ((u + const) * (w * scale + bias)).astype(BF)
+        state = jnp.dot(feats, v[n, :, h * HD : (h + 1) * HD], preferred_element_type=F32)
+        norm = nt(ones, feats)
+        rest_norm = jnp.concatenate([norm[:, HD:], jnp.zeros((8, 2 * HD - ROWS), F32)], axis=1)
+        tail = state[ROWS - 8 :]
+        tail = jnp.where(tail_row == NORM, norm[:, :HD], jnp.where(tail_row == NORM + 1, rest_norm, tail))
+        out[n, at : at + ROWS] = jnp.concatenate([state[: ROWS - 8], tail], axis=0).astype(BF)
+
+
+def keep_kernel(lens, hid, wqk, wv, picks, qb, kb, vb, lines, qa, ka, va, keep_o, num_o, den_o, feat_o):
+    keep_rows(0, product(hid[0], wqk, wv), qa, ka, va)
+    keep_rows(1, product(hid[1], wqk, wv), qa, ka, va)
+    states(0, 0, lens, ka, va, picks, keep_o)
+    states(1, 1, lens, ka, va, picks, keep_o)
+    self_kernel(lens, (qa, ka, va), (qb, kb, vb), picks, lines, num_o, den_o, feat_o)
+
+
+def self_kernel(lens, own, other, picks, lines, num_o, den_o, feat_o, late=False):
     core, _, seq, feat = place()
     z = lax.axis_index("z")
     early = jnp.where(z < 4, 5 - z, 0) + (lax.axis_index("y") == 0).astype(jnp.int32)
@@ -182,9 +195,9 @@
     scale, bias, const = lines[0:1], lines[1:2], lines[2:3]
     ones = jnp.ones((SPAN, HD), BF)
 
-    def prompt(local, _):
-        query = q[local]
-        key = k[local]
+    def prompt(local, _, q, k, v):
+        query = q[local % 2]
+        key = k[local % 2]
         seen = (tk <= tq) & (seq * SPAN + tk < lens[(local + 2 * core) % 4])
         den_all = jnp.zeros((SPAN, HD), F32)
         for h in range(OWN):
@@ -192,7 +205,7 @@
             mine = jnp.where(lane // FD == feat % 2 * OWN + h, query, jnp.zeros_like(query))
             score = nt(mine, key)
             weight = jnp.where(seen, 1.0 + score * (FD**-0.5) + score * score * (0.5 / FD), 0.0).astype(BF)
-            value = jnp.concatenate([v[local, :, h * HD : (h + 1) * HD], ones], axis=1)
+            value = jnp.concatenate([v[local % 2, :, h * HD : (h + 1) * HD], ones], axis=1)
             both = jnp.dot(weight, value, preferred_element_type=F32)
             num_o[local, :, h * HD : (h + 1) * HD] = both[:, :HD]
             den_all = jnp.where(lane == h, both[:, HD:], den_all)
@@ -202,10 +215,13 @@
         den_o[local] = den_all
         return _
 
-    lax.fori_loop(split if late else 0, 4 if late else split, prompt, 0)
-
-
-def pair_kernel(keep, recv, after, out):
+    for half, refs in ((0, own), (1, other)):
+        cut = jnp.clip(split - 2 * half, 0, 2) + 2 * half
+        lower, upper = (cut, 2 * half + 2) if late else (2 * half, cut)
+        lax.fori_loop(lower, upper, lambda n, c, refs=refs: prompt(n, c, *refs), 0)
+
+
+def pair_kernel(keep, recv, out):
     pair = (keep[...].astype(F32) + recv[...].astype(F32)).astype(BF)
     out[...] = pair.reshape(CHIPS, SLICE, HD)
 
@@ -295,13 +311,14 @@
 
 
 def own_kernel(
-    lens, state, q, k, v, picks, lines, num_i, den_i, feat_i, num, den, feat, att_o, square_o, quad_o, blank, sem
+    lens, state, qa, ka, va, qb, kb, vb, picks, lines, num_i, den_i, feat_i,
+    num, den, feat, att_o, square_o, quad_o, blank, sem
 ):
     blank[...] = jnp.zeros_like(blank)
     clear = [pltpu.make_async_copy(blank, quad_o.at[0, n], sem.at[n]) for n in range(4)]
     for copy in clear:
         copy.start()
-    self_kernel(lens, q, k, v, picks, lines, num, den, feat, late=True)
+    self_kernel(lens, (qa, ka, va), (qb, kb, vb), picks, lines, num, den, feat, late=True)
     found = attend(0, lens, part_of(state), num, den, feat, att_o)
     square_o[...] = jnp.concatenate(found + [jnp.zeros((4, HD), F32)], axis=0)
     for copy in clear:
@@ -437,21 +454,12 @@
     half = (2, OWN * ROWS, HD)
     packed = OWN * ROWS
 
-    q, k, v, send, keep, picks = call(
+    rows = [shape((2, SPAN, 128)), shape((2, SPAN, 128)), shape((2, SPAN, 512)), shape(half)]
+    qb, kb, vb, send, picks, hid, wv_b, wqk_b = call(
         project_kernel,
         [ANY] * 6,
-        [
-            shape((4, SPAN, 128)),
-            shape((4, SPAN, 128)),
-            shape((4, SPAN, 512)),
-            shape(half),
-            shape(half),
-            shape((2, packed, 128)),
-        ],
+        rows + [shape((2, packed, 128)), shape((4, SPAN, D)), shape((D, 512)), shape((D, 256))],
         scratch=[
-            pltpu.VMEM((4, SPAN, D), BF),
-            pltpu.VMEM((D, 512), BF),
-            pltpu.VMEM((D, 256), BF),
             pltpu.SMEM((4,), jnp.int32),
             pltpu.SemaphoreType.DMA((D // CHUNK, 4)),
             pltpu.SemaphoreType.DMA((3,)),
@@ -464,10 +472,11 @@
     recv = lax.ppermute(send, "c", swap)
     lines = jnp.asarray(LINES)
     own_shapes = [shape((4, SPAN, 512), F32), shape((4, SPAN, 128), F32), shape((4, OWN, SPAN, ROWS))]
-    num, den, feats = call(self_kernel, [SMEM] + [VMEM] * 5, own_shapes, flops=3_000_000_000)(
-        lengths, *near(q, k, v, picks, lines)
-    )
-    pair = call(pair_kernel, [VMEM, VMEM, ANY], shape((CHIPS, SLICE, HD)))(*near(keep, recv, den))
+    qa, ka, va, keep, num, den, feats = call(
+        keep_kernel, [SMEM] + [VMEM] * 8, rows + own_shapes, flops=3_000_000_000, limit=24
+    )(lengths, *near(hid, wqk_b, wv_b, picks, qb, kb, vb, lines))
+    qkv = (qa, ka, va, qb, kb, vb)
+    pair = call(pair_kernel, [VMEM, VMEM], shape((CHIPS, SLICE, HD)))(*near(keep, recv))
     pieces = lax.all_to_all(pair, CHIP, 0, 0)
     both = call(scan_kernel, [SMEM, VMEM], shape((CHIPS, 2 * SLICE, HD)))(owners, *near(pieces))
     back = lax.all_to_all(both, CHIP, 0, 0)
@@ -477,13 +486,13 @@
     taken = lax.ppermute(given, "c", swap)
     num, den, feats, own_att, square, quad = call(
         own_kernel,
-        [SMEM] + [VMEM] * 9,
+        [SMEM] + [VMEM] * 12,
         own_shapes + [shape((2, SPAN, 512), F32), shape((8, HD), F32), pltpu.HBM((1, 4, H, 64, HD), F32)],
         [VMEM] * 5 + [ANY],
         scratch=[pltpu.VMEM((H, 64, HD), F32), pltpu.SemaphoreType.DMA((4,))],
         flops=3_000_000_000,
-        aliases={7: 0, 8: 1, 9: 2},
-    )(lengths, *near(own_state, q, k, v, picks, lines, num, den, feats))
+        aliases={10: 0, 11: 1, 12: 2},
+    )(lengths, *near(own_state, *qkv, picks, lines, num, den, feats))
     sent = call(spread_kernel, [VMEM] * 2, shape((4, SENT, HD)), flops=500_000_000)(
         *near(back, jnp.asarray(SPREAD, BF))
     )

time: 85.3 us -> 85.2 us (level)
  transfers between devices with their start and end apart: 3 -> 3, of which waited for: 1 -> 1; matrix products, arithmetic and copies ran while one was open for 0% -> 0% of each run, Pallas kernels for 9% -> 13%
where the time goes in v5:
time: 85.2 us; the launch traced here: 85.1 us
  blocking collectives  54.5 us (64%)
  Pallas kernels  21.4 us (25%)
  starting transfers between devices  8.01 us (9%)
  between operations  0.89 us (1%)
    all_to_all x1, blocking collectives, body(): back = lax.all_to_all(both, CHIP, 0, 0)  22 us
    all_to_all x1, blocking collectives, body(): pieces = lax.all_to_all(pair, CHIP, 0, 0)  19.3 us
    all_to_all x1, blocking collectives, body(): mine = lax.all_to_all(sent, 'feat', 0, 0)  13.2 us
    pallas_call x1, Pallas kernels, body(): call(keep_kernel, [SMEM] + [VMEM] * 8, rows + own_shapes, flops=300000000...  7.17 us
    pallas_call x1, Pallas kernels, body(): call(project_kernel, [ANY] * 6, rows + [shape((2, packed, 128)), shape((4...  5.89 us
    ppermute x1, starting transfers between devices, body(): taken = lax.ppermute(given, 'c', swap)  3.41 us
    ppermute x1, starting transfers between devices, body(): recv = lax.ppermute(send, 'c', swap)  3.29 us
    pallas_call x1, Pallas kernels, body(): call(own_kernel, [SMEM] + [VMEM] * 12, own_shapes + [shape((2, SPAN, 512)...  2.17 us
  transfers between devices with their start and end apart: 3, of which 1 were waited for; matrix products, arithmetic and copies ran while one was open for 0% of the time, Pallas kernels for 13%

profile of v5, /device:TPU:1, one launch (start us, length us, event | category | flops | bytes accessed | tf_op | source)
XLA Modules:
  0.0 85.1 jit_solution(3724770241648767954)
XLA Ops:
  0.6 0.0 copy-start.3
  0.6 0.0 copy-start.1
  0.7 5.9 %shard_map.128 = (bf16[2,256,128]{2,1,0:T(8,128)(2,1)S(1)}, bf16[2,256,128]{2,1,0:T(8,128)(2,1)S(1)}, bf16[2,256,512]{2,1,0:T(8,128)(2,1)S(1)}, bf16[2,640,128]{...) custom-call(s32[4]{0:T(128)} %lens.5, ...), custom_call_target="tpu_custom_call" | custom-call | flops 3000000000 | bytes 1048576 | tf_op jit(solution)/shard_map/pallas_call | solution.py:458
  6.6 3.3 %collective-permute-start = (bf16[2,640,128]{2,1,0:T(8,128)(2,1)S(1)}, bf16[2,640,128]{2,1,0:T(8,128)(2,1)S(1)}, u32[]{:S(2)}, u32[]{:S(2)}) collective-permute-start(bf16[2,640,128]{2,1,0:T(8,128)(2,1)S(1)} %get-tuple-element.42), channel_id=1, source_target_pairs={{0,4},{4,0},{1,5},{5,1},{2,6},{6,2},{3,7},{7,3},{8,12},{12,8},{9,1... | collective-permute-start | bytes 983048 | tf_op jit(solution)/shard_map/ppermute | solution.py:472
  9.8 0.0 copy-done.3
  9.8 0.0 copy-done.1
  9.8 0.0 copy-start
  9.9 7.2 %shard_map.129 = (bf16[2,256,128]{2,1,0:T(8,128)(2,1)S(1)}, bf16[2,256,128]{2,1,0:T(8,128)(2,1)S(1)}, bf16[2,256,512]{2,1,0:T(8,128)(2,1)S(1)}, bf16[2,640,128]{...) custom-call(s32[4]{0:T(128)S(1)} %copy-done.1, ...), custom_call_target="tpu_custom_call" | custom-call | flops 3000000000 | bytes 1048576 | tf_op jit(solution)/shard_map/pallas_call | solution.py:475
  17.0 0.0 collective-permute-done.recv
  17.0 0.1 shard_map.130
  17.1 0.0 copy-start.2
  17.1 19.3 %all_to_all.15.pieces = bf16[32,40,128]{2,1,0:T(8,128)(2,1)S(1)} all-to-all(bf16[32,40,128]{2,1,0:T(8,128)(2,1)S(1)} %shard_map.130), channel_id=1, replica_groups=mesh['z'=8,'y'=4,'c'=2,'feat'=4] {'z','y'}, dimensions={0} | all-to-all | bytes 655360 | tf_op jit(solution)/shard_map/all_to_all | solution.py:480
  36.4 0.0 copy-done
  36.4 0.6 shard_map.131
  37.1 22.0 %all_to_all.16.back = bf16[32,80,128]{2,1,0:T(8,128)(2,1)S(1)} all-to-all(bf16[32,80,128]{2,1,0:T(8,128)(2,1)S(1)} %shard_map.131), channel_id=1, replica_groups=mesh['z'=8,'y'=4,'c'=2,'feat'=4] {'z','y'}, dimensions={0} | all-to-all | bytes 1310720 | tf_op jit(solution)/shard_map/all_to_all | solution.py:482
  59.0 0.2 shard_map.132
  59.2 3.4 %collective-permute-start.1 = (bf16[1536,128]{1,0:T(8,128)(2,1)S(1)}, bf16[1536,128]{1,0:T(8,128)(2,1)S(1)}, u32[]{:S(2)}, u32[]{:S(2)}) collective-permute-start(bf16[1536,128]{1,0:T(8,128)(2,1)S(1)} %get-tuple-element.51.low_mine), channel_id=1, source_target_pairs={{0,4},{4,0},{1,5},{5,1},{2,6},{6,2},{3,7},{7,3},{8,12},{12,8},{9,1... | collective-permute-start | bytes 1179656 | tf_op jit(solution)/shard_map/ppermute | solution.py:486
  62.6 0.0 copy-done.2
  62.6 0.5 shard_map.134.sent_i
  63.1 2.2 %shard_map.133 = (f32[4,256,512]{2,1,0:T(8,128)S(1)}, f32[4,256,128]{2,1,0:T(8,128)S(1)}, bf16[4,4,256,160]{3,2,1,0:T(8,128)(2,1)S(1)}, f32[2,256,512]{2,1,0:T(8...) custom-call(s32[4]{0:T(128)S(1)} %copy-done.1, ...), custom_call_target="tpu_custom_call", output_to_operand_aliasing={{0}: (10, {}), {1}: (11, {}), {2}: (12, {})} | custom-call | flops 3000000000 | bytes 1048576 | tf_op jit(solution)/shard_map/pallas_call | solution.py:487
  65.3 0.0 collective-permute-done.1.state.low_theirs
  65.3 1.9 %shard_map.135 = (f32[2,256,512]{2,1,0:T(8,128)S(1)}, bf16[4,536,128]{2,1,0:T(8,128)(2,1)S(1)}) custom-call(s32[4]{0:T(128)S(1)} %copy-done.1, bf16[1536,128]{1,0:T(8,128)(2,1)S(1)} %collective-permute-done.1.state.low_theirs, f32[4,256,512]{2,1,0:T(8,128)S(1)} %get-tuple-element.52.num, ...), custom_call_target="tpu_custom_call", output_to_operand_aliasing={{1}: (6, {})} | custom-call | flops 500000000 | bytes 1048576 | tf_op jit(solution)/shard_map/pallas_call | solution.py:499
  67.2 13.2 %all_to_all.17.sent.mine = bf16[4,536,128]{2,1,0:T(8,128)(2,1)S(1)} all-to-all(bf16[4,536,128]{2,1,0:T(8,128)(2,1)S(1)} %get-tuple-element.57), channel_id=1, replica_groups=mesh['z'=8,'y'=4,'c'=2,'feat'=4] {'feat'}, dimensions={0} | all-to-all | bytes 1097728 | tf_op jit(solution)/shard_map/all_to_all | solution.py:506
  80.4 1.3 %collective-permute-start.2 = (bf16[4,536,128]{2,1,0:T(8,128)(2,1)S(1)}, bf16[4,536,128]{2,1,0:T(8,128)(2,1)S(1)}, u32[]{:S(2)}, u32[]{:S(2)}) collective-permute-start(bf16[4,536,128]{2,1,0:T(8,128)(2,1)S(1)} %all_to_all.17.sent.mine), channel_id=1, source_target_pairs={{0,4},{4,0},{1,5},{5,1},{2,6},{6,2},{3,7},{7,3},{8,12},{12,8},{9,1... | collective-permute-start | bytes 1646600 | tf_op jit(solution)/shard_map/ppermute | solution.py:507
  81.7 1.3 %shard_map.136 = bf16[4,256,512]{2,1,0:T(8,128)(2,1)} custom-call(f32[2,256,512]{2,1,0:T(8,128)S(1)} %get-tuple-element.50.own, f32[2,256,512]{2,1,0:T(8,128)S(1)} %get-tuple-element.56.other, bf16[4,536,128]{2,1,0:T(8,128)(2,1)S(1)} %all_to_all.17.sent.mine), custom_call_target="tpu_custom_call" | custom-call | flops 500000000 | bytes 1048576 | tf_op jit(solution)/shard_map/pallas_call | solution.py:508
  83.0 0.3 collective-permute-done.2.theirs
  83.3 1.6 %shard_map.137 = (f32[1,4,16,64,128]{4,3,2,1,0:T(8,128)}, f32[1,4,17,4,128]{4,3,2,1,0:T(4,128)}, f32[1,4,16,64]{3,2,1,0:T(8,128)}, f32[1,4,4,17]{3,2,1,0:T(4,128)}) custom-call(s32[4]{0:T(128)S(1)} %copy-done, bf16[4,536,128]{2,1,0:T(8,128)(2,1)S(1)} %all_to_all.17.sent.mine, ...), custom_call_target="tpu_custom_call", output_to_operand_aliasing={{0}: (5, {})} | custom-call | bytes 1048576 | tf_op jit(solution)/shard_map/pallas_call | solution.py:517
Async XLA Ops:
  0.6 9.2 %copy-start.3 = (f32[8,160]{1,0:T(8,128)S(1)}, f32[8,160]{1,0:T(8,128)}, u32[]{:S(2)}) copy-start(f32[8,160]{1,0:T(8,128)} %constant.7.clone.lines) | copy-start | bytes 15364
  0.6 9.2 %copy-start.1 = (s32[4]{0:T(128)S(1)}, s32[4]{0:T(128)}, u32[]{:S(2)}) copy-start(s32[4]{0:T(128)} %lens.5) | copy-start | bytes 52
  6.6 10.5 %collective-permute-start = (bf16[2,640,128]{2,1,0:T(8,128)(2,1)S(1)}, bf16[2,640,128]{2,1,0:T(8,128)(2,1)S(1)}, u32[]{:S(2)}, u32[]{:S(2)}) collective-permute-start(bf16[2,640,128]{2,1,0:T(8,128)(2,1)S(1)} %get-tuple-element.42), channel_id=1, source_target_pairs={{0,4},{4,0},{1,5},{5,1},{2,6},{6,2},{3,7},{7,3},{8,12},{12,8},{9,1... | collective-permute-start | bytes 983048 | tf_op jit(solution)/shard_map/ppermute | solution.py:472
  9.8 26.6 %copy-start = (s32[4]{0:T(128)S(1)}, s32[4]{0:T(128)}, u32[]{:S(2)}) copy-start(s32[4]{0:T(128)} %owners.3) | copy-start | bytes 52
  17.1 45.5 %copy-start.2 = (bf16[256,160]{1,0:T(8,128)(2,1)S(1)}, bf16[256,160]{1,0:T(8,128)(2,1)}, u32[]{:S(2)}) copy-start(bf16[256,160]{1,0:T(8,128)(2,1)} %constant.8.clone.table) | copy-start | bytes 245764
  59.2 6.1 %collective-permute-start.1 = (bf16[1536,128]{1,0:T(8,128)(2,1)S(1)}, bf16[1536,128]{1,0:T(8,128)(2,1)S(1)}, u32[]{:S(2)}, u32[]{:S(2)}) collective-permute-start(bf16[1536,128]{1,0:T(8,128)(2,1)S(1)} %get-tuple-element.51.low_mine), channel_id=1, source_target_pairs={{0,4},{4,0},{1,5},{5,1},{2,6},{6,2},{3,7},{7,3},{8,12},{12,8},{9,1... | collective-permute-start | bytes 1179656 | tf_op jit(solution)/shard_map/ppermute | solution.py:486
  80.4 2.9 %collective-permute-start.2 = (bf16[4,536,128]{2,1,0:T(8,128)(2,1)S(1)}, bf16[4,536,128]{2,1,0:T(8,128)(2,1)S(1)}, u32[]{:S(2)}, u32[]{:S(2)}) collective-permute-start(bf16[4,536,128]{2,1,0:T(8,128)(2,1)S(1)} %all_to_all.17.sent.mine), channel_id=1, source_target_pairs={{0,4},{4,0},{1,5},{5,1},{2,6},{6,2},{3,7},{7,3},{8,12},{12,8},{9,1... | collective-permute-start | bytes 1646600 | tf_op jit(solution)/shard_map/ppermute | solution.py:507

commit v6 on v5

--- a/solution.py
+++ b/solution.py
@@ -176,12 +176,20 @@
         out[n, at : at + ROWS] = jnp.concatenate([state[: ROWS - 8], tail], axis=0).astype(BF)
 
 
-def keep_kernel(lens, hid, wqk, wv, picks, qb, kb, vb, lines, qa, ka, va, keep_o, num_o, den_o, feat_o):
+def keep_kernel(
+    lens, hid, wqk, wv, picks, qb, kb, vb, lines, qa, ka, va, keep_o, num_o, den_o, feat_o, quad_o, blank, sem
+):
+    blank[...] = jnp.zeros_like(blank)
+    clear = [pltpu.make_async_copy(blank, quad_o.at[0, n], sem.at[n]) for n in range(4)]
+    for copy in clear:
+        copy.start()
     keep_rows(0, product(hid[0], wqk, wv), qa, ka, va)
     keep_rows(1, product(hid[1], wqk, wv), qa, ka, va)
     states(0, 0, lens, ka, va, picks, keep_o)
     states(1, 1, lens, ka, va, picks, keep_o)
     self_kernel(lens, (qa, ka, va), (qb, kb, vb), picks, lines, num_o, den_o, feat_o)
+    for copy in clear:
+        copy.wait()
 
 
 def self_kernel(lens, own, other, picks, lines, num_o, den_o, feat_o, late=False):
@@ -311,18 +319,13 @@
 
 
 def own_kernel(
-    lens, state, qa, ka, va, qb, kb, vb, picks, lines, num_i, den_i, feat_i,
-    num, den, feat, att_o, square_o, quad_o, blank, sem
+    lens, state, qa, ka, va, qb, kb, vb, picks, lines, num_i, den_i, feat_i, back, table,
+    num, den, feat, att_o, square_o, sent_o
 ):
-    blank[...] = jnp.zeros_like(blank)
-    clear = [pltpu.make_async_copy(blank, quad_o.at[0, n], sem.at[n]) for n in range(4)]
-    for copy in clear:
-        copy.start()
+    spread_kernel(back, table, sent_o)
     self_kernel(lens, (qa, ka, va), (qb, kb, vb), picks, lines, num, den, feat, late=True)
     found = attend(0, lens, part_of(state), num, den, feat, att_o)
     square_o[...] = jnp.concatenate(found + [jnp.zeros((4, HD), F32)], axis=0)
-    for copy in clear:
-        copy.wait()
 
 
 def other_kernel(lens, state, num, den, feat, square, sent_i, att_o, sent_o):
@@ -472,8 +475,14 @@
     recv = lax.ppermute(send, "c", swap)
     lines = jnp.asarray(LINES)
     own_shapes = [shape((4, SPAN, 512), F32), shape((4, SPAN, 128), F32), shape((4, OWN, SPAN, ROWS))]
-    qa, ka, va, keep, num, den, feats = call(
-        keep_kernel, [SMEM] + [VMEM] * 8, rows + own_shapes, flops=3_000_000_000, limit=24
+    qa, ka, va, keep, num, den, feats, quad = call(
+        keep_kernel,
+        [SMEM] + [VMEM] * 8,
+        rows + own_shapes + [pltpu.HBM((1, 4, H, 64, HD), F32)],
+        [VMEM] * 7 + [ANY],
+        scratch=[pltpu.VMEM((H, 64, HD), F32), pltpu.SemaphoreType.DMA((4,))],
+        flops=3_000_000_000,
+        limit=24,
     )(lengths, *near(hid, wqk_b, wv_b, picks, qb, kb, vb, lines))
     qkv = (qa, ka, va, qb, kb, vb)
     pair = call(pair_kernel, [VMEM, VMEM], shape((CHIPS, SLICE, HD)))(*near(keep, recv))
@@ -484,18 +493,13 @@
         prefix_kernel, [VMEM] * 3, [shape((STATE, HD)), shape((STATE + 2 * OWN * LOW_ROWS, HD))]
     )(*near(back, keep, recv))
     taken = lax.ppermute(given, "c", swap)
-    num, den, feats, own_att, square, quad = call(
+    num, den, feats, own_att, square, sent = call(
         own_kernel,
-        [SMEM] + [VMEM] * 12,
-        own_shapes + [shape((2, SPAN, 512), F32), shape((8, HD), F32), pltpu.HBM((1, 4, H, 64, HD), F32)],
-        [VMEM] * 5 + [ANY],
-        scratch=[pltpu.VMEM((H, 64, HD), F32), pltpu.SemaphoreType.DMA((4,))],
+        [SMEM] + [VMEM] * 14,
+        own_shapes + [shape((2, SPAN, 512), F32), shape((8, HD), F32), shape((4, SENT, HD))],
         flops=3_000_000_000,
         aliases={10: 0, 11: 1, 12: 2},
-    )(lengths, *near(own_state, *qkv, picks, lines, num, den, feats))
-    sent = call(spread_kernel, [VMEM] * 2, shape((4, SENT, HD)), flops=500_000_000)(
-        *near(back, jnp.asarray(SPREAD, BF))
-    )
+    )(lengths, *near(own_state, *qkv, picks, lines, num, den, feats, back, jnp.asarray(SPREAD, BF)))
     other_att, sent = call(
         other_kernel,
         [SMEM] + [VMEM] * 6,

time: 85.2 us -> 85 us (level)
    pallas_call x3 -> x2, Pallas kernels: 9.84 us -> 9.71 us  [the longest x1 7.22 us: body(): call(keep_kernel, [SMEM] + [VMEM] * 8, rows + own_shapes + [pltpu.HBM((1,...]
where the time goes in v6:
time: 85 us; the launch traced here: 84.8 us
  blocking collectives  54.5 us (64%)
  Pallas kernels  21.1 us (25%)
  starting transfers between devices  7.99 us (9%)
  between operations  0.87 us (1%)
    all_to_all x1, blocking collectives, body(): back = lax.all_to_all(both, CHIP, 0, 0)  22 us
    all_to_all x1, blocking collectives, body(): pieces = lax.all_to_all(pair, CHIP, 0, 0)  19.3 us
    all_to_all x1, blocking collectives, body(): mine = lax.all_to_all(sent, 'feat', 0, 0)  13.2 us
    pallas_call x1, Pallas kernels, body(): call(keep_kernel, [SMEM] + [VMEM] * 8, rows + own_shapes + [pltpu.HBM((1,...  7.22 us
    pallas_call x1, Pallas kernels, body(): call(project_kernel, [ANY] * 6, rows + [shape((2, packed, 128)), shape((4...  5.89 us
    ppermute x1, starting transfers between devices, body(): taken = lax.ppermute(given, 'c', swap)  3.41 us
    ppermute x1, starting transfers between devices, body(): recv = lax.ppermute(send, 'c', swap)  3.29 us
    pallas_call x1, Pallas kernels, body(): call(own_kernel, [SMEM] + [VMEM] * 14, own_shapes + [shape((2, SPAN, 512)...  2.49 us
  transfers between devices with their start and end apart: 3, of which 1 were waited for; matrix products, arithmetic and copies ran while one was open for 0% of the time, Pallas kernels for 13%

profile of v6, /device:TPU:1, one launch (start us, length us, event | category | flops | bytes accessed | tf_op | source)
XLA Modules:
  0.0 84.8 jit_solution(2426423456316871619)
XLA Ops:
  0.6 0.0 copy-start.3
  0.6 0.0 copy-start.1
  0.7 5.9 %shard_map.128 = (bf16[2,256,128]{2,1,0:T(8,128)(2,1)S(1)}, bf16[2,256,128]{2,1,0:T(8,128)(2,1)S(1)}, bf16[2,256,512]{2,1,0:T(8,128)(2,1)S(1)}, bf16[2,640,128]{...) custom-call(s32[4]{0:T(128)} %lens.5, ...), custom_call_target="tpu_custom_call" | custom-call | flops 3000000000 | bytes 1048576 | tf_op jit(solution)/shard_map/pallas_call | solution.py:461
  6.6 3.3 %collective-permute-start = (bf16[2,640,128]{2,1,0:T(8,128)(2,1)S(1)}, bf16[2,640,128]{2,1,0:T(8,128)(2,1)S(1)}, u32[]{:S(2)}, u32[]{:S(2)}) collective-permute-start(bf16[2,640,128]{2,1,0:T(8,128)(2,1)S(1)} %get-tuple-element.43), channel_id=1, source_target_pairs={{0,4},{4,0},{1,5},{5,1},{2,6},{6,2},{3,7},{7,3},{8,12},{12,8},{9,1... | collective-permute-start | bytes 983048 | tf_op jit(solution)/shard_map/ppermute | solution.py:475
  9.8 0.0 copy-done.3
  9.8 0.0 copy-done.1
  9.8 0.0 copy-start
  9.9 7.2 %shard_map.129 = (bf16[2,256,128]{2,1,0:T(8,128)(2,1)S(1)}, bf16[2,256,128]{2,1,0:T(8,128)(2,1)S(1)}, bf16[2,256,512]{2,1,0:T(8,128)(2,1)S(1)}, bf16[2,640,128]{...) custom-call(s32[4]{0:T(128)S(1)} %copy-done.1, ...), custom_call_target="tpu_custom_call" | custom-call | flops 3000000000 | bytes 1048576 | tf_op jit(solution)/shard_map/pallas_call | solution.py:478
  17.1 0.0 collective-permute-done.recv
  17.1 0.1 shard_map.130
  17.2 0.0 copy-start.2
  17.2 19.3 %all_to_all.15.pieces = bf16[32,40,128]{2,1,0:T(8,128)(2,1)S(1)} all-to-all(bf16[32,40,128]{2,1,0:T(8,128)(2,1)S(1)} %shard_map.130), channel_id=1, replica_groups=mesh['z'=8,'y'=4,'c'=2,'feat'=4] {'z','y'}, dimensions={0} | all-to-all | bytes 655360 | tf_op jit(solution)/shard_map/all_to_all | solution.py:489
  36.5 0.0 copy-done
  36.5 0.6 shard_map.131
  37.1 22.0 %all_to_all.16.back = bf16[32,80,128]{2,1,0:T(8,128)(2,1)S(1)} all-to-all(bf16[32,80,128]{2,1,0:T(8,128)(2,1)S(1)} %shard_map.131), channel_id=1, replica_groups=mesh['z'=8,'y'=4,'c'=2,'feat'=4] {'z','y'}, dimensions={0} | all-to-all | bytes 1310720 | tf_op jit(solution)/shard_map/all_to_all | solution.py:491
  59.1 0.2 shard_map.132
  59.3 3.4 %collective-permute-start.1 = (bf16[1536,128]{1,0:T(8,128)(2,1)S(1)}, bf16[1536,128]{1,0:T(8,128)(2,1)S(1)}, u32[]{:S(2)}, u32[]{:S(2)}) collective-permute-start(bf16[1536,128]{1,0:T(8,128)(2,1)S(1)} %get-tuple-element.52.low_mine), channel_id=1, source_target_pairs={{0,4},{4,0},{1,5},{5,1},{2,6},{6,2},{3,7},{7,3},{8,12},{12,8},{9,1... | collective-permute-start | bytes 1179656 | tf_op jit(solution)/shard_map/ppermute | solution.py:495
  62.7 0.0 copy-done.2
  62.7 2.5 %shard_map.133 = (f32[4,256,512]{2,1,0:T(8,128)S(1)}, f32[4,256,128]{2,1,0:T(8,128)S(1)}, bf16[4,4,256,160]{3,2,1,0:T(8,128)(2,1)S(1)}, f32[2,256,512]{2,1,0:T(8...) custom-call(s32[4]{0:T(128)S(1)} %copy-done.1, ...), custom_call_target="tpu_custom_call", output_to_operand_aliasing={{0}: (10, {}), {1}: (11, {}), {2}: (12, {})} | custom-call | flops 3000000000 | bytes 1048576 | tf_op jit(solution)/shard_map/pallas_call | solution.py:496
  65.2 0.0 collective-permute-done.1.state.low_theirs
  65.2 1.9 %shard_map.134 = (f32[2,256,512]{2,1,0:T(8,128)S(1)}, bf16[4,536,128]{2,1,0:T(8,128)(2,1)S(1)}) custom-call(s32[4]{0:T(128)S(1)} %copy-done.1, bf16[1536,128]{1,0:T(8,128)(2,1)S(1)} %collective-permute-done.1.state.low_theirs, f32[4,256,512]{2,1,0:T(8,128)S(1)} %get-tuple-element.53.num, ...), custom_call_target="tpu_custom_call", output_to_operand_aliasing={{1}: (6, {})} | custom-call | flops 500000000 | bytes 1048576 | tf_op jit(solution)/shard_map/pallas_call | solution.py:503
  67.1 13.2 %all_to_all.17.sent.mine = bf16[4,536,128]{2,1,0:T(8,128)(2,1)S(1)} all-to-all(bf16[4,536,128]{2,1,0:T(8,128)(2,1)S(1)} %get-tuple-element.59), channel_id=1, replica_groups=mesh['z'=8,'y'=4,'c'=2,'feat'=4] {'feat'}, dimensions={0} | all-to-all | bytes 1097728 | tf_op jit(solution)/shard_map/all_to_all | solution.py:510
  80.3 1.3 %collective-permute-start.2 = (bf16[4,536,128]{2,1,0:T(8,128)(2,1)S(1)}, bf16[4,536,128]{2,1,0:T(8,128)(2,1)S(1)}, u32[]{:S(2)}, u32[]{:S(2)}) collective-permute-start(bf16[4,536,128]{2,1,0:T(8,128)(2,1)S(1)} %all_to_all.17.sent.mine), channel_id=1, source_target_pairs={{0,4},{4,0},{1,5},{5,1},{2,6},{6,2},{3,7},{7,3},{8,12},{12,8},{9,1... | collective-permute-start | bytes 1646600 | tf_op jit(solution)/shard_map/ppermute | solution.py:511
  81.6 1.3 %shard_map.135 = bf16[4,256,512]{2,1,0:T(8,128)(2,1)} custom-call(f32[2,256,512]{2,1,0:T(8,128)S(1)} %get-tuple-element.51.own, f32[2,256,512]{2,1,0:T(8,128)S(1)} %get-tuple-element.58.other, bf16[4,536,128]{2,1,0:T(8,128)(2,1)S(1)} %all_to_all.17.sent.mine), custom_call_target="tpu_custom_call" | custom-call | flops 500000000 | bytes 1048576 | tf_op jit(solution)/shard_map/pallas_call | solution.py:512
  82.9 0.3 collective-permute-done.2.theirs
  83.2 1.4 %shard_map.136 = (f32[1,4,16,64,128]{4,3,2,1,0:T(8,128)}, f32[1,4,17,4,128]{4,3,2,1,0:T(4,128)}, f32[1,4,16,64]{3,2,1,0:T(8,128)}, f32[1,4,4,17]{3,2,1,0:T(4,128)}) custom-call(s32[4]{0:T(128)S(1)} %copy-done, bf16[4,536,128]{2,1,0:T(8,128)(2,1)S(1)} %all_to_all.17.sent.mine, ...), custom_call_target="tpu_custom_call", output_to_operand_aliasing={{0}: (5, {})} | custom-call | bytes 1048576 | tf_op jit(solution)/shard_map/pallas_call | solution.py:521
Async XLA Ops:
  0.6 9.2 %copy-start.3 = (f32[8,160]{1,0:T(8,128)S(1)}, f32[8,160]{1,0:T(8,128)}, u32[]{:S(2)}) copy-start(f32[8,160]{1,0:T(8,128)} %constant.7.clone.lines) | copy-start | bytes 15364
  0.6 9.2 %copy-start.1 = (s32[4]{0:T(128)S(1)}, s32[4]{0:T(128)}, u32[]{:S(2)}) copy-start(s32[4]{0:T(128)} %lens.5) | copy-start | bytes 52
  6.6 10.5 %collective-permute-start = (bf16[2,640,128]{2,1,0:T(8,128)(2,1)S(1)}, bf16[2,640,128]{2,1,0:T(8,128)(2,1)S(1)}, u32[]{:S(2)}, u32[]{:S(2)}) collective-permute-start(bf16[2,640,128]{2,1,0:T(8,128)(2,1)S(1)} %get-tuple-element.43), channel_id=1, source_target_pairs={{0,4},{4,0},{1,5},{5,1},{2,6},{6,2},{3,7},{7,3},{8,12},{12,8},{9,1... | collective-permute-start | bytes 983048 | tf_op jit(solution)/shard_map/ppermute | solution.py:475
  9.8 26.6 %copy-start = (s32[4]{0:T(128)S(1)}, s32[4]{0:T(128)}, u32[]{:S(2)}) copy-start(s32[4]{0:T(128)} %owners.3) | copy-start | bytes 52
  17.2 45.5 %copy-start.2 = (bf16[256,160]{1,0:T(8,128)(2,1)S(1)}, bf16[256,160]{1,0:T(8,128)(2,1)}, u32[]{:S(2)}) copy-start(bf16[256,160]{1,0:T(8,128)(2,1)} %constant.8.clone.table) | copy-start | bytes 245764
  59.3 5.9 %collective-permute-start.1 = (bf16[1536,128]{1,0:T(8,128)(2,1)S(1)}, bf16[1536,128]{1,0:T(8,128)(2,1)S(1)}, u32[]{:S(2)}, u32[]{:S(2)}) collective-permute-start(bf16[1536,128]{1,0:T(8,128)(2,1)S(1)} %get-tuple-element.52.low_mine), channel_id=1, source_target_pairs={{0,4},{4,0},{1,5},{5,1},{2,6},{6,2},{3,7},{7,3},{8,12},{12,8},{9,1... | collective-permute-start | bytes 1179656 | tf_op jit(solution)/shard_map/ppermute | solution.py:495
  80.3 2.9 %collective-permute-start.2 = (bf16[4,536,128]{2,1,0:T(8,128)(2,1)S(1)}, bf16[4,536,128]{2,1,0:T(8,128)(2,1)S(1)}, u32[]{:S(2)}, u32[]{:S(2)}) collective-permute-start(bf16[4,536,128]{2,1,0:T(8,128)(2,1)S(1)} %all_to_all.17.sent.mine), channel_id=1, source_target_pairs={{0,4},{4,0},{1,5},{5,1},{2,6},{6,2},{3,7},{7,3},{8,12},{12,8},{9,1... | collective-permute-start | bytes 1646600 | tf_op jit(solution)/shard_map/ppermute | solution.py:511
